TPU v7x, 32 devices: a whole 2x2x4 slice. The times are simulated.
32 devices in a mesh: tile: 8 (over z, y), lev: 4 (over x, core).
Axes of the slice: x: 2, y: 2, z: 4, core: 2. Of those that a mesh axis runs over, the one named last changes fastest.
Arguments:
- trajectory: bfloat16 [3, 32, 16384], P(None, 'lev', 'tile'), may hold values from -6 to 6
- increment: bfloat16 [3, 32, 16384], P(None, 'lev', 'tile'), may hold values from -6 to 6
- counts: int32 [8, 8], P('tile'), may hold values from 1 to 512, 2048 in all within a row
- remap_weight: bfloat16 [8, 8, 512, 512], P('tile'), may hold values from -0.25 to 0.25
- kappa: float32 [3], replicated, may hold values from 0.1 to 0.4
- courant: float32 [16384], P('tile'), may hold values from 0.1 to 0.6
- vertical: float32 [16384], P('tile'), may hold values from -0.4 to 0.4
- offset: int32 [16384], P('tile'), may hold values from -2 to 2
Outputs:
- tangent: float32 [3, 32, 16384], P(None, 'lev', 'tile')
- grad_outer: float32 [3, 32, 16384], P(None, 'lev', 'tile')
Inputs may be any that keep to these rules, and one draw needn't show every extreme that they name: Each row of counts sums to 2048, and every row has an entry equal to 512.
All inputs are finite; a program needn't handle non-finite values.
Results may differ from a plain program's by a relative error of at most 0.0021.
The roundings to bfloat16 on the way count: a program that leaves them out, or rounds other values in their place, can miss the bound.
Values may be sent and summed in bfloat16 or wider, within the bound.
No kernel may reach another device: no remote copies, remote signals or barrier semaphores. Data moves between devices by JAX's collectives and lax.ppermute only.
A program may use at most 64 MiB of HBM per device.

v0:
```python
import functools

import jax
import jax.numpy as jnp
from jax import lax
from jax.experimental import pallas as pl
from jax.experimental.pallas import tpu as pltpu
from jax.sharding import PartitionSpec as P

HALO = 2
LANE = 128
SUB = 8
EDGE = 3
COEFS = 5
VALUE_MAX = 6.0
WEIGHT_MAX = 0.25
F16_MAX = 65504.0


VMEM = pl.BlockSpec(memory_space=pltpu.VMEM)
SMEM = pl.BlockSpec(memory_space=pltpu.SMEM)
HBM = pl.BlockSpec(memory_space=pltpu.HBM)


def send_scale(slot_count):
    bound = VALUE_MAX * WEIGHT_MAX * slot_count
    scale = 1.0
    while 2.0 * scale * bound < F16_MAX:
        scale *= 2.0
    while scale * bound >= F16_MAX:
        scale *= 0.5
    return scale


def cost(flops, moved):
    return pl.CostEstimate(flops=flops, bytes_accessed=moved, transcendentals=0)


def place(counts, which, reach, window, cols):
    begin = jnp.int32(0)
    for other in range(reach):
        begin = begin + jnp.where(other < which, counts[0, other], 0)
    base = jnp.minimum((begin // LANE) * LANE, cols - window)
    return pl.multiple_of(base, LANE), begin - base


class Plan:
    def __init__(self, tiles, slabs, reach):
        self.tiles, self.slabs, self.reach = tiles, slabs, reach
        self.rounds = reach // 2
        self.cube = tiles == reach and tiles & (tiles - 1) == 0
        if self.cube:
            self.hops = [list(range(reach - 1, 0, -2)), list(range(reach - 2, -1, -2))]
        else:
            self.hops = [list(range(-(reach // 2), 0)), list(range(reach // 2 - 1, -1, -1))]

    def target(self, tile, core, j):
        hop = self.hops[core][j]
        return tile ^ hop if self.cube else (tile + hop) % self.tiles

    def route(self, j):
        cells = [(t, v) for t in range(self.tiles) for v in range(self.slabs)]
        return [(t * self.slabs + v, self.target(t, v % 2, j) * self.slabs + v) for t, v in cells]

    def core(self):
        return lax.rem(lax.axis_index("lev"), 2)

    def has_next(self):
        return lax.axis_index("lev") < self.slabs - 2

    def has_prev(self):
        return lax.axis_index("lev") >= 2

    def group(self, core, j, sign):
        hop = jnp.where(core == 0, jnp.int32(self.hops[0][j]), jnp.int32(self.hops[1][j]))
        centre = self.reach // 2
        if not self.cube:
            return centre + hop
        tile = lax.axis_index("tile")
        return lax.rem(sign * ((tile ^ hop) - tile) + centre + self.reach, self.reach)

    def sent(self, j):
        return self.group(self.core(), j, 1)

    def taken(self, k):
        own = k < self.rounds
        return self.group(self.core() if own else 1 - self.core(), k % self.rounds, -1)


def border_kernel(plan, traj, inc, traj_out, inc_out, border, sems):
    copies = [
        pltpu.make_async_copy(traj, traj_out, sems.at[0]),
        pltpu.make_async_copy(inc, inc_out, sems.at[1]),
    ]
    for copy in copies:
        copy.start()
    for copy in copies:
        copy.wait()
    tracers, levels, _ = traj_out.shape
    lower = plan.core() == 1
    row = 0
    for ref, depth in ((traj_out, 0), (inc_out, 0), (inc_out, 1)):
        for m in range(tracers):
            x = ref[m].astype(jnp.float32)
            low, high = levels - 1 - depth, depth
            line = jnp.where(lower, x[low : low + 1], x[high : high + 1])
            border[row : row + 1, :] = line.astype(border.dtype)
            row += 1


def fetch_border(plan, traj, inc):
    tracers, _, cols = traj.shape
    like = lambda *shape: jax.ShapeDtypeStruct(shape, traj.dtype)
    return pl.pallas_call(
        functools.partial(border_kernel, plan),
        in_specs=[HBM] * 2,
        out_specs=[VMEM] * 3,
        out_shape=[like(*traj.shape), like(*inc.shape), like(EDGE * tracers, cols)],
        scratch_shapes=[pltpu.SemaphoreType.DMA((2,))],
        compiler_params=pltpu.CompilerParams(vmem_limit_bytes=4 << 20),
        cost_estimate=cost(0, 8 * traj.size),
        name="border",
    )(traj, inc)


def load_kernel(plan, weight, w_out, w_low, w_high, sems):
    reach, win = weight.shape[1:3]
    half = win // 2
    copies = []
    for j in range(plan.rounds):
        group = plan.sent(j)
        low = lax.rem(group + reach - 1, reach)
        high = lax.rem(group + 1, reach)
        low_at = pl.multiple_of(jnp.where(group == 0, half, win) - SUB, SUB)
        high_at = pl.multiple_of(jnp.where(group == reach - 2, half, 0), SUB)
        copies.append(pltpu.make_async_copy(weight.at[0, group], w_out.at[j], sems.at[3 * j]))
        copies.append(
            pltpu.make_async_copy(
                weight.at[0, low, pl.ds(low_at, SUB)], w_low.at[j], sems.at[1 + 3 * j]
            )
        )
        copies.append(
            pltpu.make_async_copy(
                weight.at[0, high, pl.ds(high_at, SUB)], w_high.at[j], sems.at[2 + 3 * j]
            )
        )
    for copy in copies:
        copy.start()
    for copy in copies:
        copy.wait()


def load(plan, weight):
    _, _, win, slots = weight.shape
    like = lambda *shape: jax.ShapeDtypeStruct(shape, weight.dtype)
    return pl.pallas_call(
        functools.partial(load_kernel, plan),
        in_specs=[HBM],
        out_specs=[VMEM] * 3,
        out_shape=[
            like(plan.rounds, win, slots),
            like(plan.rounds, SUB, slots),
            like(plan.rounds, SUB, slots),
        ],
        scratch_shapes=[pltpu.SemaphoreType.DMA((3 * plan.rounds,))],
        compiler_params=pltpu.CompilerParams(vmem_limit_bytes=8 << 20),
        cost_estimate=cost(0, 4 * plan.rounds * win * slots),
        name="fetch",
    )(weight)


def gather_kernel(plan, traj, inc, traj_too, inc_too, ext, ext_too, rows_out):
    tracers, levels, _ = traj.shape
    main = tracers * levels
    mine = pl.multiple_of(plan.core() * 2 * main, SUB)
    theirs = pl.multiple_of((1 - plan.core()) * 2 * main, SUB)
    for m in range(tracers):
        for at, t, i in ((mine, traj, inc), (theirs, traj_too, inc_too)):
            rows_out[pl.ds(at + m * levels, levels), :] = t[m].astype(jnp.float32)
            rows_out[pl.ds(at + main + m * levels, levels), :] = i[m].astype(jnp.float32)
    beyond = ext[...].astype(jnp.float32) + ext_too[...].astype(jnp.float32)
    rows_out[4 * main :, :] = jnp.zeros_like(rows_out[4 * main :, :])
    rows_out[4 * main : 4 * main + EDGE * tracers, :] = beyond


def gather(plan, traj, inc, traj_too, inc_too, ext, ext_too, rows):
    cols = traj.shape[-1]
    return pl.pallas_call(
        functools.partial(gather_kernel, plan),
        in_specs=[VMEM] * 6,
        out_specs=VMEM,
        out_shape=jax.ShapeDtypeStruct((rows, cols), jnp.float32),
        compiler_params=pltpu.CompilerParams(vmem_limit_bytes=8 << 20),
        cost_estimate=cost(0, 6 * rows * cols),
        name="gather",
    )(traj, inc, traj_too, inc_too, ext, ext_too)


def forward_kernel(plan, which, scale, tail, counts, rows_in, courant, vertical, offset, w, w_low, w_high, out):
    reach = counts.shape[1]
    rows, cols = rows_in.shape
    slots = w.shape[-1]
    window = slots + LANE
    contract = (((1,), (1,)), ((), ()))

    def slotted(group):
        base, shift = place(counts, group, reach, window, cols)
        x = rows_in[:, pl.ds(base, window)]
        x = pltpu.roll(x, lax.rem(window - shift, window), axis=1)[:, :slots]
        lane = lax.broadcasted_iota(jnp.int32, x.shape, 1)
        return jnp.where(lane < counts[0, group], x, 0.0).astype(jnp.bfloat16)

    group = plan.sent(which)
    y = slotted(group)
    out[...] = scale * lax.dot_general(y, w[which], contract, preferred_element_type=jnp.float32)
    for part, at in enumerate((cols - LANE, 0)):
        span = slice((2 + part) * LANE, (3 + part) * LANE)
        for row, ref in ((0, courant), (2, vertical)):
            value = ref[:, at : at + LANE]
            top = value.astype(jnp.bfloat16).astype(jnp.float32)
            out[tail + row : tail + row + 1, span] = scale * top
            out[tail + row + 1 : tail + row + 2, span] = scale * (value - top)
        out[tail + 4 : tail + 5, span] = scale * offset[:, at : at + LANE].astype(jnp.float32)

    @pl.when((group == 0) | (group == reach - 1))
    def _():
        z = slotted(lax.rem(group + reach - 1, reach))
        e = scale * lax.dot_general(w_low[which], z, contract, preferred_element_type=jnp.float32)
        out[tail : tail + 2 * HALO, :rows] = e[SUB - 2 * HALO :]

    @pl.when((group == reach - 2) | (group == reach - 1))
    def _():
        z = slotted(lax.rem(group + 1, reach))
        e = scale * lax.dot_general(w_high[which], z, contract, preferred_element_type=jnp.float32)
        out[tail : tail + 2 * HALO, LANE : LANE + rows] = e[: 2 * HALO]


def forward(plan, which, counts, rows_in, courant, vertical, offset, w, w_low, w_high, scale, tail):
    rows = rows_in.shape[0]
    win, slots = w.shape[1:]
    return pl.pallas_call(
        functools.partial(forward_kernel, plan, which, scale, tail),
        in_specs=[SMEM] + [VMEM] * 7,
        out_specs=VMEM,
        out_shape=jax.ShapeDtypeStruct((rows, win), jnp.float32),
        compiler_params=pltpu.CompilerParams(vmem_limit_bytes=8 << 20),
        cost_estimate=cost(2 * rows * win * slots, 4 * rows_in.size),
    )(counts, rows_in, courant, vertical, offset, w, w_low, w_high)


def stencil_kernel(plan, unscale, tail, kappa, *refs):
    rounds, reach = plan.rounds, plan.reach
    pieces = refs[: 2 * rounds]
    courant_in, vertical_in, offset_in, tangent_out = refs[2 * rounds : 2 * rounds + 4]
    windows_out = refs[2 * rounds + 4 : 3 * rounds + 4]
    acc, turn, adj = refs[3 * rounds + 4 :]
    tracers, levels, cols = tangent_out.shape
    main = tracers * levels
    rows = acc.shape[0]
    span = cols // reach
    wide = cols + LANE

    acc[...] = jnp.zeros_like(acc)
    low = jnp.zeros((2 * HALO, LANE), jnp.float32)
    high = jnp.zeros((2 * HALO, LANE), jnp.float32)
    c_low = jnp.zeros((COEFS, LANE), jnp.float32)
    c_high = jnp.zeros((COEFS, LANE), jnp.float32)
    for k, piece in enumerate(pieces):
        group = plan.taken(k)
        first = pl.multiple_of(group * span, LANE)
        second = pl.multiple_of(lax.rem(group + 1, reach) * span, LANE)
        acc[:, pl.ds(first, span)] += unscale * piece[:, :span]
        acc[:, pl.ds(second, span)] += unscale * piece[:, span:]
        is_low = (group == 0) | (group == reach - 1)
        is_high = (group == reach - 2) | (group == reach - 1)
        low = low + jnp.where(is_low, piece[tail : tail + 2 * HALO, :LANE], 0.0)
        high = high + jnp.where(is_high, piece[tail : tail + 2 * HALO, LANE : 2 * LANE], 0.0)
        c_low = jnp.where(group == reach // 2 + 1, piece[tail : tail + COEFS, 2 * LANE : 3 * LANE], c_low)
        c_high = jnp.where(group == reach // 2 - 1, piece[tail : tail + COEFS, 3 * LANE :], c_high)
    turn[...] = jnp.zeros_like(turn)
    turn[: 2 * HALO, :] = unscale * high
    turn[LANE - 2 * HALO :, :] = unscale * low
    acc[:, cols:] = turn[...].T[:rows, :]

    lane = lax.broadcasted_iota(jnp.int32, (COEFS, LANE), 1)
    beyond = unscale * jnp.where(lane < LANE // 2, c_high, c_low)
    spread = lambda row: jnp.broadcast_to(row, (SUB, wide))
    row_of = lambda ref, extra: spread(jnp.concatenate([ref[...].astype(jnp.float32), extra], axis=1))
    courant = row_of(courant_in, beyond[0:1] + beyond[1:2])
    vertical = row_of(vertical_in, beyond[2:3] + beyond[3:4])
    offset = row_of(offset_in, beyond[4:5])
    rising = jnp.maximum(vertical, 0.0)
    sinking = jnp.maximum(-vertical, 0.0)
    shifts = range(-HALO, HALO + 1)
    picked = {s: offset == jnp.float32(s) for s in shifts}
    turned = lambda x, by: x if by % wide == 0 else pltpu.roll(x, by % wide, axis=1)
    keep = 1.0 - courant - rising - sinking

    def tangent_of(delta, loss, below, above):
        departed = jnp.zeros_like(delta)
        for s in shifts:
            departed = jnp.where(picked[s], turned(delta, -s), departed)
        return (keep - loss) * delta + courant * departed + rising * below + sinking * above

    sub = lax.broadcasted_iota(jnp.int32, (SUB, wide), 0)
    has_prev, has_next = plan.has_prev(), plan.has_next()
    state_of = lambda h, m: acc[2 * h * main + m * levels : 2 * h * main + (m + 1) * levels, :]
    delta_of = lambda h, m: acc[(2 * h + 1) * main + m * levels : (2 * h + 1) * main + (m + 1) * levels, :]
    line = lambda r: acc[4 * main + r : 4 * main + r + 1, :]
    x_state = jnp.zeros((SUB, wide), jnp.float32)
    x_delta, x_below, x_above, x_kappa = x_state, x_state, x_state, x_state
    for m in range(tracers):
        here = sub == m
        outer = line(2 * tracers + m)
        first = delta_of(0, m)[:1]
        final = delta_of(1, m)[levels - 1 :]
        x_state = jnp.where(here, spread(line(m)), x_state)
        x_delta = jnp.where(here, spread(line(tracers + m)), x_delta)
        x_below = jnp.where(here, spread(jnp.where(has_next, final, outer)), x_below)
        x_above = jnp.where(here, spread(jnp.where(has_next, outer, first)), x_above)
        x_kappa = jnp.where(here, kappa[m], x_kappa)
    x_tangent = tangent_of(x_delta, 2.0 * x_kappa * x_state, x_below, x_above)

    def beside(halves, edge):
        lo, hi = halves
        lo_below = jnp.where(has_prev, edge, 0.0)
        hi_above = jnp.where(has_next, edge, 0.0)
        below = (
            jnp.where(sub == 0, spread(lo_below), pltpu.roll(lo, 1, axis=0)),
            jnp.where(sub == 0, spread(lo[levels - 1 :]), pltpu.roll(hi, 1, axis=0)),
        )
        above = (
            jnp.where(sub == levels - 1, spread(hi[:1]), pltpu.roll(lo, levels - 1, axis=0)),
            jnp.where(sub == levels - 1, spread(hi_above), pltpu.roll(hi, levels - 1, axis=0)),
        )
        return below, above

    for m in range(tracers):
        deltas = (delta_of(0, m), delta_of(1, m))
        losses = tuple(2.0 * kappa[m] * state_of(h, m) for h in range(2))
        below, above = beside(deltas, x_delta[m : m + 1])
        tangents = tuple(tangent_of(deltas[h], losses[h], below[h], above[h]) for h in range(2))
        tangent_out[m] = jnp.where(plan.core() == 0, tangents[0][:, :cols], tangents[1][:, :cols])
        t_below, t_above = beside(tangents, x_tangent[m : m + 1])
        for h in range(2):
            tangent = tangents[h]
            flux = courant * tangent
            arrived = jnp.zeros_like(tangent)
            for s in shifts:
                arrived = arrived + turned(jnp.where(picked[s], flux, 0.0), s)
            adjoint = (keep - losses[h]) * tangent + arrived + rising * t_above[h] + sinking * t_below[h]
            at = h * main + m * levels
            adj[at : at + levels, :cols] = adjoint[:, :cols]
            adj[at : at + levels, cols:] = adjoint[:, :span]
    for j in range(rounds):
        first = pl.multiple_of(plan.taken(j) * span, LANE)
        windows_out[j][...] = adj[:, pl.ds(first, 2 * span)].astype(jnp.bfloat16)


def stencil(plan, kappa, pieces, courant, vertical, offset, tracers, levels, unscale, tail):
    rows = pieces[0].shape[0]
    rounds = plan.rounds
    cols = courant.shape[1]
    span = cols // plan.reach
    return pl.pallas_call(
        functools.partial(stencil_kernel, plan, unscale, tail),
        in_specs=[SMEM] + [VMEM] * (2 * rounds + 3),
        out_specs=[VMEM] * (1 + rounds),
        out_shape=[jax.ShapeDtypeStruct((tracers, levels, cols), jnp.float32)]
        + [jax.ShapeDtypeStruct((2 * tracers * levels, 2 * span), jnp.bfloat16)] * rounds,
        scratch_shapes=[
            pltpu.VMEM((rows, cols + LANE), jnp.float32),
            pltpu.VMEM((LANE, LANE), jnp.float32),
            pltpu.VMEM((2 * tracers * levels, cols + span), jnp.float32),
        ],
        compiler_params=pltpu.CompilerParams(vmem_limit_bytes=24 << 20),
        cost_estimate=cost(100 * rows * cols, 8 * rows * cols),
        name="stencil",
    )(kappa, *pieces, courant, vertical, offset)


def backward_kernel(plan, counts, *refs):
    reach = counts.shape[1]
    pieces = refs[:-3]
    weight, mine, theirs = refs[-3:]
    tracers, levels, cols = mine.shape
    main = tracers * levels
    slots = weight.shape[-1]
    window = slots + LANE
    mine[...] = jnp.zeros_like(mine)
    theirs[...] = jnp.zeros_like(theirs)
    for j, piece in enumerate(pieces):
        group = plan.sent(j)
        grad = jnp.dot(piece[...], weight[j], preferred_element_type=jnp.float32)
        lane = lax.broadcasted_iota(jnp.int32, grad.shape, 1)
        grad = jnp.where(lane < counts[0, group], grad, 0.0)
        grad = jnp.concatenate([grad, jnp.zeros((2 * main, LANE), jnp.float32)], axis=1)
        base, shift = place(counts, group, reach, window, cols)
        grad = pltpu.roll(grad, shift, axis=1)
        own = jnp.where(plan.core() == 0, grad[:main], grad[main:])
        other = jnp.where(plan.core() == 0, grad[main:], grad[:main])
        for m in range(tracers):
            part = slice(m * levels, (m + 1) * levels)
            mine[m, :, pl.ds(base, window)] += own[part]
            theirs[m, :, pl.ds(base, window)] += other[part]


def backward(plan, counts, pieces, weight, tracers, levels, cols):
    rounds, win, slots = weight.shape
    out = jax.ShapeDtypeStruct((tracers, levels, cols), jnp.float32)
    return pl.pallas_call(
        functools.partial(backward_kernel, plan),
        in_specs=[SMEM] + [VMEM] * (rounds + 1),
        out_specs=[VMEM, VMEM],
        out_shape=[out, out],
        compiler_params=pltpu.CompilerParams(vmem_limit_bytes=12 << 20),
        cost_estimate=cost(4 * rounds * tracers * levels * win * slots, 2 * weight.size),
        name="remap_back",
    )(counts, *pieces, weight)


def step(trajectory, increment, counts, remap_weight, kappa, courant, vertical, offset):
    tracers, levels, cols = trajectory.shape
    reach, _, slots = remap_weight.shape[1:]
    tiles, slabs = lax.axis_size("tile"), lax.axis_size("lev")
    if slabs not in (2, 4) or reach % 2:
        raise ValueError("unsupported mesh")
    both = ("tile", "lev")
    plan = Plan(tiles, slabs, reach)
    routes = [plan.route(j) for j in range(plan.rounds)]
    scale = send_scale(slots)
    tail = 4 * tracers * levels + EDGE * tracers
    rows = -(-(tail + COEFS) // SUB) * SUB

    swap = [(v, v ^ 1) for v in range(slabs)]
    near = [(v, v + 1 if v % 2 else v - 1) for v in range(slabs)]
    far = [(v, v + 2 if v % 2 else v - 2) for v in range(slabs)]
    near, far = ([(a, b) for a, b in way if 0 <= b < slabs] for way in (near, far))
    traj_too = lax.ppermute(trajectory, "lev", swap)
    inc_too = lax.ppermute(increment, "lev", swap)
    traj_own, inc_own, border = fetch_border(plan, trajectory, increment)
    ext = lax.ppermute(border, "lev", near)
    ext_too = lax.ppermute(border, "lev", far)

    w, w_low, w_high = load(plan, remap_weight)
    lines = [x.reshape(1, cols) for x in (courant, vertical, offset)]
    rows_in = gather(plan, traj_own, inc_own, traj_too, inc_too, ext, ext_too, rows)
    pieces, message_0 = [], None
    for j, route in enumerate(routes):
        message = forward(plan, j, counts, rows_in, *lines, w, w_low, w_high, scale, tail)
        message = message.astype(jnp.float16)
        message_0 = message_0 if j else message
        pieces.append(lax.ppermute(message, both, route))
    if tiles != reach:
        hops = (reach // 2, -(reach // 2) - 1)
        route = [(t * slabs + v, (t + hops[v % 2]) % tiles * slabs + v) for t in range(tiles) for v in range(slabs)]
        corner = lax.ppermute(message_0[tail:, : 2 * LANE], both, route)
        low_half = lax.broadcasted_iota(jnp.int32, corner.shape, 1) < LANE
        fresh = low_half == (lax.axis_index("lev") % 2 == 0)
        pieces[0] = pieces[0].at[tail:, : 2 * LANE].set(
            jnp.where(fresh, corner, pieces[0][tail:, : 2 * LANE])
        )
    others = []
    for piece in pieces:
        others.append(lax.ppermute(piece, "lev", swap))
    whole = [piece.astype(jnp.float32) for piece in pieces + others]

    tangent, *windows = stencil(plan, kappa, whole, *lines, tracers, levels, 1.0 / scale, tail)
    returned = []
    for window, route in zip(windows, routes):
        returned.append(lax.ppermute(window, both, [(b, a) for a, b in route]))
    mine, theirs = backward(plan, counts, returned, w, tracers, levels, cols)
    return (tangent, mine + lax.ppermute(theirs, "lev", swap))


def solution(mesh):
    return jax.shard_map(
        step,
        mesh=mesh,
        in_specs=(
            P(None, "lev", "tile"),
            P(None, "lev", "tile"),
            P("tile", None),
            P("tile", None, None, None),
            P(),
            P("tile"),
            P("tile"),
            P("tile"),
        ),
        out_specs=(P(None, "lev", "tile"), P(None, "lev", "tile")),
        check_vma=False,
    )
```

profile of v0, /device:TPU:0, one launch (start us, length us, event | category | flops | bytes accessed | tf_op | source)
XLA Modules:
  0.0 50.2 jit_solution(2841479247315583357)
XLA Ops:
  0.7 0.6 %collective-permute-start = (bf16[3,8,2048]{2,1,0:T(8,128)(2,1)}, bf16[3,8,2048]{2,1,0:T(8,128)(2,1)S(1)}, u32[]{:S(2)}, u32[]{:S(2)}) collective-permute-start(bf16[3,8,2048]{2,1,0:T(8,128)(2,1)} %traj.1), channel_id=1, source_target_pairs={{0,1},{1,0},{2,3},{3,2},{4,5},{5,4},{6,7},{7,6},{8,9},{9,8},{10,11... | collective-permute-start | bytes 294920 | tf_op jit(solution)/shard_map/ppermute | solution.py:439
  1.2 0.1 collective-permute-start.1
  1.3 0.9 %copy-done.4 = bf16[3,8,2048]{2,1,0:T(8,128)(2,1)S(1)} copy-done((bf16[3,8,2048]{2,1,0:T(8,128)(2,1)S(1)}, bf16[3,8,2048]{2,1,0:T(8,128)(2,1)}, u32[]{:S(2)}) %copy-start.4) | copy-done | bytes 98328
  2.2 0.9 %copy-done.5 = bf16[3,8,2048]{2,1,0:T(8,128)(2,1)S(1)} copy-done((bf16[3,8,2048]{2,1,0:T(8,128)(2,1)S(1)}, bf16[3,8,2048]{2,1,0:T(8,128)(2,1)}, u32[]{:S(2)}) %copy-start.5) | copy-done | bytes 98328
  3.1 0.3 border.1
  3.4 0.7 %collective-permute-start.2 = (bf16[9,2048]{1,0:T(8,128)(2,1)S(1)}, bf16[9,2048]{1,0:T(8,128)(2,1)S(1)}, u32[]{:S(2)}, u32[]{:S(2)}) collective-permute-start(bf16[9,2048]{1,0:T(8,128)(2,1)S(1)} %get-tuple-element.17), channel_id=1, source_target_pairs={{1,2},{2,1},{5,6},{6,5},{9,10},{10,9},{13,14},{14,13},{17,18},{18,... | collective-permute-start | bytes 110600 | tf_op jit(solution)/shard_map/ppermute | solution.py:442
  4.1 1.3 %collective-permute-start.3 = (bf16[9,2048]{1,0:T(8,128)(2,1)S(1)}, bf16[9,2048]{1,0:T(8,128)(2,1)S(1)}, u32[]{:S(2)}, u32[]{:S(2)}) collective-permute-start(bf16[9,2048]{1,0:T(8,128)(2,1)S(1)} %get-tuple-element.17), channel_id=1, source_target_pairs={{1,3},{2,0},{5,7},{6,4},{9,11},{10,8},{13,15},{14,12},{17,19},{18,... | collective-permute-start | bytes 110600 | tf_op jit(solution)/shard_map/ppermute | solution.py:443
  5.4 2.2 %copy-done = bf16[1,8,512,512]{3,2,1,0:T(8,128)(2,1)S(1)} copy-done((bf16[1,8,512,512]{3,2,1,0:T(8,128)(2,1)S(1)}, bf16[1,8,512,512]{3,2,1,0:T(8,128)(2,1)}, u32[]{:S(2)}) %copy-start) | copy-done | bytes 4194328
  7.6 0.4 fetch.1
  8.0 3.8 %collective-permute-done.3.ext_too = bf16[9,2048]{1,0:T(8,128)(2,1)S(1)} collective-permute-done((bf16[9,2048]{1,0:T(8,128)(2,1)S(1)}, bf16[9,2048]{1,0:T(8,128)(2,1)S(1)}, u32[]{:S(2)}, u32[]{:S(2)}) %collective-permute-start.3) | collective-permute-done | bytes 36896 | tf_op jit(solution)/shard_map/ppermute | solution.py:443
  11.8 0.1 gather.1.rows_in
  11.9 0.9 %shard_map.95 = f32[112,512]{1,0:T(8,128)S(1)} custom-call(s32[1,8]{1,0:T(1,128)S(1)} %copy-done.6, f32[112,2048]{1,0:T(8,128)S(1)} %gather.1.rows_in, f32[1,2048]{1,0:T(1,128)S(1)} %bitcast.3, f32[1,2048]{1,0:T(1,128)S(1)} %bitcast.8, s32[1,2048]{1,0:T(1,128)S(1)} %bitcast.13, bf16[4,512,512]{2,1,0:T(8,128)(2,1)S(1)} %get-tuple-element.18.w.refs_4_, ...), custom_call_target="tpu_custom_call" | custom-call | flops 58720256 | bytes 917504 | tf_op jit(solution)/shard_map/pallas_call | solution.py:241
  12.8 0.9 %shard_map.96 = f32[112,512]{1,0:T(8,128)S(1)} custom-call(s32[1,8]{1,0:T(1,128)S(1)} %copy-done.6, f32[112,2048]{1,0:T(8,128)S(1)} %gather.1.rows_in, f32[1,2048]{1,0:T(1,128)S(1)} %bitcast.4, f32[1,2048]{1,0:T(1,128)S(1)} %bitcast.9, s32[1,2048]{1,0:T(1,128)S(1)} %bitcast.14, bf16[4,512,512]{2,1,0:T(8,128)(2,1)S(1)} %get-tuple-element.18.w.refs_4_, ...), custom_call_target="tpu_custom_call" | custom-call | flops 58720256 | bytes 917504 | tf_op jit(solution)/shard_map/pallas_call | solution.py:241
  13.7 1.4 %shard_map.97 = f32[112,512]{1,0:T(8,128)S(1)} custom-call(s32[1,8]{1,0:T(1,128)S(1)} %copy-done.6, f32[112,2048]{1,0:T(8,128)S(1)} %gather.1.rows_in, f32[1,2048]{1,0:T(1,128)S(1)} %bitcast.5, f32[1,2048]{1,0:T(1,128)S(1)} %bitcast.10, s32[1,2048]{1,0:T(1,128)S(1)} %bitcast.15, bf16[4,512,512]{2,1,0:T(8,128)(2,1)S(1)} %get-tuple-element.18.w.refs_4_, ...), custom_call_target="tpu_custom_call" | custom-call | flops 58720256 | bytes 917504 | tf_op jit(solution)/shard_map/pallas_call | solution.py:241
  15.2 0.9 %shard_map.98 = f32[112,512]{1,0:T(8,128)S(1)} custom-call(s32[1,8]{1,0:T(1,128)S(1)} %copy-done.6, f32[112,2048]{1,0:T(8,128)S(1)} %gather.1.rows_in, f32[1,2048]{1,0:T(1,128)S(1)} %bitcast.6, f32[1,2048]{1,0:T(1,128)S(1)} %bitcast.11, s32[1,2048]{1,0:T(1,128)S(1)} %bitcast.16, bf16[4,512,512]{2,1,0:T(8,128)(2,1)S(1)} %get-tuple-element.18.w.refs_4_, ...), custom_call_target="tpu_custom_call" | custom-call | flops 58720256 | bytes 917504 | tf_op jit(solution)/shard_map/pallas_call | solution.py:241
  16.1 4.8 %collective-permute-start.4 = (f16[112,512]{1,0:T(8,128)(2,1)S(1)}, f16[112,512]{1,0:T(8,128)(2,1)S(1)}, u32[]{:S(2)}, u32[]{:S(2)}) collective-permute-start(f16[112,512]{1,0:T(8,128)(2,1)S(1)} %convert_element_type.36), channel_id=1, source_target_pairs={{0,28},{1,25},{2,30},{3,27},{4,24},{5,29},{6,26},{7,31},{8,20},{9,... | collective-permute-start | bytes 344072 | tf_op jit(solution)/shard_map/ppermute | solution.py:453
  21.1 1.7 %collective-permute-start.6 = (f16[112,512]{1,0:T(8,128)(2,1)S(1)}, f16[112,512]{1,0:T(8,128)(2,1)S(1)}, u32[]{:S(2)}, u32[]{:S(2)}) collective-permute-start(f16[112,512]{1,0:T(8,128)(2,1)S(1)} %convert_element_type.40), channel_id=1, source_target_pairs={{0,12},{1,9},{2,14},{3,11},{4,8},{5,13},{6,10},{7,15},{8,4},{9,1},... | collective-permute-start | bytes 344072 | tf_op jit(solution)/shard_map/ppermute | solution.py:453
  22.8 2.3 %collective-permute-start.7 = (f16[112,512]{1,0:T(8,128)(2,1)S(1)}, f16[112,512]{1,0:T(8,128)(2,1)S(1)}, u32[]{:S(2)}, u32[]{:S(2)}) collective-permute-start(f16[112,512]{1,0:T(8,128)(2,1)S(1)} %convert_element_type.42), channel_id=1, source_target_pairs={{0,4},{1,1},{2,6},{3,3},{4,0},{5,5},{6,2},{7,7},{8,12},{9,9},{10,1... | collective-permute-start | bytes 344072 | tf_op jit(solution)/shard_map/ppermute | solution.py:453
  25.2 5.9 %collective-permute-done.5 = f16[112,512]{1,0:T(8,128)(2,1)S(1)} collective-permute-done((f16[112,512]{1,0:T(8,128)(2,1)S(1)}, f16[112,512]{1,0:T(8,128)(2,1)S(1)}, u32[]{:S(2)}, u32[]{:S(2)}) %collective-permute-start.5) | collective-permute-done | bytes 114720 | tf_op jit(solution)/shard_map/ppermute | solution.py:453
  31.1 0.5 %collective-permute-start.10 = (f16[112,512]{1,0:T(8,128)(2,1)S(1)}, f16[112,512]{1,0:T(8,128)(2,1)S(1)}, u32[]{:S(2)}, u32[]{:S(2)}) collective-permute-start(f16[112,512]{1,0:T(8,128)(2,1)S(1)} %collective-permute-done.6), channel_id=1, source_target_pairs={{0,1},{1,0},{2,3},{3,2},{4,5},{5,4},{6,7},{7,6},{8,9},{9,8},{10,11... | collective-permute-start | bytes 344072 | tf_op jit(solution)/shard_map/ppermute | solution.py:465
  31.8 0.6 %collective-permute-done.9 = f16[112,512]{1,0:T(8,128)(2,1)S(1)} collective-permute-done((f16[112,512]{1,0:T(8,128)(2,1)S(1)}, f16[112,512]{1,0:T(8,128)(2,1)S(1)}, u32[]{:S(2)}, u32[]{:S(2)}) %collective-permute-start.9) | collective-permute-done | bytes 114720 | tf_op jit(solution)/shard_map/ppermute | solution.py:465
  32.4 0.1 collective-permute-done.10
  32.6 0.3 collective-permute-done.11
  33.0 2.7 %stencil.1 = (f32[3,8,2048]{2,1,0:T(8,128)}, bf16[48,512]{1,0:T(8,128)(2,1)S(1)}, bf16[48,512]{1,0:T(8,128)(2,1)S(1)}, bf16[48,512]{1,0:T(8,128)(2,1)S(1)}, bf16[48,512]{1,0:T(8,128)(2,1)S(1)}) custom-call(f32[3]{0:T(128)S(1)} %copy-done.7, f32[112,512]{1,0:T(8,128)S(1)} %convert_element_type.37.refs_0_, f32[112,512]{1,0:T(8,128)S(1)} %convert_element_type.39.refs_1_, ...), custom_call_target="tpu_custom_call" | custom-call | flops 22937600 | bytes 1835008 | tf_op jit(solution)/shard_map/stencil/pallas_call | solution.py:365
  35.7 3.1 %collective-permute-start.12 = (bf16[48,512]{1,0:T(8,128)(2,1)S(1)}, bf16[48,512]{1,0:T(8,128)(2,1)S(1)}, u32[]{:S(2)}, u32[]{:S(2)}) collective-permute-start(bf16[48,512]{1,0:T(8,128)(2,1)S(1)} %get-tuple-element.22), channel_id=1, source_target_pairs={{28,0},{25,1},{30,2},{27,3},{24,4},{29,5},{26,6},{31,7},{20,8},{17... | collective-permute-start | bytes 147464 | tf_op jit(solution)/shard_map/ppermute | solution.py:471
  38.8 2.1 %collective-permute-start.14 = (bf16[48,512]{1,0:T(8,128)(2,1)S(1)}, bf16[48,512]{1,0:T(8,128)(2,1)S(1)}, u32[]{:S(2)}, u32[]{:S(2)}) collective-permute-start(bf16[48,512]{1,0:T(8,128)(2,1)S(1)} %get-tuple-element.24), channel_id=1, source_target_pairs={{12,0},{9,1},{14,2},{11,3},{8,4},{13,5},{10,6},{15,7},{4,8},{1,9},... | collective-permute-start | bytes 147464 | tf_op jit(solution)/shard_map/ppermute | solution.py:471
  40.9 3.4 %collective-permute-start.15 = (bf16[48,512]{1,0:T(8,128)(2,1)S(1)}, bf16[48,512]{1,0:T(8,128)(2,1)S(1)}, u32[]{:S(2)}, u32[]{:S(2)}) collective-permute-start(bf16[48,512]{1,0:T(8,128)(2,1)S(1)} %get-tuple-element.25), channel_id=1, source_target_pairs={{4,0},{1,1},{6,2},{3,3},{0,4},{5,5},{2,6},{7,7},{12,8},{9,9},{14,1... | collective-permute-start | bytes 147464 | tf_op jit(solution)/shard_map/ppermute | solution.py:471
  44.4 0.3 collective-permute-done.13.refs_1_
  44.7 2.2 %collective-permute-done.15.refs_3_ = bf16[48,512]{1,0:T(8,128)(2,1)S(1)} collective-permute-done((bf16[48,512]{1,0:T(8,128)(2,1)S(1)}, bf16[48,512]{1,0:T(8,128)(2,1)S(1)}, u32[]{:S(2)}, u32[]{:S(2)}) %collective-permute-start.15) | collective-permute-done | bytes 49184 | tf_op jit(solution)/shard_map/ppermute | solution.py:471
  46.9 1.1 %remap_back.1 = (f32[3,8,2048]{2,1,0:T(8,128)S(1)}, f32[3,8,2048]{2,1,0:T(8,128)S(1)}) custom-call(s32[1,8]{1,0:T(1,128)S(1)} %copy-done.6, bf16[48,512]{1,0:T(8,128)(2,1)S(1)} %collective-permute-done.12.refs_0_, bf16[48,512]{1,0:T(8,128)(2,1)S(1)} %collective-permute-done.13.refs_1_, bf16[48,512]{1,0:T(8,128)(2,1)S(1)} %collective-permute-done.14.refs_2_, ...), custom_call_target="tpu_custom_call" | custom-call | flops 100663296 | bytes 2097152 | tf_op jit(solution)/shard_map/remap_back/pallas_call | solution.py:411
  48.1 1.4 %collective-permute-done.16 = f32[3,8,2048]{2,1,0:T(8,128)S(1)} collective-permute-done((f32[3,8,2048]{2,1,0:T(8,128)S(1)}, f32[3,8,2048]{2,1,0:T(8,128)S(1)}, u32[]{:S(2)}, u32[]{:S(2)}) %collective-permute-start.16) | collective-permute-done | bytes 196640 | tf_op jit(solution)/shard_map/ppermute | solution.py:473
  49.5 0.7 %add.3 = f32[3,8,2048]{2,1,0:T(8,128)} add(f32[3,8,2048]{2,1,0:T(8,128)S(1)} %get-tuple-element.26, f32[3,8,2048]{2,1,0:T(8,128)S(1)} %collective-permute-done.16) | non-fusion elementwise | flops 49152 | bytes 589824 | tf_op jit(solution)/shard_map/add | solution.py:473
  (40 shorter events, 0.5 us)
Async XLA Ops:
  0.6 11.3 %copy-start.1 = (f32[2048]{0:T(1024)S(1)}, f32[2048]{0:T(1024)}, u32[]{:S(2)}) copy-start(f32[2048]{0:T(1024)} %param.13) | copy-start | bytes 24580
  0.6 11.3 %copy-start.2 = (f32[2048]{0:T(1024)S(1)}, f32[2048]{0:T(1024)}, u32[]{:S(2)}) copy-start(f32[2048]{0:T(1024)} %param.14) | copy-start | bytes 24580
  0.7 11.3 %copy-start.3 = (s32[2048]{0:T(1024)S(1)}, s32[2048]{0:T(1024)}, u32[]{:S(2)}) copy-start(s32[2048]{0:T(1024)} %param.15) | copy-start | bytes 24580
  0.7 11.1 %collective-permute-start = (bf16[3,8,2048]{2,1,0:T(8,128)(2,1)}, bf16[3,8,2048]{2,1,0:T(8,128)(2,1)S(1)}, u32[]{:S(2)}, u32[]{:S(2)}) collective-permute-start(bf16[3,8,2048]{2,1,0:T(8,128)(2,1)} %traj.1), channel_id=1, source_target_pairs={{0,1},{1,0},{2,3},{3,2},{4,5},{5,4},{6,7},{7,6},{8,9},{9,8},{10,11... | collective-permute-start | bytes 294920 | tf_op jit(solution)/shard_map/ppermute | solution.py:439
  1.2 10.6 %collective-permute-start.1 = (bf16[3,8,2048]{2,1,0:T(8,128)(2,1)}, bf16[3,8,2048]{2,1,0:T(8,128)(2,1)S(1)}, u32[]{:S(2)}, u32[]{:S(2)}) collective-permute-start(bf16[3,8,2048]{2,1,0:T(8,128)(2,1)} %inc.1), channel_id=1, source_target_pairs={{0,1},{1,0},{2,3},{3,2},{4,5},{5,4},{6,7},{7,6},{8,9},{9,8},{10,11... | collective-permute-start | bytes 294920 | tf_op jit(solution)/shard_map/ppermute | solution.py:440
  1.3 0.9 %copy-start.4 = (bf16[3,8,2048]{2,1,0:T(8,128)(2,1)S(1)}, bf16[3,8,2048]{2,1,0:T(8,128)(2,1)}, u32[]{:S(2)}) copy-start(bf16[3,8,2048]{2,1,0:T(8,128)(2,1)} %traj.1) | copy-start | bytes 294916
  2.2 0.9 %copy-start.5 = (bf16[3,8,2048]{2,1,0:T(8,128)(2,1)S(1)}, bf16[3,8,2048]{2,1,0:T(8,128)(2,1)}, u32[]{:S(2)}) copy-start(bf16[3,8,2048]{2,1,0:T(8,128)(2,1)} %inc.1) | copy-start | bytes 294916
  3.1 8.8 %copy-start.6 = (s32[1,8]{1,0:T(1,128)S(1)}, s32[1,8]{1,0:T(1,128)}, u32[]{:S(2)}) copy-start(s32[1,8]{1,0:T(1,128)} %counts.9) | copy-start | bytes 100
  3.4 4.6 %collective-permute-start.2 = (bf16[9,2048]{1,0:T(8,128)(2,1)S(1)}, bf16[9,2048]{1,0:T(8,128)(2,1)S(1)}, u32[]{:S(2)}, u32[]{:S(2)}) collective-permute-start(bf16[9,2048]{1,0:T(8,128)(2,1)S(1)} %get-tuple-element.17), channel_id=1, source_target_pairs={{1,2},{2,1},{5,6},{6,5},{9,10},{10,9},{13,14},{14,13},{17,18},{18,... | collective-permute-start | bytes 110600 | tf_op jit(solution)/shard_map/ppermute | solution.py:442
  4.1 7.7 %collective-permute-start.3 = (bf16[9,2048]{1,0:T(8,128)(2,1)S(1)}, bf16[9,2048]{1,0:T(8,128)(2,1)S(1)}, u32[]{:S(2)}, u32[]{:S(2)}) collective-permute-start(bf16[9,2048]{1,0:T(8,128)(2,1)S(1)} %get-tuple-element.17), channel_id=1, source_target_pairs={{1,3},{2,0},{5,7},{6,4},{9,11},{10,8},{13,15},{14,12},{17,19},{18,... | collective-permute-start | bytes 110600 | tf_op jit(solution)/shard_map/ppermute | solution.py:443
  5.4 2.2 %copy-start = (bf16[1,8,512,512]{3,2,1,0:T(8,128)(2,1)S(1)}, bf16[1,8,512,512]{3,2,1,0:T(8,128)(2,1)}, u32[]{:S(2)}) copy-start(bf16[1,8,512,512]{3,2,1,0:T(8,128)(2,1)} %weight.1) | copy-start | bytes 12582916
  15.2 17.8 %copy-start.7 = (f32[3]{0:T(128)S(1)}, f32[3]{0:T(128)}, u32[]{:S(2)}) copy-start(f32[3]{0:T(128)} %kappa.1) | copy-start | bytes 40
  16.1 9.0 %collective-permute-start.4 = (f16[112,512]{1,0:T(8,128)(2,1)S(1)}, f16[112,512]{1,0:T(8,128)(2,1)S(1)}, u32[]{:S(2)}, u32[]{:S(2)}) collective-permute-start(f16[112,512]{1,0:T(8,128)(2,1)S(1)} %convert_element_type.36), channel_id=1, source_target_pairs={{0,28},{1,25},{2,30},{3,27},{4,24},{5,29},{6,26},{7,31},{8,20},{9,... | collective-permute-start | bytes 344072 | tf_op jit(solution)/shard_map/ppermute | solution.py:453
  21.0 10.1 %collective-permute-start.5 = (f16[112,512]{1,0:T(8,128)(2,1)S(1)}, f16[112,512]{1,0:T(8,128)(2,1)S(1)}, u32[]{:S(2)}, u32[]{:S(2)}) collective-permute-start(f16[112,512]{1,0:T(8,128)(2,1)S(1)} %convert_element_type.38), channel_id=1, source_target_pairs={{0,20},{1,17},{2,22},{3,19},{4,16},{5,21},{6,18},{7,23},{8,28},{9,... | collective-permute-start | bytes 344072 | tf_op jit(solution)/shard_map/ppermute | solution.py:453
  21.1 10.0 %collective-permute-start.6 = (f16[112,512]{1,0:T(8,128)(2,1)S(1)}, f16[112,512]{1,0:T(8,128)(2,1)S(1)}, u32[]{:S(2)}, u32[]{:S(2)}) collective-permute-start(f16[112,512]{1,0:T(8,128)(2,1)S(1)} %convert_element_type.40), channel_id=1, source_target_pairs={{0,12},{1,9},{2,14},{3,11},{4,8},{5,13},{6,10},{7,15},{8,4},{9,1},... | collective-permute-start | bytes 344072 | tf_op jit(solution)/shard_map/ppermute | solution.py:453
  22.8 8.8 %collective-permute-start.7 = (f16[112,512]{1,0:T(8,128)(2,1)S(1)}, f16[112,512]{1,0:T(8,128)(2,1)S(1)}, u32[]{:S(2)}, u32[]{:S(2)}) collective-permute-start(f16[112,512]{1,0:T(8,128)(2,1)S(1)} %convert_element_type.42), channel_id=1, source_target_pairs={{0,4},{1,1},{2,6},{3,3},{4,0},{5,5},{6,2},{7,7},{8,12},{9,9},{10,1... | collective-permute-start | bytes 344072 | tf_op jit(solution)/shard_map/ppermute | solution.py:453
  25.1 6.7 %collective-permute-start.8 = (f16[112,512]{1,0:T(8,128)(2,1)S(1)}, f16[112,512]{1,0:T(8,128)(2,1)S(1)}, u32[]{:S(2)}, u32[]{:S(2)}) collective-permute-start(f16[112,512]{1,0:T(8,128)(2,1)S(1)} %collective-permute-done.4), channel_id=1, source_target_pairs={{0,1},{1,0},{2,3},{3,2},{4,5},{5,4},{6,7},{7,6},{8,9},{9,8},{10,11... | collective-permute-start | bytes 344072 | tf_op jit(solution)/shard_map/ppermute | solution.py:465
  31.1 1.3 %collective-permute-start.9 = (f16[112,512]{1,0:T(8,128)(2,1)S(1)}, f16[112,512]{1,0:T(8,128)(2,1)S(1)}, u32[]{:S(2)}, u32[]{:S(2)}) collective-permute-start(f16[112,512]{1,0:T(8,128)(2,1)S(1)} %collective-permute-done.5), channel_id=1, source_target_pairs={{0,1},{1,0},{2,3},{3,2},{4,5},{5,4},{6,7},{7,6},{8,9},{9,8},{10,11... | collective-permute-start | bytes 344072 | tf_op jit(solution)/shard_map/ppermute | solution.py:465
  31.1 1.5 %collective-permute-start.10 = (f16[112,512]{1,0:T(8,128)(2,1)S(1)}, f16[112,512]{1,0:T(8,128)(2,1)S(1)}, u32[]{:S(2)}, u32[]{:S(2)}) collective-permute-start(f16[112,512]{1,0:T(8,128)(2,1)S(1)} %collective-permute-done.6), channel_id=1, source_target_pairs={{0,1},{1,0},{2,3},{3,2},{4,5},{5,4},{6,7},{7,6},{8,9},{9,8},{10,11... | collective-permute-start | bytes 344072 | tf_op jit(solution)/shard_map/ppermute | solution.py:465
  31.6 1.3 %collective-permute-start.11 = (f16[112,512]{1,0:T(8,128)(2,1)S(1)}, f16[112,512]{1,0:T(8,128)(2,1)S(1)}, u32[]{:S(2)}, u32[]{:S(2)}) collective-permute-start(f16[112,512]{1,0:T(8,128)(2,1)S(1)} %collective-permute-done.7), channel_id=1, source_target_pairs={{0,1},{1,0},{2,3},{3,2},{4,5},{5,4},{6,7},{7,6},{8,9},{9,8},{10,11... | collective-permute-start | bytes 344072 | tf_op jit(solution)/shard_map/ppermute | solution.py:465
  35.7 8.7 %collective-permute-start.12 = (bf16[48,512]{1,0:T(8,128)(2,1)S(1)}, bf16[48,512]{1,0:T(8,128)(2,1)S(1)}, u32[]{:S(2)}, u32[]{:S(2)}) collective-permute-start(bf16[48,512]{1,0:T(8,128)(2,1)S(1)} %get-tuple-element.22), channel_id=1, source_target_pairs={{28,0},{25,1},{30,2},{27,3},{24,4},{29,5},{26,6},{31,7},{20,8},{17... | collective-permute-start | bytes 147464 | tf_op jit(solution)/shard_map/ppermute | solution.py:471
  38.8 5.9 %collective-permute-start.13 = (bf16[48,512]{1,0:T(8,128)(2,1)S(1)}, bf16[48,512]{1,0:T(8,128)(2,1)S(1)}, u32[]{:S(2)}, u32[]{:S(2)}) collective-permute-start(bf16[48,512]{1,0:T(8,128)(2,1)S(1)} %get-tuple-element.23), channel_id=1, source_target_pairs={{20,0},{17,1},{22,2},{19,3},{16,4},{21,5},{18,6},{23,7},{28,8},{25... | collective-permute-start | bytes 147464 | tf_op jit(solution)/shard_map/ppermute | solution.py:471
  38.8 5.9 %collective-permute-start.14 = (bf16[48,512]{1,0:T(8,128)(2,1)S(1)}, bf16[48,512]{1,0:T(8,128)(2,1)S(1)}, u32[]{:S(2)}, u32[]{:S(2)}) collective-permute-start(bf16[48,512]{1,0:T(8,128)(2,1)S(1)} %get-tuple-element.24), channel_id=1, source_target_pairs={{12,0},{9,1},{14,2},{11,3},{8,4},{13,5},{10,6},{15,7},{4,8},{1,9},... | collective-permute-start | bytes 147464 | tf_op jit(solution)/shard_map/ppermute | solution.py:471
  40.9 6.0 %collective-permute-start.15 = (bf16[48,512]{1,0:T(8,128)(2,1)S(1)}, bf16[48,512]{1,0:T(8,128)(2,1)S(1)}, u32[]{:S(2)}, u32[]{:S(2)}) collective-permute-start(bf16[48,512]{1,0:T(8,128)(2,1)S(1)} %get-tuple-element.25), channel_id=1, source_target_pairs={{4,0},{1,1},{6,2},{3,3},{0,4},{5,5},{2,6},{7,7},{12,8},{9,9},{14,1... | collective-permute-start | bytes 147464 | tf_op jit(solution)/shard_map/ppermute | solution.py:471
  48.0 1.5 %collective-permute-start.16 = (f32[3,8,2048]{2,1,0:T(8,128)S(1)}, f32[3,8,2048]{2,1,0:T(8,128)S(1)}, u32[]{:S(2)}, u32[]{:S(2)}) collective-permute-start(f32[3,8,2048]{2,1,0:T(8,128)S(1)} %get-tuple-element.27), channel_id=1, source_target_pairs={{0,1},{1,0},{2,3},{3,2},{4,5},{5,4},{6,7},{7,6},{8,9},{9,8},{10,11... | collective-permute-start | bytes 589832 | tf_op jit(solution)/shard_map/ppermute | solution.py:473
where the time goes:
time: 50.5 us; the launch traced here: 50.2 us
  starting transfers between devices  20.9 us (41%)
  waiting for transfers between devices  14.7 us (29%)
  Pallas kernels  8.79 us (17%)
  local copies, waits for them, and re-layouts  3.99 us (8%)
  between operations  0.94 us (2%)
  other arithmetic  0.91 us (2%)
    ppermute x4, starting transfers between devices, step(): pieces.append(lax.ppermute(message, both, route))  8.91 us
    ppermute x4, starting transfers between devices, step(): returned.append(lax.ppermute(window, both, [(b, a) for a, b in route]))  8.65 us
    ppermute x4, waiting for transfers between devices, step(): pieces.append(lax.ppermute(message, both, route))  5.92 us
    pallas_call x4, Pallas kernels, forward(): pl.pallas_call(functools.partial(forward_kernel, plan, which, scale, tail...  4.12 us
    unnamed x16, local copies, waits for them, and re-layouts  3.99 us
    ppermute x1, waiting for transfers between devices, step(): ext_too = lax.ppermute(border, 'lev', far)  3.78 us
    pallas_call x1, Pallas kernels, stencil(): pl.pallas_call(functools.partial(stencil_kernel, plan, unscale, tail), in...  2.74 us
    ppermute x4, waiting for transfers between devices, step(): returned.append(lax.ppermute(window, both, [(b, a) for a, b in route]))  2.54 us
  transfers between devices with their start and end apart: 17, of which 8 were waited for; matrix products, arithmetic and copies ran while one was open for 0% of the time, Pallas kernels for 1%

commit v1 on v0

--- a/solution.py
+++ b/solution.py
@@ -36,12 +36,17 @@
     return pl.CostEstimate(flops=flops, bytes_accessed=moved, transcendentals=0)
 
 
-def place(counts, which, reach, window, cols):
-    begin = jnp.int32(0)
-    for other in range(reach):
-        begin = begin + jnp.where(other < which, counts[0, other], 0)
-    base = jnp.minimum((begin // LANE) * LANE, cols - window)
-    return pl.multiple_of(base, LANE), begin - base
+def place(counts, which):
+    sizes = counts[...].astype(jnp.float32)
+    lane = lax.broadcasted_iota(jnp.int32, sizes.shape, 1)
+    begin = jnp.sum(jnp.where(lane < which, sizes, 0.0)).astype(jnp.int32)
+    size = jnp.sum(jnp.where(lane == which, sizes, 0.0)).astype(jnp.int32)
+    base = pl.multiple_of((begin // LANE) * LANE, LANE)
+    return base, begin - base, size
+
+
+def columns(x):
+    return [x[:, at : at + LANE] for at in range(0, x.shape[1], LANE)]
 
 
 class Plan:
@@ -83,8 +88,13 @@
         return self.group(self.core(), j, 1)
 
     def taken(self, k):
-        own = k < self.rounds
-        return self.group(self.core() if own else 1 - self.core(), k % self.rounds, -1)
+        return self.group(self.owner(k), k % self.rounds, -1)
+
+    def returned(self, k):
+        return self.group(self.owner(k), k % self.rounds, 1)
+
+    def owner(self, k):
+        return self.core() if k < self.rounds else 1 - self.core()
 
 
 def border_kernel(plan, traj, inc, traj_out, inc_out, border, sems):
@@ -170,21 +180,21 @@
 
 
 def gather_kernel(plan, traj, inc, traj_too, inc_too, ext, ext_too, rows_out):
-    tracers, levels, _ = traj.shape
+    tracers, levels, cols = traj.shape
     main = tracers * levels
     mine = pl.multiple_of(plan.core() * 2 * main, SUB)
     theirs = pl.multiple_of((1 - plan.core()) * 2 * main, SUB)
     for m in range(tracers):
         for at, t, i in ((mine, traj, inc), (theirs, traj_too, inc_too)):
-            rows_out[pl.ds(at + m * levels, levels), :] = t[m].astype(jnp.float32)
-            rows_out[pl.ds(at + main + m * levels, levels), :] = i[m].astype(jnp.float32)
+            rows_out[pl.ds(at + m * levels, levels), :cols] = t[m].astype(jnp.float32)
+            rows_out[pl.ds(at + main + m * levels, levels), :cols] = i[m].astype(jnp.float32)
+    rows_out[:, cols:] = jnp.zeros_like(rows_out[:, cols:])
+    rows_out[4 * main :, :cols] = jnp.zeros_like(rows_out[4 * main :, :cols])
     beyond = ext[...].astype(jnp.float32) + ext_too[...].astype(jnp.float32)
-    rows_out[4 * main :, :] = jnp.zeros_like(rows_out[4 * main :, :])
-    rows_out[4 * main : 4 * main + EDGE * tracers, :] = beyond
-
-
-def gather(plan, traj, inc, traj_too, inc_too, ext, ext_too, rows):
-    cols = traj.shape[-1]
+    rows_out[4 * main : 4 * main + EDGE * tracers, :cols] = beyond
+
+
+def gather(plan, traj, inc, traj_too, inc_too, ext, ext_too, rows, cols):
     return pl.pallas_call(
         functools.partial(gather_kernel, plan),
         in_specs=[VMEM] * 6,
@@ -197,18 +207,22 @@
 
 
 def forward_kernel(plan, which, scale, tail, counts, rows_in, courant, vertical, offset, w, w_low, w_high, out):
-    reach = counts.shape[1]
-    rows, cols = rows_in.shape
+    reach, rows, cols = plan.reach, rows_in.shape[0], courant.shape[1]
     slots = w.shape[-1]
-    window = slots + LANE
     contract = (((1,), (1,)), ((), ()))
+    lane = lax.broadcasted_iota(jnp.int32, (rows, LANE), 1)
 
     def slotted(group):
-        base, shift = place(counts, group, reach, window, cols)
-        x = rows_in[:, pl.ds(base, window)]
-        x = pltpu.roll(x, lax.rem(window - shift, window), axis=1)[:, :slots]
-        lane = lax.broadcasted_iota(jnp.int32, x.shape, 1)
-        return jnp.where(lane < counts[0, group], x, 0.0).astype(jnp.bfloat16)
+        base, shift, size = place(counts, group)
+        turned = [
+            pltpu.roll(x, lax.rem(LANE - shift, LANE), axis=1)
+            for x in columns(rows_in[:, pl.ds(base, slots + LANE)])
+        ]
+        parts = []
+        for at, (x, following) in enumerate(zip(turned[:-1], turned[1:])):
+            x = jnp.where(lane < LANE - shift, x, following)
+            parts.append(jnp.where(lane < size - at * LANE, x, 0.0))
+        return jnp.concatenate(parts, axis=1).astype(jnp.bfloat16)
 
     group = plan.sent(which)
     y = slotted(group)
@@ -240,7 +254,7 @@
     win, slots = w.shape[1:]
     return pl.pallas_call(
         functools.partial(forward_kernel, plan, which, scale, tail),
-        in_specs=[SMEM] + [VMEM] * 7,
+        in_specs=[VMEM] * 8,
         out_specs=VMEM,
         out_shape=jax.ShapeDtypeStruct((rows, win), jnp.float32),
         compiler_params=pltpu.CompilerParams(vmem_limit_bytes=8 << 20),
@@ -248,24 +262,10 @@
     )(counts, rows_in, courant, vertical, offset, w, w_low, w_high)
 
 
-def stencil_kernel(plan, unscale, tail, kappa, *refs):
-    rounds, reach = plan.rounds, plan.reach
-    pieces = refs[: 2 * rounds]
-    courant_in, vertical_in, offset_in, tangent_out = refs[2 * rounds : 2 * rounds + 4]
-    windows_out = refs[2 * rounds + 4 : 3 * rounds + 4]
-    acc, turn, adj = refs[3 * rounds + 4 :]
-    tracers, levels, cols = tangent_out.shape
-    main = tracers * levels
-    rows = acc.shape[0]
-    span = cols // reach
-    wide = cols + LANE
-
-    acc[...] = jnp.zeros_like(acc)
-    low = jnp.zeros((2 * HALO, LANE), jnp.float32)
-    high = jnp.zeros((2 * HALO, LANE), jnp.float32)
-    c_low = jnp.zeros((COEFS, LANE), jnp.float32)
-    c_high = jnp.zeros((COEFS, LANE), jnp.float32)
-    for k, piece in enumerate(pieces):
+def collect(plan, unscale, tail, numbers, pieces, acc, low, high, c_low, c_high):
+    reach = plan.reach
+    span = pieces[0].shape[1] // 2
+    for k, piece in zip(numbers, pieces):
         group = plan.taken(k)
         first = pl.multiple_of(group * span, LANE)
         second = pl.multiple_of(lax.rem(group + 1, reach) * span, LANE)
@@ -277,6 +277,55 @@
         high = high + jnp.where(is_high, piece[tail : tail + 2 * HALO, LANE : 2 * LANE], 0.0)
         c_low = jnp.where(group == reach // 2 + 1, piece[tail : tail + COEFS, 2 * LANE : 3 * LANE], c_low)
         c_high = jnp.where(group == reach // 2 - 1, piece[tail : tail + COEFS, 3 * LANE :], c_high)
+    return low, high, c_low, c_high
+
+
+HALO_SLOTS = ((0, 2 * HALO), (SUB, 2 * HALO), (2 * SUB, COEFS), (3 * SUB, COEFS))
+
+
+def assemble_kernel(plan, unscale, tail, numbers, *refs):
+    pieces, (acc, side) = refs[:-2], refs[-2:]
+    acc[...] = jnp.zeros_like(acc)
+    side[...] = jnp.zeros_like(side)
+    blank = [jnp.zeros((size, LANE), jnp.float32) for _, size in HALO_SLOTS]
+    halo = collect(plan, unscale, tail, numbers, pieces, acc, *blank)
+    for (at, size), part in zip(HALO_SLOTS, halo):
+        side[at : at + size, :] = part
+
+
+def assemble(plan, numbers, pieces, unscale, tail, cols):
+    rows = pieces[0].shape[0]
+    return pl.pallas_call(
+        functools.partial(assemble_kernel, plan, unscale, tail, numbers),
+        in_specs=[VMEM] * len(pieces),
+        out_specs=[VMEM] * 2,
+        out_shape=[
+            jax.ShapeDtypeStruct((rows, cols + LANE), jnp.float32),
+            jax.ShapeDtypeStruct((4 * SUB, LANE), jnp.float32),
+        ],
+        compiler_params=pltpu.CompilerParams(vmem_limit_bytes=8 << 20),
+        cost_estimate=cost(4 * rows * cols, 8 * rows * cols),
+        name="assemble",
+    )(*pieces)
+
+
+def stencil_kernel(plan, unscale, tail, numbers, kappa_in, acc_in, side, *refs):
+    rounds, reach = plan.rounds, plan.reach
+    pieces = refs[: len(numbers)]
+    courant_in, vertical_in, offset_in, tangent_out = refs[len(numbers) : len(numbers) + 4]
+    windows_out = refs[len(numbers) + 4 : len(numbers) + 4 + rounds]
+    acc, turn, adj = refs[len(numbers) + 4 + rounds :]
+    tracers = kappa_in.shape[1]
+    levels = tangent_out.shape[0] // (2 * tracers)
+    cols = courant_in.shape[1]
+    main = tracers * levels
+    rows = acc.shape[0]
+    span = cols // reach
+    wide = cols + LANE
+
+    acc[...] = acc_in[...]
+    halo = [side[at : at + size, :] for at, size in HALO_SLOTS]
+    low, high, c_low, c_high = collect(plan, unscale, tail, numbers, pieces, acc, *halo)
     turn[...] = jnp.zeros_like(turn)
     turn[: 2 * HALO, :] = unscale * high
     turn[LANE - 2 * HALO :, :] = unscale * low
@@ -285,6 +334,7 @@
     lane = lax.broadcasted_iota(jnp.int32, (COEFS, LANE), 1)
     beyond = unscale * jnp.where(lane < LANE // 2, c_high, c_low)
     spread = lambda row: jnp.broadcast_to(row, (SUB, wide))
+    kappa = [jnp.broadcast_to(kappa_in[:, m : m + 1], (SUB, wide)) for m in range(tracers)]
     row_of = lambda ref, extra: spread(jnp.concatenate([ref[...].astype(jnp.float32), extra], axis=1))
     courant = row_of(courant_in, beyond[0:1] + beyond[1:2])
     vertical = row_of(vertical_in, beyond[2:3] + beyond[3:4])
@@ -340,7 +390,9 @@
         losses = tuple(2.0 * kappa[m] * state_of(h, m) for h in range(2))
         below, above = beside(deltas, x_delta[m : m + 1])
         tangents = tuple(tangent_of(deltas[h], losses[h], below[h], above[h]) for h in range(2))
-        tangent_out[m] = jnp.where(plan.core() == 0, tangents[0][:, :cols], tangents[1][:, :cols])
+        for h in range(2):
+            at = h * main + m * levels
+            tangent_out[at : at + levels, :] = tangents[h][:, :cols]
         t_below, t_above = beside(tangents, x_tangent[m : m + 1])
         for h in range(2):
             tangent = tangents[h]
@@ -357,66 +409,94 @@
         windows_out[j][...] = adj[:, pl.ds(first, 2 * span)].astype(jnp.bfloat16)
 
 
-def stencil(plan, kappa, pieces, courant, vertical, offset, tracers, levels, unscale, tail):
+def stencil(plan, kappa, acc, side, numbers, pieces, courant, vertical, offset, levels, unscale, tail):
     rows = pieces[0].shape[0]
-    rounds = plan.rounds
     cols = courant.shape[1]
     span = cols // plan.reach
-    return pl.pallas_call(
-        functools.partial(stencil_kernel, plan, unscale, tail),
-        in_specs=[SMEM] + [VMEM] * (2 * rounds + 3),
-        out_specs=[VMEM] * (1 + rounds),
-        out_shape=[jax.ShapeDtypeStruct((tracers, levels, cols), jnp.float32)]
-        + [jax.ShapeDtypeStruct((2 * tracers * levels, 2 * span), jnp.bfloat16)] * rounds,
+    main = 2 * kappa.shape[1] * levels
+    return pl.pallas_call(
+        functools.partial(stencil_kernel, plan, unscale, tail, numbers),
+        in_specs=[VMEM] * (6 + len(pieces)),
+        out_specs=[VMEM] * (1 + plan.rounds),
+        out_shape=[jax.ShapeDtypeStruct((main, cols), jnp.float32)]
+        + [jax.ShapeDtypeStruct((main, 2 * span), jnp.bfloat16)] * plan.rounds,
         scratch_shapes=[
             pltpu.VMEM((rows, cols + LANE), jnp.float32),
             pltpu.VMEM((LANE, LANE), jnp.float32),
-            pltpu.VMEM((2 * tracers * levels, cols + span), jnp.float32),
+            pltpu.VMEM((main, cols + span), jnp.float32),
         ],
         compiler_params=pltpu.CompilerParams(vmem_limit_bytes=24 << 20),
         cost_estimate=cost(100 * rows * cols, 8 * rows * cols),
         name="stencil",
-    )(kappa, *pieces, courant, vertical, offset)
-
-
-def backward_kernel(plan, counts, *refs):
-    reach = counts.shape[1]
-    pieces = refs[:-3]
-    weight, mine, theirs = refs[-3:]
-    tracers, levels, cols = mine.shape
+    )(kappa, acc, side, *pieces, courant, vertical, offset)
+
+
+def emit_kernel(plan, both, out):
+    tracers, levels, _ = out.shape
+    at = pl.multiple_of(plan.core() * tracers * levels, SUB)
+    for m in range(tracers):
+        out[m] = both[pl.ds(at + m * levels, levels), :]
+
+
+def emit(plan, both, tracers):
+    main, cols = both.shape
+    return pl.pallas_call(
+        functools.partial(emit_kernel, plan),
+        in_specs=[VMEM],
+        out_specs=VMEM,
+        out_shape=jax.ShapeDtypeStruct((tracers, main // 2 // tracers, cols), jnp.float32),
+        compiler_params=pltpu.CompilerParams(vmem_limit_bytes=4 << 20),
+        cost_estimate=cost(0, 4 * both.size),
+        name="emit",
+    )(both)
+
+
+def backward_kernel(plan, last, numbers, counts, weight, *refs):
+    pieces = refs[: len(numbers)]
+    start = refs[len(numbers)] if last else None
+    out = refs[len(numbers) + last]
+    acc = refs[-1] if last else out
+    slots = weight.shape[-1]
+    main = acc.shape[0]
+    acc[...] = start[...] if last else jnp.zeros_like(acc)
+    lane = lax.broadcasted_iota(jnp.int32, (main, LANE), 1)
+    blank = jnp.zeros((main, LANE), jnp.float32)
+    for k, piece in zip(numbers, pieces):
+        group = plan.returned(k)
+        both = piece[...].astype(jnp.float32)
+        own = jnp.where(plan.core() == 0, both[:main], both[main:]).astype(jnp.bfloat16)
+        grad = jnp.dot(own, weight[0, group], preferred_element_type=jnp.float32)
+        base, shift, size = place(counts, group)
+        turned = [
+            pltpu.roll(jnp.where(lane < size - at * LANE, x, 0.0), shift, axis=1)
+            for at, x in enumerate(columns(grad))
+        ]
+        placed = [
+            jnp.where(lane < shift, before, x) for before, x in zip([blank] + turned, turned + [blank])
+        ]
+        acc[:, pl.ds(base, slots + LANE)] += jnp.concatenate(placed, axis=1)
+    if last:
+        tracers, levels, cols = out.shape
+        for m in range(tracers):
+            out[m] = acc[m * levels : (m + 1) * levels, :cols]
+
+
+def backward(plan, counts, weight, numbers, pieces, start, shape):
+    tracers, levels, cols = shape
+    slots = weight.shape[-1]
     main = tracers * levels
-    slots = weight.shape[-1]
-    window = slots + LANE
-    mine[...] = jnp.zeros_like(mine)
-    theirs[...] = jnp.zeros_like(theirs)
-    for j, piece in enumerate(pieces):
-        group = plan.sent(j)
-        grad = jnp.dot(piece[...], weight[j], preferred_element_type=jnp.float32)
-        lane = lax.broadcasted_iota(jnp.int32, grad.shape, 1)
-        grad = jnp.where(lane < counts[0, group], grad, 0.0)
-        grad = jnp.concatenate([grad, jnp.zeros((2 * main, LANE), jnp.float32)], axis=1)
-        base, shift = place(counts, group, reach, window, cols)
-        grad = pltpu.roll(grad, shift, axis=1)
-        own = jnp.where(plan.core() == 0, grad[:main], grad[main:])
-        other = jnp.where(plan.core() == 0, grad[main:], grad[:main])
-        for m in range(tracers):
-            part = slice(m * levels, (m + 1) * levels)
-            mine[m, :, pl.ds(base, window)] += own[part]
-            theirs[m, :, pl.ds(base, window)] += other[part]
-
-
-def backward(plan, counts, pieces, weight, tracers, levels, cols):
-    rounds, win, slots = weight.shape
-    out = jax.ShapeDtypeStruct((tracers, levels, cols), jnp.float32)
-    return pl.pallas_call(
-        functools.partial(backward_kernel, plan),
-        in_specs=[SMEM] + [VMEM] * (rounds + 1),
-        out_specs=[VMEM, VMEM],
-        out_shape=[out, out],
+    last = start is not None
+    padded = (main, cols + slots)
+    return pl.pallas_call(
+        functools.partial(backward_kernel, plan, int(last), numbers),
+        in_specs=[VMEM] * (2 + len(pieces) + last),
+        out_specs=VMEM,
+        out_shape=jax.ShapeDtypeStruct(shape if last else padded, jnp.float32),
+        scratch_shapes=[pltpu.VMEM(padded, jnp.float32)] if last else [],
         compiler_params=pltpu.CompilerParams(vmem_limit_bytes=12 << 20),
-        cost_estimate=cost(4 * rounds * tracers * levels * win * slots, 2 * weight.size),
-        name="remap_back",
-    )(counts, *pieces, weight)
+        cost_estimate=cost(2 * len(pieces) * main * 512 * slots, weight.size),
+        name="back_last" if last else "back",
+    )(counts, weight, *pieces, *([start] if last else []))
 
 
 def step(trajectory, increment, counts, remap_weight, kappa, courant, vertical, offset):
@@ -436,15 +516,16 @@
     near = [(v, v + 1 if v % 2 else v - 1) for v in range(slabs)]
     far = [(v, v + 2 if v % 2 else v - 2) for v in range(slabs)]
     near, far = ([(a, b) for a, b in way if 0 <= b < slabs] for way in (near, far))
-    traj_too = lax.ppermute(trajectory, "lev", swap)
-    inc_too = lax.ppermute(increment, "lev", swap)
     traj_own, inc_own, border = fetch_border(plan, trajectory, increment)
     ext = lax.ppermute(border, "lev", near)
     ext_too = lax.ppermute(border, "lev", far)
 
+    traj_too = lax.ppermute(trajectory, "lev", swap)
+    inc_too = lax.ppermute(increment, "lev", swap)
+
     w, w_low, w_high = load(plan, remap_weight)
     lines = [x.reshape(1, cols) for x in (courant, vertical, offset)]
-    rows_in = gather(plan, traj_own, inc_own, traj_too, inc_too, ext, ext_too, rows)
+    rows_in = gather(plan, traj_own, inc_own, traj_too, inc_too, ext, ext_too, rows, cols + slots)
     pieces, message_0 = [], None
     for j, route in enumerate(routes):
         message = forward(plan, j, counts, rows_in, *lines, w, w_low, w_high, scale, tail)
@@ -464,13 +545,25 @@
     for piece in pieces:
         others.append(lax.ppermute(piece, "lev", swap))
     whole = [piece.astype(jnp.float32) for piece in pieces + others]
-
-    tangent, *windows = stencil(plan, kappa, whole, *lines, tracers, levels, 1.0 / scale, tail)
-    returned = []
+    final = plan.rounds - 1
+    early = [k for k in range(2 * plan.rounds) if k % plan.rounds != final]
+    late = [final, plan.rounds + final]
+    pick = lambda values, numbers: [values[k] for k in numbers]
+
+    acc, side = assemble(plan, early, pick(whole, early), 1.0 / scale, tail, cols)
+    tangents, *windows = stencil(
+        plan, kappa.reshape(1, -1), acc, side, late, pick(whole, late), *lines, levels, 1.0 / scale, tail
+    )
+    returned, regained = [], []
     for window, route in zip(windows, routes):
         returned.append(lax.ppermute(window, both, [(b, a) for a, b in route]))
-    mine, theirs = backward(plan, counts, returned, w, tracers, levels, cols)
-    return (tangent, mine + lax.ppermute(theirs, "lev", swap))
+    for window in returned:
+        regained.append(lax.ppermute(window, "lev", swap))
+    tangent = emit(plan, tangents, tracers)
+    parts = returned + regained
+    grad = backward(plan, counts, remap_weight, early, pick(parts, early), None, trajectory.shape)
+    grad = backward(plan, counts, remap_weight, late, pick(parts, late), grad, trajectory.shape)
+    return (tangent, grad)
 
 
 def solution(mesh):

time: 50.5 us -> 46.2 us (0.915)
  the two profiles are of different devices: /device:TPU:0 before, /device:TPU:3 now
where the time goes in v1:
time: 46.2 us; the launch traced here: 45.9 us
  starting transfers between devices  31.6 us (68%)
  Pallas kernels  7.58 us (16%)
  local copies, waits for them, and re-layouts  4 us (9%)
  waiting for transfers between devices  1.53 us (3%)
  between operations  0.94 us (2%)
    ppermute x4, starting transfers between devices, step(): others.append(lax.ppermute(piece, 'lev', swap))  12.6 us
    ppermute x4, starting transfers between devices, step(): regained.append(lax.ppermute(window, 'lev', swap))  7.59 us
    ppermute x4, starting transfers between devices, step(): pieces.append(lax.ppermute(message, both, route))  4.4 us
    ppermute x4, starting transfers between devices, step(): returned.append(lax.ppermute(window, both, [(b, a) for a, b in route]))  4.26 us
    unnamed x18, local copies, waits for them, and re-layouts  4 us
    pallas_call x4, Pallas kernels, forward(): pl.pallas_call(functools.partial(forward_kernel, plan, which, scale, tail...  2.55 us
    pallas_call x2, Pallas kernels, backward(): pl.pallas_call(functools.partial(backward_kernel, plan, int(last), number...  1.83 us
    pallas_call x1, Pallas kernels, stencil(): pl.pallas_call(functools.partial(stencil_kernel, plan, unscale, tail, num...  1.47 us
  transfers between devices with their start and end apart: 20, of which 3 were waited for; matrix products, arithmetic and copies ran while one was open for 0% of the time, Pallas kernels for 6%

profile of v1, /device:TPU:3, one launch (start us, length us, event | category | flops | bytes accessed | tf_op | source)
XLA Modules:
  0.0 45.9 jit_solution(6337273104979409737)
XLA Ops:
  0.6 0.7 %collective-permute-start = (bf16[3,8,2048]{2,1,0:T(8,128)(2,1)}, bf16[3,8,2048]{2,1,0:T(8,128)(2,1)S(1)}, u32[]{:S(2)}, u32[]{:S(2)}) collective-permute-start(bf16[3,8,2048]{2,1,0:T(8,128)(2,1)} %traj.1), channel_id=1, source_target_pairs={{0,1},{1,0},{2,3},{3,2},{4,5},{5,4},{6,7},{7,6},{8,9},{9,8},{10,11... | collective-permute-start | bytes 294920 | tf_op jit(solution)/shard_map/ppermute | solution.py:523
  1.5 0.9 %copy-done.5 = bf16[3,8,2048]{2,1,0:T(8,128)(2,1)S(1)} copy-done((bf16[3,8,2048]{2,1,0:T(8,128)(2,1)S(1)}, bf16[3,8,2048]{2,1,0:T(8,128)(2,1)}, u32[]{:S(2)}) %copy-start.5) | copy-done | bytes 98328
  2.3 0.9 %copy-done.6 = bf16[3,8,2048]{2,1,0:T(8,128)(2,1)S(1)} copy-done((bf16[3,8,2048]{2,1,0:T(8,128)(2,1)S(1)}, bf16[3,8,2048]{2,1,0:T(8,128)(2,1)}, u32[]{:S(2)}) %copy-start.6) | copy-done | bytes 98328
  3.2 0.3 border.1
  3.6 1.3 %collective-permute-start.3 = (bf16[9,2048]{1,0:T(8,128)(2,1)S(1)}, bf16[9,2048]{1,0:T(8,128)(2,1)S(1)}, u32[]{:S(2)}, u32[]{:S(2)}) collective-permute-start(bf16[9,2048]{1,0:T(8,128)(2,1)S(1)} %get-tuple-element.17), channel_id=1, source_target_pairs={{1,3},{2,0},{5,7},{6,4},{9,11},{10,8},{13,15},{14,12},{17,19},{18,... | collective-permute-start | bytes 110600 | tf_op jit(solution)/shard_map/ppermute | solution.py:521
  4.9 0.7 %collective-permute-start.2 = (bf16[9,2048]{1,0:T(8,128)(2,1)S(1)}, bf16[9,2048]{1,0:T(8,128)(2,1)S(1)}, u32[]{:S(2)}, u32[]{:S(2)}) collective-permute-start(bf16[9,2048]{1,0:T(8,128)(2,1)S(1)} %get-tuple-element.17), channel_id=1, source_target_pairs={{1,2},{2,1},{5,6},{6,5},{9,10},{10,9},{13,14},{14,13},{17,18},{18,... | collective-permute-start | bytes 110600 | tf_op jit(solution)/shard_map/ppermute | solution.py:520
  5.6 2.2 %copy-done = bf16[1,8,512,512]{3,2,1,0:T(8,128)(2,1)S(1)} copy-done((bf16[1,8,512,512]{3,2,1,0:T(8,128)(2,1)S(1)}, bf16[1,8,512,512]{3,2,1,0:T(8,128)(2,1)}, u32[]{:S(2)}) %copy-start) | copy-done | bytes 4194328
  7.8 0.4 fetch.1
  8.2 0.4 collective-permute-done.3.ext_too
  8.7 0.8 %shard_map.97 = f32[112,512]{1,0:T(8,128)S(1)} custom-call(s32[1,8]{1,0:T(1,128)S(1)} %copy-done.7, f32[112,2560]{1,0:T(8,128)S(1)} %gather.1.rows_in, f32[1,2048]{1,0:T(1,128)S(1)} %bitcast.4, f32[1,2048]{1,0:T(1,128)S(1)} %bitcast.9, s32[1,2048]{1,0:T(1,128)S(1)} %bitcast.14, bf16[4,512,512]{2,1,0:T(8,128)(2,1)S(1)} %get-tuple-element.18.w, ...), custom_call_target="tpu_custom_call" | custom-call | flops 58720256 | bytes 1146880 | tf_op jit(solution)/shard_map/pallas_call | solution.py:255
  9.6 0.8 %shard_map.96 = f32[112,512]{1,0:T(8,128)S(1)} custom-call(s32[1,8]{1,0:T(1,128)S(1)} %copy-done.7, f32[112,2560]{1,0:T(8,128)S(1)} %gather.1.rows_in, f32[1,2048]{1,0:T(1,128)S(1)} %bitcast.5, f32[1,2048]{1,0:T(1,128)S(1)} %bitcast.10, s32[1,2048]{1,0:T(1,128)S(1)} %bitcast.15, bf16[4,512,512]{2,1,0:T(8,128)(2,1)S(1)} %get-tuple-element.18.w, ...), custom_call_target="tpu_custom_call" | custom-call | flops 58720256 | bytes 1146880 | tf_op jit(solution)/shard_map/pallas_call | solution.py:255
  10.4 0.5 %shard_map.95 = f32[112,512]{1,0:T(8,128)S(1)} custom-call(s32[1,8]{1,0:T(1,128)S(1)} %copy-done.7, f32[112,2560]{1,0:T(8,128)S(1)} %gather.1.rows_in, f32[1,2048]{1,0:T(1,128)S(1)} %bitcast.6, f32[1,2048]{1,0:T(1,128)S(1)} %bitcast.11, s32[1,2048]{1,0:T(1,128)S(1)} %bitcast.16, bf16[4,512,512]{2,1,0:T(8,128)(2,1)S(1)} %get-tuple-element.18.w, ...), custom_call_target="tpu_custom_call" | custom-call | flops 58720256 | bytes 1146880 | tf_op jit(solution)/shard_map/pallas_call | solution.py:255
  10.9 1.4 %collective-permute-start.6 = (f16[112,512]{1,0:T(8,128)(2,1)S(1)}, f16[112,512]{1,0:T(8,128)(2,1)S(1)}, u32[]{:S(2)}, u32[]{:S(2)}) collective-permute-start(f16[112,512]{1,0:T(8,128)(2,1)S(1)} %convert_element_type.40), channel_id=1, source_target_pairs={{0,12},{1,9},{2,14},{3,11},{4,8},{5,13},{6,10},{7,15},{8,4},{9,1},... | collective-permute-start | bytes 344072 | tf_op jit(solution)/shard_map/ppermute | solution.py:534
  12.3 2.4 %collective-permute-start.5 = (f16[112,512]{1,0:T(8,128)(2,1)S(1)}, f16[112,512]{1,0:T(8,128)(2,1)S(1)}, u32[]{:S(2)}, u32[]{:S(2)}) collective-permute-start(f16[112,512]{1,0:T(8,128)(2,1)S(1)} %convert_element_type.38), channel_id=1, source_target_pairs={{0,20},{1,17},{2,22},{3,19},{4,16},{5,21},{6,18},{7,23},{8,28},{9,... | collective-permute-start | bytes 344072 | tf_op jit(solution)/shard_map/ppermute | solution.py:534
  14.7 0.5 shard_map.98
  15.2 0.7 %collective-permute-start.10 = (f16[112,512]{1,0:T(8,128)(2,1)S(1)}, f16[112,512]{1,0:T(8,128)(2,1)S(1)}, u32[]{:S(2)}, u32[]{:S(2)}) collective-permute-start(f16[112,512]{1,0:T(8,128)(2,1)S(1)} %convert_element_type.45), channel_id=1, source_target_pairs={{0,4},{1,1},{2,6},{3,3},{4,0},{5,5},{6,2},{7,7},{8,12},{9,9},{10,1... | collective-permute-start | bytes 344072 | tf_op jit(solution)/shard_map/ppermute | solution.py:534
  15.8 7.9 %collective-permute-start.9 = (f16[112,512]{1,0:T(8,128)(2,1)S(1)}, f16[112,512]{1,0:T(8,128)(2,1)S(1)}, u32[]{:S(2)}, u32[]{:S(2)}) collective-permute-start(f16[112,512]{1,0:T(8,128)(2,1)S(1)} %collective-permute-done.6), channel_id=1, source_target_pairs={{0,1},{1,0},{2,3},{3,2},{4,5},{5,4},{6,7},{7,6},{8,9},{9,8},{10,11... | collective-permute-start | bytes 344072 | tf_op jit(solution)/shard_map/ppermute | solution.py:546
  23.8 1.2 %collective-permute-start.8 = (f16[112,512]{1,0:T(8,128)(2,1)S(1)}, f16[112,512]{1,0:T(8,128)(2,1)S(1)}, u32[]{:S(2)}, u32[]{:S(2)}) collective-permute-start(f16[112,512]{1,0:T(8,128)(2,1)S(1)} %collective-permute-done.5), channel_id=1, source_target_pairs={{0,1},{1,0},{2,3},{3,2},{4,5},{5,4},{6,7},{7,6},{8,9},{9,8},{10,11... | collective-permute-start | bytes 344072 | tf_op jit(solution)/shard_map/ppermute | solution.py:546
  24.9 2.3 %collective-permute-start.7 = (f16[112,512]{1,0:T(8,128)(2,1)S(1)}, f16[112,512]{1,0:T(8,128)(2,1)S(1)}, u32[]{:S(2)}, u32[]{:S(2)}) collective-permute-start(f16[112,512]{1,0:T(8,128)(2,1)S(1)} %collective-permute-done.4), channel_id=1, source_target_pairs={{0,1},{1,0},{2,3},{3,2},{4,5},{5,4},{6,7},{7,6},{8,9},{9,8},{10,11... | collective-permute-start | bytes 344072 | tf_op jit(solution)/shard_map/ppermute | solution.py:546
  27.2 1.2 %collective-permute-start.11 = (f16[112,512]{1,0:T(8,128)(2,1)S(1)}, f16[112,512]{1,0:T(8,128)(2,1)S(1)}, u32[]{:S(2)}, u32[]{:S(2)}) collective-permute-start(f16[112,512]{1,0:T(8,128)(2,1)S(1)} %collective-permute-done.10), channel_id=1, source_target_pairs={{0,1},{1,0},{2,3},{3,2},{4,5},{5,4},{6,7},{7,6},{8,9},{9,8},{10,11... | collective-permute-start | bytes 344072 | tf_op jit(solution)/shard_map/ppermute | solution.py:546
  28.9 0.5 %collective-permute-done.11 = f16[112,512]{1,0:T(8,128)(2,1)S(1)} collective-permute-done((f16[112,512]{1,0:T(8,128)(2,1)S(1)}, f16[112,512]{1,0:T(8,128)(2,1)S(1)}, u32[]{:S(2)}, u32[]{:S(2)}) %collective-permute-start.11) | collective-permute-done | bytes 114720 | tf_op jit(solution)/shard_map/ppermute | solution.py:546
  29.4 1.5 %stencil.1 = (f32[48,2048]{1,0:T(8,128)S(1)}, bf16[48,512]{1,0:T(8,128)(2,1)S(1)}, bf16[48,512]{1,0:T(8,128)(2,1)S(1)}, bf16[48,512]{1,0:T(8,128)(2,1)S(1)}, bf16[48,512]{1,0:T(8,128)(2,1)S(1)}) custom-call(f32[1,3]{1,0:T(1,128)S(1)} %bitcast.19, f32[112,2176]{1,0:T(8,128)S(1)} %get-tuple-element.21.acc_in, f32[32,128]{1,0:T(8,128)S(1)} %get-tuple-element.22.side, ...), custom_call_target="tpu_custom_call" | custom-call | flops 22937600 | bytes 1835008 | tf_op jit(solution)/shard_map/stencil/pallas_call | solution.py:417
  30.9 2.9 %collective-permute-start.14 = (bf16[48,512]{1,0:T(8,128)(2,1)S(1)}, bf16[48,512]{1,0:T(8,128)(2,1)S(1)}, u32[]{:S(2)}, u32[]{:S(2)}) collective-permute-start(bf16[48,512]{1,0:T(8,128)(2,1)S(1)} %get-tuple-element.25), channel_id=1, source_target_pairs={{28,0},{25,1},{30,2},{27,3},{24,4},{29,5},{26,6},{31,7},{20,8},{17... | collective-permute-start | bytes 147464 | tf_op jit(solution)/shard_map/ppermute | solution.py:559
  33.8 0.7 %collective-permute-start.16 = (bf16[48,512]{1,0:T(8,128)(2,1)S(1)}, bf16[48,512]{1,0:T(8,128)(2,1)S(1)}, u32[]{:S(2)}, u32[]{:S(2)}) collective-permute-start(bf16[48,512]{1,0:T(8,128)(2,1)S(1)} %get-tuple-element.27), channel_id=1, source_target_pairs={{12,0},{9,1},{14,2},{11,3},{8,4},{13,5},{10,6},{15,7},{4,8},{1,9},... | collective-permute-start | bytes 147464 | tf_op jit(solution)/shard_map/ppermute | solution.py:559
  34.5 0.7 %collective-permute-start.12 = (bf16[48,512]{1,0:T(8,128)(2,1)S(1)}, bf16[48,512]{1,0:T(8,128)(2,1)S(1)}, u32[]{:S(2)}, u32[]{:S(2)}) collective-permute-start(bf16[48,512]{1,0:T(8,128)(2,1)S(1)} %get-tuple-element.24), channel_id=1, source_target_pairs={{4,0},{1,1},{6,2},{3,3},{0,4},{5,5},{2,6},{7,7},{12,8},{9,9},{14,1... | collective-permute-start | bytes 147464 | tf_op jit(solution)/shard_map/ppermute | solution.py:559
  35.2 0.5 %collective-permute-done.14.refs_0_ = bf16[48,512]{1,0:T(8,128)(2,1)S(1)} collective-permute-done((bf16[48,512]{1,0:T(8,128)(2,1)S(1)}, bf16[48,512]{1,0:T(8,128)(2,1)S(1)}, u32[]{:S(2)}, u32[]{:S(2)}) %collective-permute-start.14) | collective-permute-done | bytes 49184 | tf_op jit(solution)/shard_map/ppermute | solution.py:559
  35.7 4.3 %collective-permute-start.17 = (bf16[48,512]{1,0:T(8,128)(2,1)S(1)}, bf16[48,512]{1,0:T(8,128)(2,1)S(1)}, u32[]{:S(2)}, u32[]{:S(2)}) collective-permute-start(bf16[48,512]{1,0:T(8,128)(2,1)S(1)} %collective-permute-done.14.refs_0_), channel_id=1, source_target_pairs={{0,1},{1,0},{2,3},{3,2},{4,5},{5,4},{6,7},{7,6},{8,9},{9,8},{10,11... | collective-permute-start | bytes 147464 | tf_op jit(solution)/shard_map/ppermute | solution.py:561
  40.0 0.3 collective-permute-start.18
  40.6 2.7 %collective-permute-start.13 = (bf16[48,512]{1,0:T(8,128)(2,1)S(1)}, bf16[48,512]{1,0:T(8,128)(2,1)S(1)}, u32[]{:S(2)}, u32[]{:S(2)}) collective-permute-start(bf16[48,512]{1,0:T(8,128)(2,1)S(1)} %collective-permute-done.12.refs_0_), channel_id=1, source_target_pairs={{0,1},{1,0},{2,3},{3,2},{4,5},{5,4},{6,7},{7,6},{8,9},{9,8},{10,11... | collective-permute-start | bytes 147464 | tf_op jit(solution)/shard_map/ppermute | solution.py:561
  43.3 0.7 %emit.1 = f32[3,8,2048]{2,1,0:T(8,128)} custom-call(f32[48,2048]{1,0:T(8,128)S(1)} %get-tuple-element.23.both), custom_call_target="tpu_custom_call" | custom-call | bytes 393216 | tf_op jit(solution)/shard_map/emit/pallas_call | solution.py:443
  44.0 0.7 %back.1.refs_2_ = f32[24,2560]{1,0:T(8,128)S(1)} custom-call(s32[1,8]{1,0:T(1,128)S(1)} %copy-done.7, bf16[1,8,512,512]{3,2,1,0:T(8,128)(2,1)S(1)} %copy-done.1, bf16[48,512]{1,0:T(8,128)(2,1)S(1)} %collective-permute-done.14.refs_0_, bf16[48,512]{1,0:T(8,128)(2,1)S(1)} %collective-permute-done.15.refs_1_, ...), custom_call_target="tpu_custom_call" | custom-call | flops 75497472 | bytes 2097152 | tf_op jit(solution)/shard_map/back/pallas_call | solution.py:490
  44.8 1.1 %back_last.1 = f32[3,8,2048]{2,1,0:T(8,128)} custom-call(s32[1,8]{1,0:T(1,128)S(1)} %copy-done.7, bf16[1,8,512,512]{3,2,1,0:T(8,128)(2,1)S(1)} %copy-done.1, bf16[48,512]{1,0:T(8,128)(2,1)S(1)} %collective-permute-done.12.refs_0_, bf16[48,512]{1,0:T(8,128)(2,1)S(1)} %collective-permute-done.13.refs_1_, f32[24,2560]{1,0:T(8,128)S(1)} %back.1.refs_2_), custom_call_target="tpu_custom_call" | custom-call | flops 25165824 | bytes 2097152 | tf_op jit(solution)/shard_map/back_last/pallas_call | solution.py:490
  (50 shorter events, 0.9 us)
Async XLA Ops:
  0.6 8.0 %collective-permute-start = (bf16[3,8,2048]{2,1,0:T(8,128)(2,1)}, bf16[3,8,2048]{2,1,0:T(8,128)(2,1)S(1)}, u32[]{:S(2)}, u32[]{:S(2)}) collective-permute-start(bf16[3,8,2048]{2,1,0:T(8,128)(2,1)} %traj.1), channel_id=1, source_target_pairs={{0,1},{1,0},{2,3},{3,2},{4,5},{5,4},{6,7},{7,6},{8,9},{9,8},{10,11... | collective-permute-start | bytes 294920 | tf_op jit(solution)/shard_map/ppermute | solution.py:523
  1.4 7.2 %collective-permute-start.1 = (bf16[3,8,2048]{2,1,0:T(8,128)(2,1)}, bf16[3,8,2048]{2,1,0:T(8,128)(2,1)S(1)}, u32[]{:S(2)}, u32[]{:S(2)}) collective-permute-start(bf16[3,8,2048]{2,1,0:T(8,128)(2,1)} %inc.1), channel_id=1, source_target_pairs={{0,1},{1,0},{2,3},{3,2},{4,5},{5,4},{6,7},{7,6},{8,9},{9,8},{10,11... | collective-permute-start | bytes 294920 | tf_op jit(solution)/shard_map/ppermute | solution.py:524
  1.4 0.9 %copy-start.5 = (bf16[3,8,2048]{2,1,0:T(8,128)(2,1)S(1)}, bf16[3,8,2048]{2,1,0:T(8,128)(2,1)}, u32[]{:S(2)}) copy-start(bf16[3,8,2048]{2,1,0:T(8,128)(2,1)} %traj.1) | copy-start | bytes 294916
  2.3 0.9 %copy-start.6 = (bf16[3,8,2048]{2,1,0:T(8,128)(2,1)S(1)}, bf16[3,8,2048]{2,1,0:T(8,128)(2,1)}, u32[]{:S(2)}) copy-start(bf16[3,8,2048]{2,1,0:T(8,128)(2,1)} %inc.1) | copy-start | bytes 294916
  3.6 5.1 %copy-start.7 = (s32[1,8]{1,0:T(1,128)S(1)}, s32[1,8]{1,0:T(1,128)}, u32[]{:S(2)}) copy-start(s32[1,8]{1,0:T(1,128)} %counts.11) | copy-start | bytes 100
  3.6 5.0 %collective-permute-start.3 = (bf16[9,2048]{1,0:T(8,128)(2,1)S(1)}, bf16[9,2048]{1,0:T(8,128)(2,1)S(1)}, u32[]{:S(2)}, u32[]{:S(2)}) collective-permute-start(bf16[9,2048]{1,0:T(8,128)(2,1)S(1)} %get-tuple-element.17), channel_id=1, source_target_pairs={{1,3},{2,0},{5,7},{6,4},{9,11},{10,8},{13,15},{14,12},{17,19},{18,... | collective-permute-start | bytes 110600 | tf_op jit(solution)/shard_map/ppermute | solution.py:521
  4.9 3.7 %collective-permute-start.2 = (bf16[9,2048]{1,0:T(8,128)(2,1)S(1)}, bf16[9,2048]{1,0:T(8,128)(2,1)S(1)}, u32[]{:S(2)}, u32[]{:S(2)}) collective-permute-start(bf16[9,2048]{1,0:T(8,128)(2,1)S(1)} %get-tuple-element.17), channel_id=1, source_target_pairs={{1,2},{2,1},{5,6},{6,5},{9,10},{10,9},{13,14},{14,13},{17,18},{18,... | collective-permute-start | bytes 110600 | tf_op jit(solution)/shard_map/ppermute | solution.py:520
  5.6 2.2 %copy-start = (bf16[1,8,512,512]{3,2,1,0:T(8,128)(2,1)S(1)}, bf16[1,8,512,512]{3,2,1,0:T(8,128)(2,1)}, u32[]{:S(2)}) copy-start(bf16[1,8,512,512]{3,2,1,0:T(8,128)(2,1)} %weight.5) | copy-start | bytes 12582916
  7.8 1.0 %copy-start.2 = (f32[2048]{0:T(1024)S(1)}, f32[2048]{0:T(1024)}, u32[]{:S(2)}) copy-start(f32[2048]{0:T(1024)} %param.13) | copy-start | bytes 24580
  7.8 1.0 %copy-start.3 = (f32[2048]{0:T(1024)S(1)}, f32[2048]{0:T(1024)}, u32[]{:S(2)}) copy-start(f32[2048]{0:T(1024)} %param.14) | copy-start | bytes 24580
  7.8 1.0 %copy-start.4 = (s32[2048]{0:T(1024)S(1)}, s32[2048]{0:T(1024)}, u32[]{:S(2)}) copy-start(s32[2048]{0:T(1024)} %param.15) | copy-start | bytes 24580
  10.9 5.0 %collective-permute-start.6 = (f16[112,512]{1,0:T(8,128)(2,1)S(1)}, f16[112,512]{1,0:T(8,128)(2,1)S(1)}, u32[]{:S(2)}, u32[]{:S(2)}) collective-permute-start(f16[112,512]{1,0:T(8,128)(2,1)S(1)} %convert_element_type.40), channel_id=1, source_target_pairs={{0,12},{1,9},{2,14},{3,11},{4,8},{5,13},{6,10},{7,15},{8,4},{9,1},... | collective-permute-start | bytes 344072 | tf_op jit(solution)/shard_map/ppermute | solution.py:534
  12.3 11.5 %collective-permute-start.5 = (f16[112,512]{1,0:T(8,128)(2,1)S(1)}, f16[112,512]{1,0:T(8,128)(2,1)S(1)}, u32[]{:S(2)}, u32[]{:S(2)}) collective-permute-start(f16[112,512]{1,0:T(8,128)(2,1)S(1)} %convert_element_type.38), channel_id=1, source_target_pairs={{0,20},{1,17},{2,22},{3,19},{4,16},{5,21},{6,18},{7,23},{8,28},{9,... | collective-permute-start | bytes 344072 | tf_op jit(solution)/shard_map/ppermute | solution.py:534
  14.6 10.3 %collective-permute-start.4 = (f16[112,512]{1,0:T(8,128)(2,1)S(1)}, f16[112,512]{1,0:T(8,128)(2,1)S(1)}, u32[]{:S(2)}, u32[]{:S(2)}) collective-permute-start(f16[112,512]{1,0:T(8,128)(2,1)S(1)} %convert_element_type.36), channel_id=1, source_target_pairs={{0,28},{1,25},{2,30},{3,27},{4,24},{5,29},{6,26},{7,31},{8,20},{9,... | collective-permute-start | bytes 344072 | tf_op jit(solution)/shard_map/ppermute | solution.py:534
  15.1 14.3 %copy-start.8 = (f32[3]{0:T(128)S(1)}, f32[3]{0:T(128)}, u32[]{:S(2)}) copy-start(f32[3]{0:T(128)} %param.12) | copy-start | bytes 40
  15.2 12.1 %collective-permute-start.10 = (f16[112,512]{1,0:T(8,128)(2,1)S(1)}, f16[112,512]{1,0:T(8,128)(2,1)S(1)}, u32[]{:S(2)}, u32[]{:S(2)}) collective-permute-start(f16[112,512]{1,0:T(8,128)(2,1)S(1)} %convert_element_type.45), channel_id=1, source_target_pairs={{0,4},{1,1},{2,6},{3,3},{4,0},{5,5},{6,2},{7,7},{8,12},{9,9},{10,1... | collective-permute-start | bytes 344072 | tf_op jit(solution)/shard_map/ppermute | solution.py:534
  15.8 12.7 %collective-permute-start.9 = (f16[112,512]{1,0:T(8,128)(2,1)S(1)}, f16[112,512]{1,0:T(8,128)(2,1)S(1)}, u32[]{:S(2)}, u32[]{:S(2)}) collective-permute-start(f16[112,512]{1,0:T(8,128)(2,1)S(1)} %collective-permute-done.6), channel_id=1, source_target_pairs={{0,1},{1,0},{2,3},{3,2},{4,5},{5,4},{6,7},{7,6},{8,9},{9,8},{10,11... | collective-permute-start | bytes 344072 | tf_op jit(solution)/shard_map/ppermute | solution.py:546
  23.8 4.8 %collective-permute-start.8 = (f16[112,512]{1,0:T(8,128)(2,1)S(1)}, f16[112,512]{1,0:T(8,128)(2,1)S(1)}, u32[]{:S(2)}, u32[]{:S(2)}) collective-permute-start(f16[112,512]{1,0:T(8,128)(2,1)S(1)} %collective-permute-done.5), channel_id=1, source_target_pairs={{0,1},{1,0},{2,3},{3,2},{4,5},{5,4},{6,7},{7,6},{8,9},{9,8},{10,11... | collective-permute-start | bytes 344072 | tf_op jit(solution)/shard_map/ppermute | solution.py:546
  24.9 3.6 %collective-permute-start.7 = (f16[112,512]{1,0:T(8,128)(2,1)S(1)}, f16[112,512]{1,0:T(8,128)(2,1)S(1)}, u32[]{:S(2)}, u32[]{:S(2)}) collective-permute-start(f16[112,512]{1,0:T(8,128)(2,1)S(1)} %collective-permute-done.4), channel_id=1, source_target_pairs={{0,1},{1,0},{2,3},{3,2},{4,5},{5,4},{6,7},{7,6},{8,9},{9,8},{10,11... | collective-permute-start | bytes 344072 | tf_op jit(solution)/shard_map/ppermute | solution.py:546
  27.2 2.1 %collective-permute-start.11 = (f16[112,512]{1,0:T(8,128)(2,1)S(1)}, f16[112,512]{1,0:T(8,128)(2,1)S(1)}, u32[]{:S(2)}, u32[]{:S(2)}) collective-permute-start(f16[112,512]{1,0:T(8,128)(2,1)S(1)} %collective-permute-done.10), channel_id=1, source_target_pairs={{0,1},{1,0},{2,3},{3,2},{4,5},{5,4},{6,7},{7,6},{8,9},{9,8},{10,11... | collective-permute-start | bytes 344072 | tf_op jit(solution)/shard_map/ppermute | solution.py:546
  28.6 15.4 %copy-start.1 = (bf16[1,8,512,512]{3,2,1,0:T(8,128)(2,1)S(1)}, bf16[1,8,512,512]{3,2,1,0:T(8,128)(2,1)}, u32[]{:S(2)}) copy-start(bf16[1,8,512,512]{3,2,1,0:T(8,128)(2,1)} %weight.5) | copy-start | bytes 12582916
  30.9 4.8 %collective-permute-start.14 = (bf16[48,512]{1,0:T(8,128)(2,1)S(1)}, bf16[48,512]{1,0:T(8,128)(2,1)S(1)}, u32[]{:S(2)}, u32[]{:S(2)}) collective-permute-start(bf16[48,512]{1,0:T(8,128)(2,1)S(1)} %get-tuple-element.25), channel_id=1, source_target_pairs={{28,0},{25,1},{30,2},{27,3},{24,4},{29,5},{26,6},{31,7},{20,8},{17... | collective-permute-start | bytes 147464 | tf_op jit(solution)/shard_map/ppermute | solution.py:559
  33.8 6.2 %collective-permute-start.15 = (bf16[48,512]{1,0:T(8,128)(2,1)S(1)}, bf16[48,512]{1,0:T(8,128)(2,1)S(1)}, u32[]{:S(2)}, u32[]{:S(2)}) collective-permute-start(bf16[48,512]{1,0:T(8,128)(2,1)S(1)} %get-tuple-element.26), channel_id=1, source_target_pairs={{20,0},{17,1},{22,2},{19,3},{16,4},{21,5},{18,6},{23,7},{28,8},{25... | collective-permute-start | bytes 147464 | tf_op jit(solution)/shard_map/ppermute | solution.py:559
  33.8 6.5 %collective-permute-start.16 = (bf16[48,512]{1,0:T(8,128)(2,1)S(1)}, bf16[48,512]{1,0:T(8,128)(2,1)S(1)}, u32[]{:S(2)}, u32[]{:S(2)}) collective-permute-start(bf16[48,512]{1,0:T(8,128)(2,1)S(1)} %get-tuple-element.27), channel_id=1, source_target_pairs={{12,0},{9,1},{14,2},{11,3},{8,4},{13,5},{10,6},{15,7},{4,8},{1,9},... | collective-permute-start | bytes 147464 | tf_op jit(solution)/shard_map/ppermute | solution.py:559
  34.5 6.1 %collective-permute-start.12 = (bf16[48,512]{1,0:T(8,128)(2,1)S(1)}, bf16[48,512]{1,0:T(8,128)(2,1)S(1)}, u32[]{:S(2)}, u32[]{:S(2)}) collective-permute-start(bf16[48,512]{1,0:T(8,128)(2,1)S(1)} %get-tuple-element.24), channel_id=1, source_target_pairs={{4,0},{1,1},{6,2},{3,3},{0,4},{5,5},{2,6},{7,7},{12,8},{9,9},{14,1... | collective-permute-start | bytes 147464 | tf_op jit(solution)/shard_map/ppermute | solution.py:559
  35.7 8.3 %collective-permute-start.17 = (bf16[48,512]{1,0:T(8,128)(2,1)S(1)}, bf16[48,512]{1,0:T(8,128)(2,1)S(1)}, u32[]{:S(2)}, u32[]{:S(2)}) collective-permute-start(bf16[48,512]{1,0:T(8,128)(2,1)S(1)} %collective-permute-done.14.refs_0_), channel_id=1, source_target_pairs={{0,1},{1,0},{2,3},{3,2},{4,5},{5,4},{6,7},{7,6},{8,9},{9,8},{10,11... | collective-permute-start | bytes 147464 | tf_op jit(solution)/shard_map/ppermute | solution.py:561
  40.0 3.9 %collective-permute-start.18 = (bf16[48,512]{1,0:T(8,128)(2,1)S(1)}, bf16[48,512]{1,0:T(8,128)(2,1)S(1)}, u32[]{:S(2)}, u32[]{:S(2)}) collective-permute-start(bf16[48,512]{1,0:T(8,128)(2,1)S(1)} %collective-permute-done.15.refs_1_), channel_id=1, source_target_pairs={{0,1},{1,0},{2,3},{3,2},{4,5},{5,4},{6,7},{7,6},{8,9},{9,8},{10,11... | collective-permute-start | bytes 147464 | tf_op jit(solution)/shard_map/ppermute | solution.py:561
  40.3 3.7 %collective-permute-start.19 = (bf16[48,512]{1,0:T(8,128)(2,1)S(1)}, bf16[48,512]{1,0:T(8,128)(2,1)S(1)}, u32[]{:S(2)}, u32[]{:S(2)}) collective-permute-start(bf16[48,512]{1,0:T(8,128)(2,1)S(1)} %collective-permute-done.16.refs_2_), channel_id=1, source_target_pairs={{0,1},{1,0},{2,3},{3,2},{4,5},{5,4},{6,7},{7,6},{8,9},{9,8},{10,11... | collective-permute-start | bytes 147464 | tf_op jit(solution)/shard_map/ppermute | solution.py:561
  40.6 4.2 %collective-permute-start.13 = (bf16[48,512]{1,0:T(8,128)(2,1)S(1)}, bf16[48,512]{1,0:T(8,128)(2,1)S(1)}, u32[]{:S(2)}, u32[]{:S(2)}) collective-permute-start(bf16[48,512]{1,0:T(8,128)(2,1)S(1)} %collective-permute-done.12.refs_0_), channel_id=1, source_target_pairs={{0,1},{1,0},{2,3},{3,2},{4,5},{5,4},{6,7},{7,6},{8,9},{9,8},{10,11... | collective-permute-start | bytes 147464 | tf_op jit(solution)/shard_map/ppermute | solution.py:561

commit v2 on v1

--- a/solution.py
+++ b/solution.py
@@ -55,9 +55,19 @@
         self.rounds = reach // 2
         self.cube = tiles == reach and tiles & (tiles - 1) == 0
         if self.cube:
-            self.hops = [list(range(reach - 1, 0, -2)), list(range(reach - 2, -1, -2))]
+            self.hops = self.balanced(reach)
         else:
             self.hops = [list(range(-(reach // 2), 0)), list(range(reach // 2 - 1, -1, -1))]
+
+    def balanced(self, reach):
+        hops, load = [[], []], [0, 0]
+        for flip in range(reach - 1, -1, -1):
+            core = 0 if (load[0], len(hops[0])) < (load[1], len(hops[1])) else 1
+            core = 1 if flip == 0 or len(hops[0]) == self.rounds else core
+            core = 0 if len(hops[1]) == self.rounds - (flip > 0) else core
+            hops[core].append(flip)
+            load[core] += (flip >> 1) + (flip & 1)
+        return hops
 
     def target(self, tile, core, j):
         hop = self.hops[core][j]
@@ -97,7 +107,7 @@
         return self.core() if k < self.rounds else 1 - self.core()
 
 
-def border_kernel(plan, traj, inc, traj_out, inc_out, border, sems):
+def border_kernel(plan, traj, inc, traj_out, inc_out, border, lines, sems):
     copies = [
         pltpu.make_async_copy(traj, traj_out, sems.at[0]),
         pltpu.make_async_copy(inc, inc_out, sems.at[1]),
@@ -106,7 +116,7 @@
         copy.start()
     for copy in copies:
         copy.wait()
-    tracers, levels, _ = traj_out.shape
+    tracers, levels, cols = traj_out.shape
     lower = plan.core() == 1
     row = 0
     for ref, depth in ((traj_out, 0), (inc_out, 0), (inc_out, 1)):
@@ -114,19 +124,37 @@
             x = ref[m].astype(jnp.float32)
             low, high = levels - 1 - depth, depth
             line = jnp.where(lower, x[low : low + 1], x[high : high + 1])
-            border[row : row + 1, :] = line.astype(border.dtype)
+            if row < SUB:
+                lines[row : row + 1, :cols] = line
+            else:
+                part = cols // SUB
+                at = cols + (row - SUB) * part
+                for piece in range(SUB):
+                    lines[piece : piece + 1, at : at + part] = line[:, piece * part : (piece + 1) * part]
             row += 1
+    border[...] = lines[...].astype(border.dtype)
+
+
+def unpacked(border, count, cols):
+    part = cols // SUB
+    rows = [border[:, :cols]]
+    for row in range(SUB, count):
+        at = cols + (row - SUB) * part
+        pieces = [border[piece : piece + 1, at : at + part] for piece in range(SUB)]
+        rows.append(jnp.concatenate(pieces, axis=1))
+    return jnp.concatenate(rows, axis=0)[:count]
 
 
 def fetch_border(plan, traj, inc):
     tracers, _, cols = traj.shape
     like = lambda *shape: jax.ShapeDtypeStruct(shape, traj.dtype)
+    wide = cols + max(0, EDGE * tracers - SUB) * (cols // SUB)
     return pl.pallas_call(
         functools.partial(border_kernel, plan),
         in_specs=[HBM] * 2,
         out_specs=[VMEM] * 3,
-        out_shape=[like(*traj.shape), like(*inc.shape), like(EDGE * tracers, cols)],
-        scratch_shapes=[pltpu.SemaphoreType.DMA((2,))],
+        out_shape=[like(*traj.shape), like(*inc.shape), like(SUB, wide)],
+        scratch_shapes=[pltpu.VMEM((SUB, wide), jnp.float32), pltpu.SemaphoreType.DMA((2,))],
         compiler_params=pltpu.CompilerParams(vmem_limit_bytes=4 << 20),
         cost_estimate=cost(0, 8 * traj.size),
         name="border",
@@ -191,7 +219,7 @@
     rows_out[:, cols:] = jnp.zeros_like(rows_out[:, cols:])
     rows_out[4 * main :, :cols] = jnp.zeros_like(rows_out[4 * main :, :cols])
     beyond = ext[...].astype(jnp.float32) + ext_too[...].astype(jnp.float32)
-    rows_out[4 * main : 4 * main + EDGE * tracers, :cols] = beyond
+    rows_out[4 * main : 4 * main + EDGE * tracers, :cols] = unpacked(beyond, EDGE * tracers, cols)
 
 
 def gather(plan, traj, inc, traj_too, inc_too, ext, ext_too, rows, cols):

time: 46.2 us -> 45.2 us (0.978)
  the two profiles are of different devices: /device:TPU:3 before, /device:TPU:1 now
where the time goes in v2:
time: 45.2 us; the launch traced here: 44.9 us
  starting transfers between devices  23.4 us (52%)
  waiting for transfers between devices  8.46 us (19%)
  Pallas kernels  7.94 us (18%)
  local copies, waits for them, and re-layouts  3.99 us (9%)
  between operations  0.92 us (2%)
    ppermute x4, waiting for transfers between devices, step(): pieces.append(lax.ppermute(message, both, route))  5.54 us
    ppermute x4, starting transfers between devices, step(): pieces.append(lax.ppermute(message, both, route))  5.54 us
    ppermute x4, starting transfers between devices, step(): regained.append(lax.ppermute(window, 'lev', swap))  5.25 us
    ppermute x4, starting transfers between devices, step(): returned.append(lax.ppermute(window, both, [(b, a) for a, b in route]))  5.17 us
    ppermute x1, starting transfers between devices, step(): ext_too = lax.ppermute(border, 'lev', far)  4.18 us
    unnamed x18, local copies, waits for them, and re-layouts  3.99 us
    pallas_call x4, Pallas kernels, forward(): pl.pallas_call(functools.partial(forward_kernel, plan, which, scale, tail...  2.89 us
    ppermute x1, starting transfers between devices, step(): ext = lax.ppermute(border, 'lev', near)  1.92 us
  transfers between devices with their start and end apart: 20, of which 7 were waited for; matrix products, arithmetic and copies ran while one was open for 0% of the time, Pallas kernels for 6%

profile of v2, /device:TPU:1, one launch (start us, length us, event | category | flops | bytes accessed | tf_op | source)
XLA Modules:
  0.0 44.9 jit_solution(3690894380837733815)
XLA Ops:
  0.7 0.5 %collective-permute-start.1 = (bf16[3,8,2048]{2,1,0:T(8,128)(2,1)}, bf16[3,8,2048]{2,1,0:T(8,128)(2,1)S(1)}, u32[]{:S(2)}, u32[]{:S(2)}) collective-permute-start(bf16[3,8,2048]{2,1,0:T(8,128)(2,1)} %inc.1), channel_id=1, source_target_pairs={{0,1},{1,0},{2,3},{3,2},{4,5},{5,4},{6,7},{7,6},{8,9},{9,8},{10,11... | collective-permute-start | bytes 294920 | tf_op jit(solution)/shard_map/ppermute | solution.py:552
  1.2 0.9 %copy-done.5 = bf16[3,8,2048]{2,1,0:T(8,128)(2,1)S(1)} copy-done((bf16[3,8,2048]{2,1,0:T(8,128)(2,1)S(1)}, bf16[3,8,2048]{2,1,0:T(8,128)(2,1)}, u32[]{:S(2)}) %copy-start.5) | copy-done | bytes 98328
  2.1 0.9 %copy-done.6 = bf16[3,8,2048]{2,1,0:T(8,128)(2,1)S(1)} copy-done((bf16[3,8,2048]{2,1,0:T(8,128)(2,1)S(1)}, bf16[3,8,2048]{2,1,0:T(8,128)(2,1)}, u32[]{:S(2)}) %copy-start.6) | copy-done | bytes 98328
  3.0 0.3 border.1
  3.4 4.2 %collective-permute-start.3 = (bf16[8,2304]{1,0:T(8,128)(2,1)S(1)}, bf16[8,2304]{1,0:T(8,128)(2,1)S(1)}, u32[]{:S(2)}, u32[]{:S(2)}) collective-permute-start(bf16[8,2304]{1,0:T(8,128)(2,1)S(1)} %get-tuple-element.17), channel_id=1, source_target_pairs={{1,3},{2,0},{5,7},{6,4},{9,11},{10,8},{13,15},{14,12},{17,19},{18,... | collective-permute-start | bytes 110600 | tf_op jit(solution)/shard_map/ppermute | solution.py:549
  7.5 1.9 %collective-permute-start.2 = (bf16[8,2304]{1,0:T(8,128)(2,1)S(1)}, bf16[8,2304]{1,0:T(8,128)(2,1)S(1)}, u32[]{:S(2)}, u32[]{:S(2)}) collective-permute-start(bf16[8,2304]{1,0:T(8,128)(2,1)S(1)} %get-tuple-element.17), channel_id=1, source_target_pairs={{1,2},{2,1},{5,6},{6,5},{9,10},{10,9},{13,14},{14,13},{17,18},{18,... | collective-permute-start | bytes 110600 | tf_op jit(solution)/shard_map/ppermute | solution.py:548
  9.5 2.2 %copy-done = bf16[1,8,512,512]{3,2,1,0:T(8,128)(2,1)S(1)} copy-done((bf16[1,8,512,512]{3,2,1,0:T(8,128)(2,1)S(1)}, bf16[1,8,512,512]{3,2,1,0:T(8,128)(2,1)}, u32[]{:S(2)}) %copy-start) | copy-done | bytes 4194328
  11.7 0.4 fetch.1
  12.1 0.7 %collective-permute-done.2.ext = bf16[8,2304]{1,0:T(8,128)(2,1)S(1)} collective-permute-done((bf16[8,2304]{1,0:T(8,128)(2,1)S(1)}, bf16[8,2304]{1,0:T(8,128)(2,1)S(1)}, u32[]{:S(2)}, u32[]{:S(2)}) %collective-permute-start.2) | collective-permute-done | bytes 36896 | tf_op jit(solution)/shard_map/ppermute | solution.py:548
  12.9 1.2 %shard_map.97 = f32[112,512]{1,0:T(8,128)S(1)} custom-call(s32[1,8]{1,0:T(1,128)S(1)} %copy-done.7, f32[112,2560]{1,0:T(8,128)S(1)} %gather.1.rows_in, f32[1,2048]{1,0:T(1,128)S(1)} %bitcast.4, f32[1,2048]{1,0:T(1,128)S(1)} %bitcast.9, s32[1,2048]{1,0:T(1,128)S(1)} %bitcast.14, bf16[4,512,512]{2,1,0:T(8,128)(2,1)S(1)} %get-tuple-element.18.w, ...), custom_call_target="tpu_custom_call" | custom-call | flops 58720256 | bytes 1146880 | tf_op jit(solution)/shard_map/pallas_call | solution.py:283
  14.1 0.8 %shard_map.96 = f32[112,512]{1,0:T(8,128)S(1)} custom-call(s32[1,8]{1,0:T(1,128)S(1)} %copy-done.7, f32[112,2560]{1,0:T(8,128)S(1)} %gather.1.rows_in, f32[1,2048]{1,0:T(1,128)S(1)} %bitcast.5, f32[1,2048]{1,0:T(1,128)S(1)} %bitcast.10, s32[1,2048]{1,0:T(1,128)S(1)} %bitcast.15, bf16[4,512,512]{2,1,0:T(8,128)(2,1)S(1)} %get-tuple-element.18.w, ...), custom_call_target="tpu_custom_call" | custom-call | flops 58720256 | bytes 1146880 | tf_op jit(solution)/shard_map/pallas_call | solution.py:283
  14.9 0.5 %shard_map.95 = f32[112,512]{1,0:T(8,128)S(1)} custom-call(s32[1,8]{1,0:T(1,128)S(1)} %copy-done.7, f32[112,2560]{1,0:T(8,128)S(1)} %gather.1.rows_in, f32[1,2048]{1,0:T(1,128)S(1)} %bitcast.6, f32[1,2048]{1,0:T(1,128)S(1)} %bitcast.11, s32[1,2048]{1,0:T(1,128)S(1)} %bitcast.16, bf16[4,512,512]{2,1,0:T(8,128)(2,1)S(1)} %get-tuple-element.18.w, ...), custom_call_target="tpu_custom_call" | custom-call | flops 58720256 | bytes 1146880 | tf_op jit(solution)/shard_map/pallas_call | solution.py:283
  15.4 1.9 %collective-permute-start.6 = (f16[112,512]{1,0:T(8,128)(2,1)S(1)}, f16[112,512]{1,0:T(8,128)(2,1)S(1)}, u32[]{:S(2)}, u32[]{:S(2)}) collective-permute-start(f16[112,512]{1,0:T(8,128)(2,1)S(1)} %convert_element_type.40), channel_id=1, source_target_pairs={{0,8},{1,13},{2,10},{3,15},{4,12},{5,9},{6,14},{7,11},{8,0},{9,5},... | collective-permute-start | bytes 344072 | tf_op jit(solution)/shard_map/ppermute | solution.py:562
  17.4 2.4 %collective-permute-start.5 = (f16[112,512]{1,0:T(8,128)(2,1)S(1)}, f16[112,512]{1,0:T(8,128)(2,1)S(1)}, u32[]{:S(2)}, u32[]{:S(2)}) collective-permute-start(f16[112,512]{1,0:T(8,128)(2,1)S(1)} %convert_element_type.38), channel_id=1, source_target_pairs={{0,20},{1,17},{2,22},{3,19},{4,16},{5,21},{6,18},{7,23},{8,28},{9,... | collective-permute-start | bytes 344072 | tf_op jit(solution)/shard_map/ppermute | solution.py:562
  19.7 0.6 %collective-permute-start.4 = (f16[112,512]{1,0:T(8,128)(2,1)S(1)}, f16[112,512]{1,0:T(8,128)(2,1)S(1)}, u32[]{:S(2)}, u32[]{:S(2)}) collective-permute-start(f16[112,512]{1,0:T(8,128)(2,1)S(1)} %convert_element_type.36), channel_id=1, source_target_pairs={{0,24},{1,29},{2,26},{3,31},{4,28},{5,25},{6,30},{7,27},{8,16},{9,... | collective-permute-start | bytes 344072 | tf_op jit(solution)/shard_map/ppermute | solution.py:562
  20.3 0.5 %shard_map.98 = f32[112,512]{1,0:T(8,128)S(1)} custom-call(s32[1,8]{1,0:T(1,128)S(1)} %copy-done.7, f32[112,2560]{1,0:T(8,128)S(1)} %gather.1.rows_in, f32[1,2048]{1,0:T(1,128)S(1)} %bitcast.7, f32[1,2048]{1,0:T(1,128)S(1)} %bitcast.12, s32[1,2048]{1,0:T(1,128)S(1)} %bitcast.17, bf16[4,512,512]{2,1,0:T(8,128)(2,1)S(1)} %get-tuple-element.18.w, ...), custom_call_target="tpu_custom_call" | custom-call | flops 58720256 | bytes 1146880 | tf_op jit(solution)/shard_map/pallas_call | solution.py:283
  20.8 0.7 %collective-permute-start.10 = (f16[112,512]{1,0:T(8,128)(2,1)S(1)}, f16[112,512]{1,0:T(8,128)(2,1)S(1)}, u32[]{:S(2)}, u32[]{:S(2)}) collective-permute-start(f16[112,512]{1,0:T(8,128)(2,1)S(1)} %convert_element_type.45), channel_id=1, source_target_pairs={{0,4},{1,1},{2,6},{3,3},{4,0},{5,5},{6,2},{7,7},{8,12},{9,9},{10,1... | collective-permute-start | bytes 344072 | tf_op jit(solution)/shard_map/ppermute | solution.py:562
  21.7 5.5 %collective-permute-done.5 = f16[112,512]{1,0:T(8,128)(2,1)S(1)} collective-permute-done((f16[112,512]{1,0:T(8,128)(2,1)S(1)}, f16[112,512]{1,0:T(8,128)(2,1)S(1)}, u32[]{:S(2)}, u32[]{:S(2)}) %collective-permute-start.5) | collective-permute-done | bytes 114720 | tf_op jit(solution)/shard_map/ppermute | solution.py:562
  27.2 0.5 %collective-permute-start.7 = (f16[112,512]{1,0:T(8,128)(2,1)S(1)}, f16[112,512]{1,0:T(8,128)(2,1)S(1)}, u32[]{:S(2)}, u32[]{:S(2)}) collective-permute-start(f16[112,512]{1,0:T(8,128)(2,1)S(1)} %collective-permute-done.4), channel_id=1, source_target_pairs={{0,1},{1,0},{2,3},{3,2},{4,5},{5,4},{6,7},{7,6},{8,9},{9,8},{10,11... | collective-permute-start | bytes 344072 | tf_op jit(solution)/shard_map/ppermute | solution.py:574
  27.9 0.6 %collective-permute-done.8 = f16[112,512]{1,0:T(8,128)(2,1)S(1)} collective-permute-done((f16[112,512]{1,0:T(8,128)(2,1)S(1)}, f16[112,512]{1,0:T(8,128)(2,1)S(1)}, u32[]{:S(2)}, u32[]{:S(2)}) %collective-permute-start.8) | collective-permute-done | bytes 114720 | tf_op jit(solution)/shard_map/ppermute | solution.py:574
  29.1 1.5 %stencil.1 = (f32[48,2048]{1,0:T(8,128)S(1)}, bf16[48,512]{1,0:T(8,128)(2,1)S(1)}, bf16[48,512]{1,0:T(8,128)(2,1)S(1)}, bf16[48,512]{1,0:T(8,128)(2,1)S(1)}, bf16[48,512]{1,0:T(8,128)(2,1)S(1)}) custom-call(f32[1,3]{1,0:T(1,128)S(1)} %bitcast.19, f32[112,2176]{1,0:T(8,128)S(1)} %get-tuple-element.21.acc_in, f32[32,128]{1,0:T(8,128)S(1)} %get-tuple-element.22.side, ...), custom_call_target="tpu_custom_call" | custom-call | flops 22937600 | bytes 1835008 | tf_op jit(solution)/shard_map/stencil/pallas_call | solution.py:445
  30.6 2.7 %collective-permute-start.14 = (bf16[48,512]{1,0:T(8,128)(2,1)S(1)}, bf16[48,512]{1,0:T(8,128)(2,1)S(1)}, u32[]{:S(2)}, u32[]{:S(2)}) collective-permute-start(bf16[48,512]{1,0:T(8,128)(2,1)S(1)} %get-tuple-element.25), channel_id=1, source_target_pairs={{24,0},{29,1},{26,2},{31,3},{28,4},{25,5},{30,6},{27,7},{16,8},{21... | collective-permute-start | bytes 147464 | tf_op jit(solution)/shard_map/ppermute | solution.py:587
  33.3 1.8 %collective-permute-start.15 = (bf16[48,512]{1,0:T(8,128)(2,1)S(1)}, bf16[48,512]{1,0:T(8,128)(2,1)S(1)}, u32[]{:S(2)}, u32[]{:S(2)}) collective-permute-start(bf16[48,512]{1,0:T(8,128)(2,1)S(1)} %get-tuple-element.26), channel_id=1, source_target_pairs={{20,0},{17,1},{22,2},{19,3},{16,4},{21,5},{18,6},{23,7},{28,8},{25... | collective-permute-start | bytes 147464 | tf_op jit(solution)/shard_map/ppermute | solution.py:587
  35.1 0.7 %collective-permute-start.12 = (bf16[48,512]{1,0:T(8,128)(2,1)S(1)}, bf16[48,512]{1,0:T(8,128)(2,1)S(1)}, u32[]{:S(2)}, u32[]{:S(2)}) collective-permute-start(bf16[48,512]{1,0:T(8,128)(2,1)S(1)} %get-tuple-element.24), channel_id=1, source_target_pairs={{4,0},{1,1},{6,2},{3,3},{0,4},{5,5},{2,6},{7,7},{12,8},{9,9},{14,1... | collective-permute-start | bytes 147464 | tf_op jit(solution)/shard_map/ppermute | solution.py:587
  35.8 0.5 %collective-permute-done.14.refs_0_ = bf16[48,512]{1,0:T(8,128)(2,1)S(1)} collective-permute-done((bf16[48,512]{1,0:T(8,128)(2,1)S(1)}, bf16[48,512]{1,0:T(8,128)(2,1)S(1)}, u32[]{:S(2)}, u32[]{:S(2)}) %collective-permute-start.14) | collective-permute-done | bytes 49184 | tf_op jit(solution)/shard_map/ppermute | solution.py:587
  36.3 2.5 %collective-permute-start.17 = (bf16[48,512]{1,0:T(8,128)(2,1)S(1)}, bf16[48,512]{1,0:T(8,128)(2,1)S(1)}, u32[]{:S(2)}, u32[]{:S(2)}) collective-permute-start(bf16[48,512]{1,0:T(8,128)(2,1)S(1)} %collective-permute-done.14.refs_0_), channel_id=1, source_target_pairs={{0,1},{1,0},{2,3},{3,2},{4,5},{5,4},{6,7},{7,6},{8,9},{9,8},{10,11... | collective-permute-start | bytes 147464 | tf_op jit(solution)/shard_map/ppermute | solution.py:589
  38.8 0.8 %collective-permute-done.15.refs_1_ = bf16[48,512]{1,0:T(8,128)(2,1)S(1)} collective-permute-done((bf16[48,512]{1,0:T(8,128)(2,1)S(1)}, bf16[48,512]{1,0:T(8,128)(2,1)S(1)}, u32[]{:S(2)}, u32[]{:S(2)}) %collective-permute-start.15) | collective-permute-done | bytes 49184 | tf_op jit(solution)/shard_map/ppermute | solution.py:587
  39.5 1.2 %collective-permute-start.18 = (bf16[48,512]{1,0:T(8,128)(2,1)S(1)}, bf16[48,512]{1,0:T(8,128)(2,1)S(1)}, u32[]{:S(2)}, u32[]{:S(2)}) collective-permute-start(bf16[48,512]{1,0:T(8,128)(2,1)S(1)} %collective-permute-done.15.refs_1_), channel_id=1, source_target_pairs={{0,1},{1,0},{2,3},{3,2},{4,5},{5,4},{6,7},{7,6},{8,9},{9,8},{10,11... | collective-permute-start | bytes 147464 | tf_op jit(solution)/shard_map/ppermute | solution.py:589
  40.7 1.6 %collective-permute-start.13 = (bf16[48,512]{1,0:T(8,128)(2,1)S(1)}, bf16[48,512]{1,0:T(8,128)(2,1)S(1)}, u32[]{:S(2)}, u32[]{:S(2)}) collective-permute-start(bf16[48,512]{1,0:T(8,128)(2,1)S(1)} %collective-permute-done.12.refs_0_), channel_id=1, source_target_pairs={{0,1},{1,0},{2,3},{3,2},{4,5},{5,4},{6,7},{7,6},{8,9},{9,8},{10,11... | collective-permute-start | bytes 147464 | tf_op jit(solution)/shard_map/ppermute | solution.py:589
  42.3 0.7 %emit.1 = f32[3,8,2048]{2,1,0:T(8,128)} custom-call(f32[48,2048]{1,0:T(8,128)S(1)} %get-tuple-element.23.both), custom_call_target="tpu_custom_call" | custom-call | bytes 393216 | tf_op jit(solution)/shard_map/emit/pallas_call | solution.py:471
  43.0 0.8 %back.1.refs_2_ = f32[24,2560]{1,0:T(8,128)S(1)} custom-call(s32[1,8]{1,0:T(1,128)S(1)} %copy-done.7, bf16[1,8,512,512]{3,2,1,0:T(8,128)(2,1)S(1)} %copy-done.1, bf16[48,512]{1,0:T(8,128)(2,1)S(1)} %collective-permute-done.14.refs_0_, bf16[48,512]{1,0:T(8,128)(2,1)S(1)} %collective-permute-done.15.refs_1_, ...), custom_call_target="tpu_custom_call" | custom-call | flops 75497472 | bytes 2097152 | tf_op jit(solution)/shard_map/back/pallas_call | solution.py:518
  43.8 1.1 %back_last.1 = f32[3,8,2048]{2,1,0:T(8,128)} custom-call(s32[1,8]{1,0:T(1,128)S(1)} %copy-done.7, bf16[1,8,512,512]{3,2,1,0:T(8,128)(2,1)S(1)} %copy-done.1, bf16[48,512]{1,0:T(8,128)(2,1)S(1)} %collective-permute-done.12.refs_0_, bf16[48,512]{1,0:T(8,128)(2,1)S(1)} %collective-permute-done.13.refs_1_, f32[24,2560]{1,0:T(8,128)S(1)} %back.1.refs_2_), custom_call_target="tpu_custom_call" | custom-call | flops 25165824 | bytes 2097152 | tf_op jit(solution)/shard_map/back_last/pallas_call | solution.py:518
  (50 shorter events, 1.1 us)
Async XLA Ops:
  0.6 12.2 %collective-permute-start = (bf16[3,8,2048]{2,1,0:T(8,128)(2,1)}, bf16[3,8,2048]{2,1,0:T(8,128)(2,1)S(1)}, u32[]{:S(2)}, u32[]{:S(2)}) collective-permute-start(bf16[3,8,2048]{2,1,0:T(8,128)(2,1)} %traj.1), channel_id=1, source_target_pairs={{0,1},{1,0},{2,3},{3,2},{4,5},{5,4},{6,7},{7,6},{8,9},{9,8},{10,11... | collective-permute-start | bytes 294920 | tf_op jit(solution)/shard_map/ppermute | solution.py:551
  0.7 12.1 %collective-permute-start.1 = (bf16[3,8,2048]{2,1,0:T(8,128)(2,1)}, bf16[3,8,2048]{2,1,0:T(8,128)(2,1)S(1)}, u32[]{:S(2)}, u32[]{:S(2)}) collective-permute-start(bf16[3,8,2048]{2,1,0:T(8,128)(2,1)} %inc.1), channel_id=1, source_target_pairs={{0,1},{1,0},{2,3},{3,2},{4,5},{5,4},{6,7},{7,6},{8,9},{9,8},{10,11... | collective-permute-start | bytes 294920 | tf_op jit(solution)/shard_map/ppermute | solution.py:552
  1.2 0.9 %copy-start.5 = (bf16[3,8,2048]{2,1,0:T(8,128)(2,1)S(1)}, bf16[3,8,2048]{2,1,0:T(8,128)(2,1)}, u32[]{:S(2)}) copy-start(bf16[3,8,2048]{2,1,0:T(8,128)(2,1)} %traj.1) | copy-start | bytes 294916
  2.1 0.9 %copy-start.6 = (bf16[3,8,2048]{2,1,0:T(8,128)(2,1)S(1)}, bf16[3,8,2048]{2,1,0:T(8,128)(2,1)}, u32[]{:S(2)}) copy-start(bf16[3,8,2048]{2,1,0:T(8,128)(2,1)} %inc.1) | copy-start | bytes 294916
  3.3 9.6 %copy-start.7 = (s32[1,8]{1,0:T(1,128)S(1)}, s32[1,8]{1,0:T(1,128)}, u32[]{:S(2)}) copy-start(s32[1,8]{1,0:T(1,128)} %counts.11) | copy-start | bytes 100
  3.4 8.7 %collective-permute-start.3 = (bf16[8,2304]{1,0:T(8,128)(2,1)S(1)}, bf16[8,2304]{1,0:T(8,128)(2,1)S(1)}, u32[]{:S(2)}, u32[]{:S(2)}) collective-permute-start(bf16[8,2304]{1,0:T(8,128)(2,1)S(1)} %get-tuple-element.17), channel_id=1, source_target_pairs={{1,3},{2,0},{5,7},{6,4},{9,11},{10,8},{13,15},{14,12},{17,19},{18,... | collective-permute-start | bytes 110600 | tf_op jit(solution)/shard_map/ppermute | solution.py:549
  7.5 5.3 %collective-permute-start.2 = (bf16[8,2304]{1,0:T(8,128)(2,1)S(1)}, bf16[8,2304]{1,0:T(8,128)(2,1)S(1)}, u32[]{:S(2)}, u32[]{:S(2)}) collective-permute-start(bf16[8,2304]{1,0:T(8,128)(2,1)S(1)} %get-tuple-element.17), channel_id=1, source_target_pairs={{1,2},{2,1},{5,6},{6,5},{9,10},{10,9},{13,14},{14,13},{17,18},{18,... | collective-permute-start | bytes 110600 | tf_op jit(solution)/shard_map/ppermute | solution.py:548
  9.5 2.2 %copy-start = (bf16[1,8,512,512]{3,2,1,0:T(8,128)(2,1)S(1)}, bf16[1,8,512,512]{3,2,1,0:T(8,128)(2,1)}, u32[]{:S(2)}) copy-start(bf16[1,8,512,512]{3,2,1,0:T(8,128)(2,1)} %weight.5) | copy-start | bytes 12582916
  11.7 1.3 %copy-start.2 = (f32[2048]{0:T(1024)S(1)}, f32[2048]{0:T(1024)}, u32[]{:S(2)}) copy-start(f32[2048]{0:T(1024)} %param.13) | copy-start | bytes 24580
  11.7 1.3 %copy-start.3 = (f32[2048]{0:T(1024)S(1)}, f32[2048]{0:T(1024)}, u32[]{:S(2)}) copy-start(f32[2048]{0:T(1024)} %param.14) | copy-start | bytes 24580
  11.7 1.3 %copy-start.4 = (s32[2048]{0:T(1024)S(1)}, s32[2048]{0:T(1024)}, u32[]{:S(2)}) copy-start(s32[2048]{0:T(1024)} %param.15) | copy-start | bytes 24580
  15.4 6.1 %collective-permute-start.6 = (f16[112,512]{1,0:T(8,128)(2,1)S(1)}, f16[112,512]{1,0:T(8,128)(2,1)S(1)}, u32[]{:S(2)}, u32[]{:S(2)}) collective-permute-start(f16[112,512]{1,0:T(8,128)(2,1)S(1)} %convert_element_type.40), channel_id=1, source_target_pairs={{0,8},{1,13},{2,10},{3,15},{4,12},{5,9},{6,14},{7,11},{8,0},{9,5},... | collective-permute-start | bytes 344072 | tf_op jit(solution)/shard_map/ppermute | solution.py:562
  17.4 9.9 %collective-permute-start.5 = (f16[112,512]{1,0:T(8,128)(2,1)S(1)}, f16[112,512]{1,0:T(8,128)(2,1)S(1)}, u32[]{:S(2)}, u32[]{:S(2)}) collective-permute-start(f16[112,512]{1,0:T(8,128)(2,1)S(1)} %convert_element_type.38), channel_id=1, source_target_pairs={{0,20},{1,17},{2,22},{3,19},{4,16},{5,21},{6,18},{7,23},{8,28},{9,... | collective-permute-start | bytes 344072 | tf_op jit(solution)/shard_map/ppermute | solution.py:562
  19.7 7.5 %collective-permute-start.4 = (f16[112,512]{1,0:T(8,128)(2,1)S(1)}, f16[112,512]{1,0:T(8,128)(2,1)S(1)}, u32[]{:S(2)}, u32[]{:S(2)}) collective-permute-start(f16[112,512]{1,0:T(8,128)(2,1)S(1)} %convert_element_type.36), channel_id=1, source_target_pairs={{0,24},{1,29},{2,26},{3,31},{4,28},{5,25},{6,30},{7,27},{8,16},{9,... | collective-permute-start | bytes 344072 | tf_op jit(solution)/shard_map/ppermute | solution.py:562
  20.8 8.3 %copy-start.8 = (f32[3]{0:T(128)S(1)}, f32[3]{0:T(128)}, u32[]{:S(2)}) copy-start(f32[3]{0:T(128)} %param.12) | copy-start | bytes 40
  20.8 6.9 %collective-permute-start.10 = (f16[112,512]{1,0:T(8,128)(2,1)S(1)}, f16[112,512]{1,0:T(8,128)(2,1)S(1)}, u32[]{:S(2)}, u32[]{:S(2)}) collective-permute-start(f16[112,512]{1,0:T(8,128)(2,1)S(1)} %convert_element_type.45), channel_id=1, source_target_pairs={{0,4},{1,1},{2,6},{3,3},{4,0},{5,5},{6,2},{7,7},{8,12},{9,9},{10,1... | collective-permute-start | bytes 344072 | tf_op jit(solution)/shard_map/ppermute | solution.py:562
  21.5 6.4 %collective-permute-start.9 = (f16[112,512]{1,0:T(8,128)(2,1)S(1)}, f16[112,512]{1,0:T(8,128)(2,1)S(1)}, u32[]{:S(2)}, u32[]{:S(2)}) collective-permute-start(f16[112,512]{1,0:T(8,128)(2,1)S(1)} %collective-permute-done.6), channel_id=1, source_target_pairs={{0,1},{1,0},{2,3},{3,2},{4,5},{5,4},{6,7},{7,6},{8,9},{9,8},{10,11... | collective-permute-start | bytes 344072 | tf_op jit(solution)/shard_map/ppermute | solution.py:574
  27.2 1.3 %collective-permute-start.8 = (f16[112,512]{1,0:T(8,128)(2,1)S(1)}, f16[112,512]{1,0:T(8,128)(2,1)S(1)}, u32[]{:S(2)}, u32[]{:S(2)}) collective-permute-start(f16[112,512]{1,0:T(8,128)(2,1)S(1)} %collective-permute-done.5), channel_id=1, source_target_pairs={{0,1},{1,0},{2,3},{3,2},{4,5},{5,4},{6,7},{7,6},{8,9},{9,8},{10,11... | collective-permute-start | bytes 344072 | tf_op jit(solution)/shard_map/ppermute | solution.py:574
  27.2 1.5 %collective-permute-start.7 = (f16[112,512]{1,0:T(8,128)(2,1)S(1)}, f16[112,512]{1,0:T(8,128)(2,1)S(1)}, u32[]{:S(2)}, u32[]{:S(2)}) collective-permute-start(f16[112,512]{1,0:T(8,128)(2,1)S(1)} %collective-permute-done.4), channel_id=1, source_target_pairs={{0,1},{1,0},{2,3},{3,2},{4,5},{5,4},{6,7},{7,6},{8,9},{9,8},{10,11... | collective-permute-start | bytes 344072 | tf_op jit(solution)/shard_map/ppermute | solution.py:574
  27.7 1.3 %collective-permute-start.11 = (f16[112,512]{1,0:T(8,128)(2,1)S(1)}, f16[112,512]{1,0:T(8,128)(2,1)S(1)}, u32[]{:S(2)}, u32[]{:S(2)}) collective-permute-start(f16[112,512]{1,0:T(8,128)(2,1)S(1)} %collective-permute-done.10), channel_id=1, source_target_pairs={{0,1},{1,0},{2,3},{3,2},{4,5},{5,4},{6,7},{7,6},{8,9},{9,8},{10,11... | collective-permute-start | bytes 344072 | tf_op jit(solution)/shard_map/ppermute | solution.py:574
  28.5 14.5 %copy-start.1 = (bf16[1,8,512,512]{3,2,1,0:T(8,128)(2,1)S(1)}, bf16[1,8,512,512]{3,2,1,0:T(8,128)(2,1)}, u32[]{:S(2)}) copy-start(bf16[1,8,512,512]{3,2,1,0:T(8,128)(2,1)} %weight.5) | copy-start | bytes 12582916
  30.6 5.7 %collective-permute-start.14 = (bf16[48,512]{1,0:T(8,128)(2,1)S(1)}, bf16[48,512]{1,0:T(8,128)(2,1)S(1)}, u32[]{:S(2)}, u32[]{:S(2)}) collective-permute-start(bf16[48,512]{1,0:T(8,128)(2,1)S(1)} %get-tuple-element.25), channel_id=1, source_target_pairs={{24,0},{29,1},{26,2},{31,3},{28,4},{25,5},{30,6},{27,7},{16,8},{21... | collective-permute-start | bytes 147464 | tf_op jit(solution)/shard_map/ppermute | solution.py:587
  33.3 6.2 %collective-permute-start.15 = (bf16[48,512]{1,0:T(8,128)(2,1)S(1)}, bf16[48,512]{1,0:T(8,128)(2,1)S(1)}, u32[]{:S(2)}, u32[]{:S(2)}) collective-permute-start(bf16[48,512]{1,0:T(8,128)(2,1)S(1)} %get-tuple-element.26), channel_id=1, source_target_pairs={{20,0},{17,1},{22,2},{19,3},{16,4},{21,5},{18,6},{23,7},{28,8},{25... | collective-permute-start | bytes 147464 | tf_op jit(solution)/shard_map/ppermute | solution.py:587
  35.1 5.6 %collective-permute-start.16 = (bf16[48,512]{1,0:T(8,128)(2,1)S(1)}, bf16[48,512]{1,0:T(8,128)(2,1)S(1)}, u32[]{:S(2)}, u32[]{:S(2)}) collective-permute-start(bf16[48,512]{1,0:T(8,128)(2,1)S(1)} %get-tuple-element.27), channel_id=1, source_target_pairs={{8,0},{13,1},{10,2},{15,3},{12,4},{9,5},{14,6},{11,7},{0,8},{5,9},... | collective-permute-start | bytes 147464 | tf_op jit(solution)/shard_map/ppermute | solution.py:587
  35.1 5.6 %collective-permute-start.12 = (bf16[48,512]{1,0:T(8,128)(2,1)S(1)}, bf16[48,512]{1,0:T(8,128)(2,1)S(1)}, u32[]{:S(2)}, u32[]{:S(2)}) collective-permute-start(bf16[48,512]{1,0:T(8,128)(2,1)S(1)} %get-tuple-element.24), channel_id=1, source_target_pairs={{4,0},{1,1},{6,2},{3,3},{0,4},{5,5},{2,6},{7,7},{12,8},{9,9},{14,1... | collective-permute-start | bytes 147464 | tf_op jit(solution)/shard_map/ppermute | solution.py:587
  36.3 6.7 %collective-permute-start.17 = (bf16[48,512]{1,0:T(8,128)(2,1)S(1)}, bf16[48,512]{1,0:T(8,128)(2,1)S(1)}, u32[]{:S(2)}, u32[]{:S(2)}) collective-permute-start(bf16[48,512]{1,0:T(8,128)(2,1)S(1)} %collective-permute-done.14.refs_0_), channel_id=1, source_target_pairs={{0,1},{1,0},{2,3},{3,2},{4,5},{5,4},{6,7},{7,6},{8,9},{9,8},{10,11... | collective-permute-start | bytes 147464 | tf_op jit(solution)/shard_map/ppermute | solution.py:589
  39.5 3.5 %collective-permute-start.18 = (bf16[48,512]{1,0:T(8,128)(2,1)S(1)}, bf16[48,512]{1,0:T(8,128)(2,1)S(1)}, u32[]{:S(2)}, u32[]{:S(2)}) collective-permute-start(bf16[48,512]{1,0:T(8,128)(2,1)S(1)} %collective-permute-done.15.refs_1_), channel_id=1, source_target_pairs={{0,1},{1,0},{2,3},{3,2},{4,5},{5,4},{6,7},{7,6},{8,9},{9,8},{10,11... | collective-permute-start | bytes 147464 | tf_op jit(solution)/shard_map/ppermute | solution.py:589
  40.7 2.3 %collective-permute-start.19 = (bf16[48,512]{1,0:T(8,128)(2,1)S(1)}, bf16[48,512]{1,0:T(8,128)(2,1)S(1)}, u32[]{:S(2)}, u32[]{:S(2)}) collective-permute-start(bf16[48,512]{1,0:T(8,128)(2,1)S(1)} %collective-permute-done.16.refs_2_), channel_id=1, source_target_pairs={{0,1},{1,0},{2,3},{3,2},{4,5},{5,4},{6,7},{7,6},{8,9},{9,8},{10,11... | collective-permute-start | bytes 147464 | tf_op jit(solution)/shard_map/ppermute | solution.py:589
  40.7 3.1 %collective-permute-start.13 = (bf16[48,512]{1,0:T(8,128)(2,1)S(1)}, bf16[48,512]{1,0:T(8,128)(2,1)S(1)}, u32[]{:S(2)}, u32[]{:S(2)}) collective-permute-start(bf16[48,512]{1,0:T(8,128)(2,1)S(1)} %collective-permute-done.12.refs_0_), channel_id=1, source_target_pairs={{0,1},{1,0},{2,3},{3,2},{4,5},{5,4},{6,7},{7,6},{8,9},{9,8},{10,11... | collective-permute-start | bytes 147464 | tf_op jit(solution)/shard_map/ppermute | solution.py:589

commit v3 on v2

--- a/solution.py
+++ b/solution.py
@@ -47,6 +47,16 @@
 
 def columns(x):
     return [x[:, at : at + LANE] for at in range(0, x.shape[1], LANE)]
+
+
+def shifted(x, lane, shift, size):
+    turned = [
+        pltpu.roll(jnp.where(lane < size - at * LANE, part, 0.0), shift, axis=1)
+        for at, part in enumerate(columns(x))
+    ]
+    blank = jnp.zeros_like(turned[0])
+    parts = [jnp.where(lane < shift, low, high) for low, high in zip([blank] + turned, turned + [blank])]
+    return jnp.concatenate(parts, axis=1)
 
 
 class Plan:
@@ -264,16 +274,21 @@
             out[tail + row + 1 : tail + row + 2, span] = scale * (value - top)
         out[tail + 4 : tail + 5, span] = scale * offset[:, at : at + LANE].astype(jnp.float32)
 
+    def edge(weights, group):
+        base, shift, size = place(counts, group)
+        lane = lax.broadcasted_iota(jnp.int32, (SUB, LANE), 1)
+        weights = shifted(weights.astype(jnp.float32), lane, shift, size).astype(jnp.bfloat16)
+        x = rows_in[:, pl.ds(base, slots + LANE)].astype(jnp.bfloat16)
+        return scale * lax.dot_general(weights, x, contract, preferred_element_type=jnp.float32)
+
     @pl.when((group == 0) | (group == reach - 1))
     def _():
-        z = slotted(lax.rem(group + reach - 1, reach))
-        e = scale * lax.dot_general(w_low[which], z, contract, preferred_element_type=jnp.float32)
+        e = edge(w_low[which], lax.rem(group + reach - 1, reach))
         out[tail : tail + 2 * HALO, :rows] = e[SUB - 2 * HALO :]
 
     @pl.when((group == reach - 2) | (group == reach - 1))
     def _():
-        z = slotted(lax.rem(group + 1, reach))
-        e = scale * lax.dot_general(w_high[which], z, contract, preferred_element_type=jnp.float32)
+        e = edge(w_high[which], lax.rem(group + 1, reach))
         out[tail : tail + 2 * HALO, LANE : LANE + rows] = e[: 2 * HALO]
 
 
@@ -488,21 +503,13 @@
     main = acc.shape[0]
     acc[...] = start[...] if last else jnp.zeros_like(acc)
     lane = lax.broadcasted_iota(jnp.int32, (main, LANE), 1)
-    blank = jnp.zeros((main, LANE), jnp.float32)
     for k, piece in zip(numbers, pieces):
         group = plan.returned(k)
         both = piece[...].astype(jnp.float32)
         own = jnp.where(plan.core() == 0, both[:main], both[main:]).astype(jnp.bfloat16)
         grad = jnp.dot(own, weight[0, group], preferred_element_type=jnp.float32)
         base, shift, size = place(counts, group)
-        turned = [
-            pltpu.roll(jnp.where(lane < size - at * LANE, x, 0.0), shift, axis=1)
-            for at, x in enumerate(columns(grad))
-        ]
-        placed = [
-            jnp.where(lane < shift, before, x) for before, x in zip([blank] + turned, turned + [blank])
-        ]
-        acc[:, pl.ds(base, slots + LANE)] += jnp.concatenate(placed, axis=1)
+        acc[:, pl.ds(base, slots + LANE)] += shifted(grad, lane, shift, size)
     if last:
         tracers, levels, cols = out.shape
         for m in range(tracers):
@@ -544,14 +551,14 @@
     near = [(v, v + 1 if v % 2 else v - 1) for v in range(slabs)]
     far = [(v, v + 2 if v % 2 else v - 2) for v in range(slabs)]
     near, far = ([(a, b) for a, b in way if 0 <= b < slabs] for way in (near, far))
-    traj_own, inc_own, border = fetch_border(plan, trajectory, increment)
+    traj_own, inc_own, border = fetch_border(plan, *(pltpu.with_memory_space_constraint(x, pltpu.HBM) for x in (trajectory, increment)))
     ext = lax.ppermute(border, "lev", near)
     ext_too = lax.ppermute(border, "lev", far)
 
     traj_too = lax.ppermute(trajectory, "lev", swap)
     inc_too = lax.ppermute(increment, "lev", swap)
 
-    w, w_low, w_high = load(plan, remap_weight)
+    w, w_low, w_high = load(plan, pltpu.with_memory_space_constraint(remap_weight, pltpu.HBM))
     lines = [x.reshape(1, cols) for x in (courant, vertical, offset)]
     rows_in = gather(plan, traj_own, inc_own, traj_too, inc_too, ext, ext_too, rows, cols + slots)
     pieces, message_0 = [], None

time: 45.2 us -> 44.2 us (0.978)
  local copies, waits for them, and re-layouts: 3.99 us -> 0.04 us
  Pallas kernels: 7.94 us -> 9.95 us
  waiting for transfers between devices: 8.46 us -> 9.45 us
    unnamed x18 -> x12, local copies, waits for them, and re-layouts: 3.99 us -> 0.04 us
    pallas_call x1, Pallas kernels: 0.39 us -> 1.74 us  [load(): pl.pallas_call(functools.partial(load_kernel, plan), in_specs=[HBM], out_...]
    ppermute x1, waiting for transfers between devices: 0.74 us -> 1.6 us  [step(): ext = lax.ppermute(border, 'lev', near)]
    pallas_call x1, Pallas kernels: 0.34 us -> 1.06 us  [fetch_border(): pl.pallas_call(functools.partial(border_kernel, plan), in_specs=[HBM] * 2...]
  transfers between devices with their start and end apart: 20 -> 20, of which waited for: 7 -> 8; matrix products, arithmetic and copies ran while one was open for 0% -> 0% of each run, Pallas kernels for 6% -> 11%
where the time goes in v3:
time: 44.2 us; the launch traced here: 43.9 us
  starting transfers between devices  23.4 us (53%)
  Pallas kernels  9.95 us (23%)
  waiting for transfers between devices  9.45 us (21%)
  between operations  0.93 us (2%)
    ppermute x4, waiting for transfers between devices, step(): pieces.append(lax.ppermute(message, both, route))  5.79 us
    ppermute x4, starting transfers between devices, step(): regained.append(lax.ppermute(window, 'lev', swap))  5.36 us
    ppermute x4, starting transfers between devices, step(): pieces.append(lax.ppermute(message, both, route))  5.27 us
    ppermute x4, starting transfers between devices, step(): returned.append(lax.ppermute(window, both, [(b, a) for a, b in route]))  5.17 us
    ppermute x1, starting transfers between devices, step(): ext_too = lax.ppermute(border, 'lev', far)  4.31 us
    pallas_call x4, Pallas kernels, forward(): pl.pallas_call(functools.partial(forward_kernel, plan, which, scale, tail...  2.84 us
    ppermute x1, starting transfers between devices, step(): ext = lax.ppermute(border, 'lev', near)  1.92 us
    pallas_call x2, Pallas kernels, backward(): pl.pallas_call(functools.partial(backward_kernel, plan, int(last), number...  1.84 us
  transfers between devices with their start and end apart: 20, of which 8 were waited for; matrix products, arithmetic and copies ran while one was open for 0% of the time, Pallas kernels for 11%

profile of v3, /device:TPU:1, one launch (start us, length us, event | category | flops | bytes accessed | tf_op | source)
XLA Modules:
  0.0 43.9 jit_solution(18329749558932289852)
XLA Ops:
  0.7 0.5 %collective-permute-start.1 = (bf16[3,8,2048]{2,1,0:T(8,128)(2,1)}, bf16[3,8,2048]{2,1,0:T(8,128)(2,1)S(1)}, u32[]{:S(2)}, u32[]{:S(2)}) collective-permute-start(bf16[3,8,2048]{2,1,0:T(8,128)(2,1)} %inc.1), channel_id=1, source_target_pairs={{0,1},{1,0},{2,3},{3,2},{4,5},{5,4},{6,7},{7,6},{8,9},{9,8},{10,11... | collective-permute-start | bytes 294920 | tf_op jit(solution)/shard_map/ppermute | solution.py:559
  1.2 1.1 %border.1 = (bf16[3,8,2048]{2,1,0:T(8,128)(2,1)S(1)}, bf16[3,8,2048]{2,1,0:T(8,128)(2,1)S(1)}, bf16[8,2304]{1,0:T(8,128)(2,1)S(1)}) custom-call(bf16[3,8,2048]{2,1,0:T(8,128)(2,1)} %traj.1, bf16[3,8,2048]{2,1,0:T(8,128)(2,1)} %inc.1), custom_call_target="tpu_custom_call" | custom-call | bytes 393216 | tf_op jit(solution)/shard_map/border/pallas_call | solution.py:162
  2.3 4.3 %collective-permute-start.3 = (bf16[8,2304]{1,0:T(8,128)(2,1)S(1)}, bf16[8,2304]{1,0:T(8,128)(2,1)S(1)}, u32[]{:S(2)}, u32[]{:S(2)}) collective-permute-start(bf16[8,2304]{1,0:T(8,128)(2,1)S(1)} %get-tuple-element.17), channel_id=1, source_target_pairs={{1,3},{2,0},{5,7},{6,4},{9,11},{10,8},{13,15},{14,12},{17,19},{18,... | collective-permute-start | bytes 110600 | tf_op jit(solution)/shard_map/ppermute | solution.py:556
  6.6 1.9 %collective-permute-start.2 = (bf16[8,2304]{1,0:T(8,128)(2,1)S(1)}, bf16[8,2304]{1,0:T(8,128)(2,1)S(1)}, u32[]{:S(2)}, u32[]{:S(2)}) collective-permute-start(bf16[8,2304]{1,0:T(8,128)(2,1)S(1)} %get-tuple-element.17), channel_id=1, source_target_pairs={{1,2},{2,1},{5,6},{6,5},{9,10},{10,9},{13,14},{14,13},{17,18},{18,... | collective-permute-start | bytes 110600 | tf_op jit(solution)/shard_map/ppermute | solution.py:555
  8.6 1.7 %fetch.1 = (bf16[4,512,512]{2,1,0:T(8,128)(2,1)S(1)}, bf16[4,8,512]{2,1,0:T(8,128)(2,1)S(1)}, bf16[4,8,512]{2,1,0:T(8,128)(2,1)S(1)}) custom-call(bf16[1,8,512,512]{3,2,1,0:T(8,128)(2,1)} %weight.5), custom_call_target="tpu_custom_call" | custom-call | bytes 4194304 | tf_op jit(solution)/shard_map/fetch/pallas_call | solution.py:204
  10.3 1.6 %collective-permute-done.2.ext = bf16[8,2304]{1,0:T(8,128)(2,1)S(1)} collective-permute-done((bf16[8,2304]{1,0:T(8,128)(2,1)S(1)}, bf16[8,2304]{1,0:T(8,128)(2,1)S(1)}, u32[]{:S(2)}, u32[]{:S(2)}) %collective-permute-start.2) | collective-permute-done | bytes 36896 | tf_op jit(solution)/shard_map/ppermute | solution.py:555
  12.0 1.1 %shard_map.97 = f32[112,512]{1,0:T(8,128)S(1)} custom-call(s32[1,8]{1,0:T(1,128)S(1)} %copy-done.4, f32[112,2560]{1,0:T(8,128)S(1)} %gather.1.rows_in, f32[1,2048]{1,0:T(1,128)S(1)} %bitcast.4, f32[1,2048]{1,0:T(1,128)S(1)} %bitcast.9, s32[1,2048]{1,0:T(1,128)S(1)} %bitcast.14, bf16[4,512,512]{2,1,0:T(8,128)(2,1)S(1)} %get-tuple-element.18.w, ...), custom_call_target="tpu_custom_call" | custom-call | flops 58720256 | bytes 1146880 | tf_op jit(solution)/shard_map/pallas_call | solution.py:298
  13.1 0.8 %shard_map.96 = f32[112,512]{1,0:T(8,128)S(1)} custom-call(s32[1,8]{1,0:T(1,128)S(1)} %copy-done.4, f32[112,2560]{1,0:T(8,128)S(1)} %gather.1.rows_in, f32[1,2048]{1,0:T(1,128)S(1)} %bitcast.5, f32[1,2048]{1,0:T(1,128)S(1)} %bitcast.10, s32[1,2048]{1,0:T(1,128)S(1)} %bitcast.15, bf16[4,512,512]{2,1,0:T(8,128)(2,1)S(1)} %get-tuple-element.18.w, ...), custom_call_target="tpu_custom_call" | custom-call | flops 58720256 | bytes 1146880 | tf_op jit(solution)/shard_map/pallas_call | solution.py:298
  13.9 0.5 %shard_map.95 = f32[112,512]{1,0:T(8,128)S(1)} custom-call(s32[1,8]{1,0:T(1,128)S(1)} %copy-done.4, f32[112,2560]{1,0:T(8,128)S(1)} %gather.1.rows_in, f32[1,2048]{1,0:T(1,128)S(1)} %bitcast.6, f32[1,2048]{1,0:T(1,128)S(1)} %bitcast.11, s32[1,2048]{1,0:T(1,128)S(1)} %bitcast.16, bf16[4,512,512]{2,1,0:T(8,128)(2,1)S(1)} %get-tuple-element.18.w, ...), custom_call_target="tpu_custom_call" | custom-call | flops 58720256 | bytes 1146880 | tf_op jit(solution)/shard_map/pallas_call | solution.py:298
  14.5 1.6 %collective-permute-start.6 = (f16[112,512]{1,0:T(8,128)(2,1)S(1)}, f16[112,512]{1,0:T(8,128)(2,1)S(1)}, u32[]{:S(2)}, u32[]{:S(2)}) collective-permute-start(f16[112,512]{1,0:T(8,128)(2,1)S(1)} %convert_element_type.40), channel_id=1, source_target_pairs={{0,8},{1,13},{2,10},{3,15},{4,12},{5,9},{6,14},{7,11},{8,0},{9,5},... | collective-permute-start | bytes 344072 | tf_op jit(solution)/shard_map/ppermute | solution.py:569
  16.2 2.4 %collective-permute-start.5 = (f16[112,512]{1,0:T(8,128)(2,1)S(1)}, f16[112,512]{1,0:T(8,128)(2,1)S(1)}, u32[]{:S(2)}, u32[]{:S(2)}) collective-permute-start(f16[112,512]{1,0:T(8,128)(2,1)S(1)} %convert_element_type.38), channel_id=1, source_target_pairs={{0,20},{1,17},{2,22},{3,19},{4,16},{5,21},{6,18},{7,23},{8,28},{9,... | collective-permute-start | bytes 344072 | tf_op jit(solution)/shard_map/ppermute | solution.py:569
  18.5 0.6 %collective-permute-start.4 = (f16[112,512]{1,0:T(8,128)(2,1)S(1)}, f16[112,512]{1,0:T(8,128)(2,1)S(1)}, u32[]{:S(2)}, u32[]{:S(2)}) collective-permute-start(f16[112,512]{1,0:T(8,128)(2,1)S(1)} %convert_element_type.36), channel_id=1, source_target_pairs={{0,24},{1,29},{2,26},{3,31},{4,28},{5,25},{6,30},{7,27},{8,16},{9,... | collective-permute-start | bytes 344072 | tf_op jit(solution)/shard_map/ppermute | solution.py:569
  19.1 0.5 %shard_map.98 = f32[112,512]{1,0:T(8,128)S(1)} custom-call(s32[1,8]{1,0:T(1,128)S(1)} %copy-done.4, f32[112,2560]{1,0:T(8,128)S(1)} %gather.1.rows_in, f32[1,2048]{1,0:T(1,128)S(1)} %bitcast.7, f32[1,2048]{1,0:T(1,128)S(1)} %bitcast.12, s32[1,2048]{1,0:T(1,128)S(1)} %bitcast.17, bf16[4,512,512]{2,1,0:T(8,128)(2,1)S(1)} %get-tuple-element.18.w, ...), custom_call_target="tpu_custom_call" | custom-call | flops 58720256 | bytes 1146880 | tf_op jit(solution)/shard_map/pallas_call | solution.py:298
  19.6 0.7 %collective-permute-start.10 = (f16[112,512]{1,0:T(8,128)(2,1)S(1)}, f16[112,512]{1,0:T(8,128)(2,1)S(1)}, u32[]{:S(2)}, u32[]{:S(2)}) collective-permute-start(f16[112,512]{1,0:T(8,128)(2,1)S(1)} %convert_element_type.45), channel_id=1, source_target_pairs={{0,4},{1,1},{2,6},{3,3},{4,0},{5,5},{6,2},{7,7},{8,12},{9,9},{10,1... | collective-permute-start | bytes 344072 | tf_op jit(solution)/shard_map/ppermute | solution.py:569
  20.3 0.2 collective-permute-done.6
  20.5 0.2 collective-permute-start.9
  20.7 5.5 %collective-permute-done.5 = f16[112,512]{1,0:T(8,128)(2,1)S(1)} collective-permute-done((f16[112,512]{1,0:T(8,128)(2,1)S(1)}, f16[112,512]{1,0:T(8,128)(2,1)S(1)}, u32[]{:S(2)}, u32[]{:S(2)}) %collective-permute-start.5) | collective-permute-done | bytes 114720 | tf_op jit(solution)/shard_map/ppermute | solution.py:569
  26.3 0.5 %collective-permute-start.7 = (f16[112,512]{1,0:T(8,128)(2,1)S(1)}, f16[112,512]{1,0:T(8,128)(2,1)S(1)}, u32[]{:S(2)}, u32[]{:S(2)}) collective-permute-start(f16[112,512]{1,0:T(8,128)(2,1)S(1)} %collective-permute-done.4), channel_id=1, source_target_pairs={{0,1},{1,0},{2,3},{3,2},{4,5},{5,4},{6,7},{7,6},{8,9},{9,8},{10,11... | collective-permute-start | bytes 344072 | tf_op jit(solution)/shard_map/ppermute | solution.py:581
  27.0 0.6 %collective-permute-done.8 = f16[112,512]{1,0:T(8,128)(2,1)S(1)} collective-permute-done((f16[112,512]{1,0:T(8,128)(2,1)S(1)}, f16[112,512]{1,0:T(8,128)(2,1)S(1)}, u32[]{:S(2)}, u32[]{:S(2)}) %collective-permute-start.8) | collective-permute-done | bytes 114720 | tf_op jit(solution)/shard_map/ppermute | solution.py:581
  27.8 0.2 assemble.1
  28.1 1.5 %stencil.1 = (f32[48,2048]{1,0:T(8,128)S(1)}, bf16[48,512]{1,0:T(8,128)(2,1)S(1)}, bf16[48,512]{1,0:T(8,128)(2,1)S(1)}, bf16[48,512]{1,0:T(8,128)(2,1)S(1)}, bf16[48,512]{1,0:T(8,128)(2,1)S(1)}) custom-call(f32[1,3]{1,0:T(1,128)S(1)} %bitcast.19, f32[112,2176]{1,0:T(8,128)S(1)} %get-tuple-element.21.acc_in, f32[32,128]{1,0:T(8,128)S(1)} %get-tuple-element.22.side, ...), custom_call_target="tpu_custom_call" | custom-call | flops 22937600 | bytes 1835008 | tf_op jit(solution)/shard_map/stencil/pallas_call | solution.py:460
  29.6 2.9 %collective-permute-start.14 = (bf16[48,512]{1,0:T(8,128)(2,1)S(1)}, bf16[48,512]{1,0:T(8,128)(2,1)S(1)}, u32[]{:S(2)}, u32[]{:S(2)}) collective-permute-start(bf16[48,512]{1,0:T(8,128)(2,1)S(1)} %get-tuple-element.25), channel_id=1, source_target_pairs={{24,0},{29,1},{26,2},{31,3},{28,4},{25,5},{30,6},{27,7},{16,8},{21... | collective-permute-start | bytes 147464 | tf_op jit(solution)/shard_map/ppermute | solution.py:594
  32.6 1.6 %collective-permute-start.15 = (bf16[48,512]{1,0:T(8,128)(2,1)S(1)}, bf16[48,512]{1,0:T(8,128)(2,1)S(1)}, u32[]{:S(2)}, u32[]{:S(2)}) collective-permute-start(bf16[48,512]{1,0:T(8,128)(2,1)S(1)} %get-tuple-element.26), channel_id=1, source_target_pairs={{20,0},{17,1},{22,2},{19,3},{16,4},{21,5},{18,6},{23,7},{28,8},{25... | collective-permute-start | bytes 147464 | tf_op jit(solution)/shard_map/ppermute | solution.py:594
  34.1 0.7 %collective-permute-start.12 = (bf16[48,512]{1,0:T(8,128)(2,1)S(1)}, bf16[48,512]{1,0:T(8,128)(2,1)S(1)}, u32[]{:S(2)}, u32[]{:S(2)}) collective-permute-start(bf16[48,512]{1,0:T(8,128)(2,1)S(1)} %get-tuple-element.24), channel_id=1, source_target_pairs={{4,0},{1,1},{6,2},{3,3},{0,4},{5,5},{2,6},{7,7},{12,8},{9,9},{14,1... | collective-permute-start | bytes 147464 | tf_op jit(solution)/shard_map/ppermute | solution.py:594
  34.8 0.5 %collective-permute-done.14.refs_0_ = bf16[48,512]{1,0:T(8,128)(2,1)S(1)} collective-permute-done((bf16[48,512]{1,0:T(8,128)(2,1)S(1)}, bf16[48,512]{1,0:T(8,128)(2,1)S(1)}, u32[]{:S(2)}, u32[]{:S(2)}) %collective-permute-start.14) | collective-permute-done | bytes 49184 | tf_op jit(solution)/shard_map/ppermute | solution.py:594
  35.3 2.5 %collective-permute-start.17 = (bf16[48,512]{1,0:T(8,128)(2,1)S(1)}, bf16[48,512]{1,0:T(8,128)(2,1)S(1)}, u32[]{:S(2)}, u32[]{:S(2)}) collective-permute-start(bf16[48,512]{1,0:T(8,128)(2,1)S(1)} %collective-permute-done.14.refs_0_), channel_id=1, source_target_pairs={{0,1},{1,0},{2,3},{3,2},{4,5},{5,4},{6,7},{7,6},{8,9},{9,8},{10,11... | collective-permute-start | bytes 147464 | tf_op jit(solution)/shard_map/ppermute | solution.py:596
  37.8 0.7 %collective-permute-done.15.refs_1_ = bf16[48,512]{1,0:T(8,128)(2,1)S(1)} collective-permute-done((bf16[48,512]{1,0:T(8,128)(2,1)S(1)}, bf16[48,512]{1,0:T(8,128)(2,1)S(1)}, u32[]{:S(2)}, u32[]{:S(2)}) %collective-permute-start.15) | collective-permute-done | bytes 49184 | tf_op jit(solution)/shard_map/ppermute | solution.py:594
  38.5 1.3 %collective-permute-start.18 = (bf16[48,512]{1,0:T(8,128)(2,1)S(1)}, bf16[48,512]{1,0:T(8,128)(2,1)S(1)}, u32[]{:S(2)}, u32[]{:S(2)}) collective-permute-start(bf16[48,512]{1,0:T(8,128)(2,1)S(1)} %collective-permute-done.15.refs_1_), channel_id=1, source_target_pairs={{0,1},{1,0},{2,3},{3,2},{4,5},{5,4},{6,7},{7,6},{8,9},{9,8},{10,11... | collective-permute-start | bytes 147464 | tf_op jit(solution)/shard_map/ppermute | solution.py:596
  39.8 1.6 %collective-permute-start.13 = (bf16[48,512]{1,0:T(8,128)(2,1)S(1)}, bf16[48,512]{1,0:T(8,128)(2,1)S(1)}, u32[]{:S(2)}, u32[]{:S(2)}) collective-permute-start(bf16[48,512]{1,0:T(8,128)(2,1)S(1)} %collective-permute-done.12.refs_0_), channel_id=1, source_target_pairs={{0,1},{1,0},{2,3},{3,2},{4,5},{5,4},{6,7},{7,6},{8,9},{9,8},{10,11... | collective-permute-start | bytes 147464 | tf_op jit(solution)/shard_map/ppermute | solution.py:596
  41.4 0.7 %emit.1 = f32[3,8,2048]{2,1,0:T(8,128)} custom-call(f32[48,2048]{1,0:T(8,128)S(1)} %get-tuple-element.23.both), custom_call_target="tpu_custom_call" | custom-call | bytes 393216 | tf_op jit(solution)/shard_map/emit/pallas_call | solution.py:486
  42.1 0.8 %back.1.refs_2_ = f32[24,2560]{1,0:T(8,128)S(1)} custom-call(s32[1,8]{1,0:T(1,128)S(1)} %copy-done.4, bf16[1,8,512,512]{3,2,1,0:T(8,128)(2,1)S(1)} %copy-done, bf16[48,512]{1,0:T(8,128)(2,1)S(1)} %collective-permute-done.14.refs_0_, bf16[48,512]{1,0:T(8,128)(2,1)S(1)} %collective-permute-done.15.refs_1_, ...), custom_call_target="tpu_custom_call" | custom-call | flops 75497472 | bytes 2097152 | tf_op jit(solution)/shard_map/back/pallas_call | solution.py:525
  42.9 1.1 %back_last.1 = f32[3,8,2048]{2,1,0:T(8,128)} custom-call(s32[1,8]{1,0:T(1,128)S(1)} %copy-done.4, bf16[1,8,512,512]{3,2,1,0:T(8,128)(2,1)S(1)} %copy-done, bf16[48,512]{1,0:T(8,128)(2,1)S(1)} %collective-permute-done.12.refs_0_, bf16[48,512]{1,0:T(8,128)(2,1)S(1)} %collective-permute-done.13.refs_1_, f32[24,2560]{1,0:T(8,128)S(1)} %back.1.refs_2_), custom_call_target="tpu_custom_call" | custom-call | flops 25165824 | bytes 2097152 | tf_op jit(solution)/shard_map/back_last/pallas_call | solution.py:525
  (44 shorter events, 0.8 us)
Async XLA Ops:
  0.6 11.3 %collective-permute-start = (bf16[3,8,2048]{2,1,0:T(8,128)(2,1)}, bf16[3,8,2048]{2,1,0:T(8,128)(2,1)S(1)}, u32[]{:S(2)}, u32[]{:S(2)}) collective-permute-start(bf16[3,8,2048]{2,1,0:T(8,128)(2,1)} %traj.1), channel_id=1, source_target_pairs={{0,1},{1,0},{2,3},{3,2},{4,5},{5,4},{6,7},{7,6},{8,9},{9,8},{10,11... | collective-permute-start | bytes 294920 | tf_op jit(solution)/shard_map/ppermute | solution.py:558
  0.7 11.2 %collective-permute-start.1 = (bf16[3,8,2048]{2,1,0:T(8,128)(2,1)}, bf16[3,8,2048]{2,1,0:T(8,128)(2,1)S(1)}, u32[]{:S(2)}, u32[]{:S(2)}) collective-permute-start(bf16[3,8,2048]{2,1,0:T(8,128)(2,1)} %inc.1), channel_id=1, source_target_pairs={{0,1},{1,0},{2,3},{3,2},{4,5},{5,4},{6,7},{7,6},{8,9},{9,8},{10,11... | collective-permute-start | bytes 294920 | tf_op jit(solution)/shard_map/ppermute | solution.py:559
  2.3 9.7 %copy-start.1 = (f32[2048]{0:T(1024)S(1)}, f32[2048]{0:T(1024)}, u32[]{:S(2)}) copy-start(f32[2048]{0:T(1024)} %param.13) | copy-start | bytes 24580
  2.3 9.7 %copy-start.2 = (f32[2048]{0:T(1024)S(1)}, f32[2048]{0:T(1024)}, u32[]{:S(2)}) copy-start(f32[2048]{0:T(1024)} %param.14) | copy-start | bytes 24580
  2.3 9.7 %copy-start.3 = (s32[2048]{0:T(1024)S(1)}, s32[2048]{0:T(1024)}, u32[]{:S(2)}) copy-start(s32[2048]{0:T(1024)} %param.15) | copy-start | bytes 24580
  2.3 9.7 %copy-start.4 = (s32[1,8]{1,0:T(1,128)S(1)}, s32[1,8]{1,0:T(1,128)}, u32[]{:S(2)}) copy-start(s32[1,8]{1,0:T(1,128)} %counts.11) | copy-start | bytes 100
  2.3 8.0 %collective-permute-start.3 = (bf16[8,2304]{1,0:T(8,128)(2,1)S(1)}, bf16[8,2304]{1,0:T(8,128)(2,1)S(1)}, u32[]{:S(2)}, u32[]{:S(2)}) collective-permute-start(bf16[8,2304]{1,0:T(8,128)(2,1)S(1)} %get-tuple-element.17), channel_id=1, source_target_pairs={{1,3},{2,0},{5,7},{6,4},{9,11},{10,8},{13,15},{14,12},{17,19},{18,... | collective-permute-start | bytes 110600 | tf_op jit(solution)/shard_map/ppermute | solution.py:556
  6.6 5.3 %collective-permute-start.2 = (bf16[8,2304]{1,0:T(8,128)(2,1)S(1)}, bf16[8,2304]{1,0:T(8,128)(2,1)S(1)}, u32[]{:S(2)}, u32[]{:S(2)}) collective-permute-start(bf16[8,2304]{1,0:T(8,128)(2,1)S(1)} %get-tuple-element.17), channel_id=1, source_target_pairs={{1,2},{2,1},{5,6},{6,5},{9,10},{10,9},{13,14},{14,13},{17,18},{18,... | collective-permute-start | bytes 110600 | tf_op jit(solution)/shard_map/ppermute | solution.py:555
  14.5 6.1 %collective-permute-start.6 = (f16[112,512]{1,0:T(8,128)(2,1)S(1)}, f16[112,512]{1,0:T(8,128)(2,1)S(1)}, u32[]{:S(2)}, u32[]{:S(2)}) collective-permute-start(f16[112,512]{1,0:T(8,128)(2,1)S(1)} %convert_element_type.40), channel_id=1, source_target_pairs={{0,8},{1,13},{2,10},{3,15},{4,12},{5,9},{6,14},{7,11},{8,0},{9,5},... | collective-permute-start | bytes 344072 | tf_op jit(solution)/shard_map/ppermute | solution.py:569
  16.2 10.1 %collective-permute-start.5 = (f16[112,512]{1,0:T(8,128)(2,1)S(1)}, f16[112,512]{1,0:T(8,128)(2,1)S(1)}, u32[]{:S(2)}, u32[]{:S(2)}) collective-permute-start(f16[112,512]{1,0:T(8,128)(2,1)S(1)} %convert_element_type.38), channel_id=1, source_target_pairs={{0,20},{1,17},{2,22},{3,19},{4,16},{5,21},{6,18},{7,23},{8,28},{9,... | collective-permute-start | bytes 344072 | tf_op jit(solution)/shard_map/ppermute | solution.py:569
  18.5 7.7 %collective-permute-start.4 = (f16[112,512]{1,0:T(8,128)(2,1)S(1)}, f16[112,512]{1,0:T(8,128)(2,1)S(1)}, u32[]{:S(2)}, u32[]{:S(2)}) collective-permute-start(f16[112,512]{1,0:T(8,128)(2,1)S(1)} %convert_element_type.36), channel_id=1, source_target_pairs={{0,24},{1,29},{2,26},{3,31},{4,28},{5,25},{6,30},{7,27},{8,16},{9,... | collective-permute-start | bytes 344072 | tf_op jit(solution)/shard_map/ppermute | solution.py:569
  19.6 8.5 %copy-start.5 = (f32[3]{0:T(128)S(1)}, f32[3]{0:T(128)}, u32[]{:S(2)}) copy-start(f32[3]{0:T(128)} %param.12) | copy-start | bytes 40
  19.6 7.2 %collective-permute-start.10 = (f16[112,512]{1,0:T(8,128)(2,1)S(1)}, f16[112,512]{1,0:T(8,128)(2,1)S(1)}, u32[]{:S(2)}, u32[]{:S(2)}) collective-permute-start(f16[112,512]{1,0:T(8,128)(2,1)S(1)} %convert_element_type.45), channel_id=1, source_target_pairs={{0,4},{1,1},{2,6},{3,3},{4,0},{5,5},{6,2},{7,7},{8,12},{9,9},{10,1... | collective-permute-start | bytes 344072 | tf_op jit(solution)/shard_map/ppermute | solution.py:569
  20.5 6.4 %collective-permute-start.9 = (f16[112,512]{1,0:T(8,128)(2,1)S(1)}, f16[112,512]{1,0:T(8,128)(2,1)S(1)}, u32[]{:S(2)}, u32[]{:S(2)}) collective-permute-start(f16[112,512]{1,0:T(8,128)(2,1)S(1)} %collective-permute-done.6), channel_id=1, source_target_pairs={{0,1},{1,0},{2,3},{3,2},{4,5},{5,4},{6,7},{7,6},{8,9},{9,8},{10,11... | collective-permute-start | bytes 344072 | tf_op jit(solution)/shard_map/ppermute | solution.py:581
  26.3 1.3 %collective-permute-start.8 = (f16[112,512]{1,0:T(8,128)(2,1)S(1)}, f16[112,512]{1,0:T(8,128)(2,1)S(1)}, u32[]{:S(2)}, u32[]{:S(2)}) collective-permute-start(f16[112,512]{1,0:T(8,128)(2,1)S(1)} %collective-permute-done.5), channel_id=1, source_target_pairs={{0,1},{1,0},{2,3},{3,2},{4,5},{5,4},{6,7},{7,6},{8,9},{9,8},{10,11... | collective-permute-start | bytes 344072 | tf_op jit(solution)/shard_map/ppermute | solution.py:581
  26.3 1.5 %collective-permute-start.7 = (f16[112,512]{1,0:T(8,128)(2,1)S(1)}, f16[112,512]{1,0:T(8,128)(2,1)S(1)}, u32[]{:S(2)}, u32[]{:S(2)}) collective-permute-start(f16[112,512]{1,0:T(8,128)(2,1)S(1)} %collective-permute-done.4), channel_id=1, source_target_pairs={{0,1},{1,0},{2,3},{3,2},{4,5},{5,4},{6,7},{7,6},{8,9},{9,8},{10,11... | collective-permute-start | bytes 344072 | tf_op jit(solution)/shard_map/ppermute | solution.py:581
  26.8 1.3 %collective-permute-start.11 = (f16[112,512]{1,0:T(8,128)(2,1)S(1)}, f16[112,512]{1,0:T(8,128)(2,1)S(1)}, u32[]{:S(2)}, u32[]{:S(2)}) collective-permute-start(f16[112,512]{1,0:T(8,128)(2,1)S(1)} %collective-permute-done.10), channel_id=1, source_target_pairs={{0,1},{1,0},{2,3},{3,2},{4,5},{5,4},{6,7},{7,6},{8,9},{9,8},{10,11... | collective-permute-start | bytes 344072 | tf_op jit(solution)/shard_map/ppermute | solution.py:581
  27.6 14.5 %copy-start = (bf16[1,8,512,512]{3,2,1,0:T(8,128)(2,1)S(1)}, bf16[1,8,512,512]{3,2,1,0:T(8,128)(2,1)}, u32[]{:S(2)}) copy-start(bf16[1,8,512,512]{3,2,1,0:T(8,128)(2,1)} %weight.5) | copy-start | bytes 12582916
  29.6 5.7 %collective-permute-start.14 = (bf16[48,512]{1,0:T(8,128)(2,1)S(1)}, bf16[48,512]{1,0:T(8,128)(2,1)S(1)}, u32[]{:S(2)}, u32[]{:S(2)}) collective-permute-start(bf16[48,512]{1,0:T(8,128)(2,1)S(1)} %get-tuple-element.25), channel_id=1, source_target_pairs={{24,0},{29,1},{26,2},{31,3},{28,4},{25,5},{30,6},{27,7},{16,8},{21... | collective-permute-start | bytes 147464 | tf_op jit(solution)/shard_map/ppermute | solution.py:594
  32.6 5.9 %collective-permute-start.15 = (bf16[48,512]{1,0:T(8,128)(2,1)S(1)}, bf16[48,512]{1,0:T(8,128)(2,1)S(1)}, u32[]{:S(2)}, u32[]{:S(2)}) collective-permute-start(bf16[48,512]{1,0:T(8,128)(2,1)S(1)} %get-tuple-element.26), channel_id=1, source_target_pairs={{20,0},{17,1},{22,2},{19,3},{16,4},{21,5},{18,6},{23,7},{28,8},{25... | collective-permute-start | bytes 147464 | tf_op jit(solution)/shard_map/ppermute | solution.py:594
  34.1 5.6 %collective-permute-start.16 = (bf16[48,512]{1,0:T(8,128)(2,1)S(1)}, bf16[48,512]{1,0:T(8,128)(2,1)S(1)}, u32[]{:S(2)}, u32[]{:S(2)}) collective-permute-start(bf16[48,512]{1,0:T(8,128)(2,1)S(1)} %get-tuple-element.27), channel_id=1, source_target_pairs={{8,0},{13,1},{10,2},{15,3},{12,4},{9,5},{14,6},{11,7},{0,8},{5,9},... | collective-permute-start | bytes 147464 | tf_op jit(solution)/shard_map/ppermute | solution.py:594
  34.1 5.6 %collective-permute-start.12 = (bf16[48,512]{1,0:T(8,128)(2,1)S(1)}, bf16[48,512]{1,0:T(8,128)(2,1)S(1)}, u32[]{:S(2)}, u32[]{:S(2)}) collective-permute-start(bf16[48,512]{1,0:T(8,128)(2,1)S(1)} %get-tuple-element.24), channel_id=1, source_target_pairs={{4,0},{1,1},{6,2},{3,3},{0,4},{5,5},{2,6},{7,7},{12,8},{9,9},{14,1... | collective-permute-start | bytes 147464 | tf_op jit(solution)/shard_map/ppermute | solution.py:594
  35.3 6.7 %collective-permute-start.17 = (bf16[48,512]{1,0:T(8,128)(2,1)S(1)}, bf16[48,512]{1,0:T(8,128)(2,1)S(1)}, u32[]{:S(2)}, u32[]{:S(2)}) collective-permute-start(bf16[48,512]{1,0:T(8,128)(2,1)S(1)} %collective-permute-done.14.refs_0_), channel_id=1, source_target_pairs={{0,1},{1,0},{2,3},{3,2},{4,5},{5,4},{6,7},{7,6},{8,9},{9,8},{10,11... | collective-permute-start | bytes 147464 | tf_op jit(solution)/shard_map/ppermute | solution.py:596
  38.5 3.6 %collective-permute-start.18 = (bf16[48,512]{1,0:T(8,128)(2,1)S(1)}, bf16[48,512]{1,0:T(8,128)(2,1)S(1)}, u32[]{:S(2)}, u32[]{:S(2)}) collective-permute-start(bf16[48,512]{1,0:T(8,128)(2,1)S(1)} %collective-permute-done.15.refs_1_), channel_id=1, source_target_pairs={{0,1},{1,0},{2,3},{3,2},{4,5},{5,4},{6,7},{7,6},{8,9},{9,8},{10,11... | collective-permute-start | bytes 147464 | tf_op jit(solution)/shard_map/ppermute | solution.py:596
  39.8 2.3 %collective-permute-start.19 = (bf16[48,512]{1,0:T(8,128)(2,1)S(1)}, bf16[48,512]{1,0:T(8,128)(2,1)S(1)}, u32[]{:S(2)}, u32[]{:S(2)}) collective-permute-start(bf16[48,512]{1,0:T(8,128)(2,1)S(1)} %collective-permute-done.16.refs_2_), channel_id=1, source_target_pairs={{0,1},{1,0},{2,3},{3,2},{4,5},{5,4},{6,7},{7,6},{8,9},{9,8},{10,11... | collective-permute-start | bytes 147464 | tf_op jit(solution)/shard_map/ppermute | solution.py:596
  39.8 3.1 %collective-permute-start.13 = (bf16[48,512]{1,0:T(8,128)(2,1)S(1)}, bf16[48,512]{1,0:T(8,128)(2,1)S(1)}, u32[]{:S(2)}, u32[]{:S(2)}) collective-permute-start(bf16[48,512]{1,0:T(8,128)(2,1)S(1)} %collective-permute-done.12.refs_0_), channel_id=1, source_target_pairs={{0,1},{1,0},{2,3},{3,2},{4,5},{5,4},{6,7},{7,6},{8,9},{9,8},{10,11... | collective-permute-start | bytes 147464 | tf_op jit(solution)/shard_map/ppermute | solution.py:596

commit v4 on v3

--- a/solution.py
+++ b/solution.py
@@ -12,6 +12,8 @@
 SUB = 8
 EDGE = 3
 COEFS = 5
+PACK = 1024
+TUNED = {8: ((5, 2, 6, 1), (4, 3, 7, 0))}
 VALUE_MAX = 6.0
 WEIGHT_MAX = 0.25
 F16_MAX = 65504.0
@@ -39,8 +41,10 @@
 def place(counts, which):
     sizes = counts[...].astype(jnp.float32)
     lane = lax.broadcasted_iota(jnp.int32, sizes.shape, 1)
-    begin = jnp.sum(jnp.where(lane < which, sizes, 0.0)).astype(jnp.int32)
-    size = jnp.sum(jnp.where(lane == which, sizes, 0.0)).astype(jnp.int32)
+    packed = jnp.sum(jnp.where(lane < which, PACK * sizes, jnp.where(lane == which, sizes, 0.0)))
+    packed = packed.astype(jnp.int32)
+    begin = packed // PACK
+    size = packed - begin * PACK
     base = pl.multiple_of((begin // LANE) * LANE, LANE)
     return base, begin - base, size
 
@@ -65,7 +69,7 @@
         self.rounds = reach // 2
         self.cube = tiles == reach and tiles & (tiles - 1) == 0
         if self.cube:
-            self.hops = self.balanced(reach)
+            self.hops = TUNED.get(reach) or self.balanced(reach)
         else:
             self.hops = [list(range(-(reach // 2), 0)), list(range(reach // 2 - 1, -1, -1))]
 
@@ -281,15 +285,10 @@
         x = rows_in[:, pl.ds(base, slots + LANE)].astype(jnp.bfloat16)
         return scale * lax.dot_general(weights, x, contract, preferred_element_type=jnp.float32)
 
-    @pl.when((group == 0) | (group == reach - 1))
-    def _():
-        e = edge(w_low[which], lax.rem(group + reach - 1, reach))
-        out[tail : tail + 2 * HALO, :rows] = e[SUB - 2 * HALO :]
-
-    @pl.when((group == reach - 2) | (group == reach - 1))
-    def _():
-        e = edge(w_high[which], lax.rem(group + 1, reach))
-        out[tail : tail + 2 * HALO, LANE : LANE + rows] = e[: 2 * HALO]
+    e = edge(w_low[which], lax.rem(group + reach - 1, reach))
+    out[tail : tail + 2 * HALO, :rows] = e[SUB - 2 * HALO :]
+    e = edge(w_high[which], lax.rem(group + 1, reach))
+    out[tail : tail + 2 * HALO, LANE : LANE + rows] = e[: 2 * HALO]
 
 
 def forward(plan, which, counts, rows_in, courant, vertical, offset, w, w_low, w_high, scale, tail):
@@ -580,9 +579,8 @@
     for piece in pieces:
         others.append(lax.ppermute(piece, "lev", swap))
     whole = [piece.astype(jnp.float32) for piece in pieces + others]
-    final = plan.rounds - 1
-    early = [k for k in range(2 * plan.rounds) if k % plan.rounds != final]
-    late = [final, plan.rounds + final]
+    early = list(range(2 * plan.rounds - 1))
+    late = [2 * plan.rounds - 1]
     pick = lambda values, numbers: [values[k] for k in numbers]
 
     acc, side = assemble(plan, early, pick(whole, early), 1.0 / scale, tail, cols)

time: 44.2 us -> 42.3 us (0.957)
  waiting for transfers between devices: 9.45 us -> 2.88 us
  starting transfers between devices: 23.4 us -> 28.5 us
  Pallas kernels: 9.95 us -> 9.4 us
    ppermute x4, starting transfers between devices: 0.77 us -> 6.73 us  [step(): others.append(lax.ppermute(piece, 'lev', swap))]
    ppermute x4, waiting for transfers between devices: 5.79 us -> 1.17 us  [step(): pieces.append(lax.ppermute(message, both, route))]
    ppermute x1, starting transfers between devices: 4.31 us -> 1.29 us  [step(): ext_too = lax.ppermute(border, 'lev', far)]
    ppermute x1, starting transfers between devices: 1.92 us -> 4.63 us  [step(): ext = lax.ppermute(border, 'lev', near)]
    ppermute x1, waiting for transfers between devices: 1.6 us -> 0.01 us  [step(): ext = lax.ppermute(border, 'lev', near)]
    ppermute x4, starting transfers between devices: 5.36 us -> 3.97 us  [step(): regained.append(lax.ppermute(window, 'lev', swap))]
    ppermute x4, starting transfers between devices: 5.17 us -> 5.9 us  [step(): returned.append(lax.ppermute(window, both, [(b, a) for a, b in route]))]
    pallas_call x4, Pallas kernels: 2.84 us -> 2.3 us  [forward(): pl.pallas_call(functools.partial(forward_kernel, plan, which, scale, tail...]
  transfers between devices with their start and end apart: 20 -> 20, of which waited for: 8 -> 4; matrix products, arithmetic and copies ran while one was open for 0% -> 0% of each run, Pallas kernels for 11% -> 12%
where the time goes in v4:
time: 42.3 us; the launch traced here: 42 us
  starting transfers between devices  28.5 us (67%)
  Pallas kernels  9.4 us (22%)
  waiting for transfers between devices  2.88 us (7%)
  between operations  0.97 us (2%)
    ppermute x4, starting transfers between devices, step(): others.append(lax.ppermute(piece, 'lev', swap))  6.73 us
    ppermute x4, starting transfers between devices, step(): returned.append(lax.ppermute(window, both, [(b, a) for a, b in route]))  5.9 us
    ppermute x4, starting transfers between devices, step(): pieces.append(lax.ppermute(message, both, route))  5.43 us
    ppermute x1, starting transfers between devices, step(): ext = lax.ppermute(border, 'lev', near)  4.63 us
    ppermute x4, starting transfers between devices, step(): regained.append(lax.ppermute(window, 'lev', swap))  3.97 us
    pallas_call x4, Pallas kernels, forward(): pl.pallas_call(functools.partial(forward_kernel, plan, which, scale, tail...  2.3 us
    pallas_call x2, Pallas kernels, backward(): pl.pallas_call(functools.partial(backward_kernel, plan, int(last), number...  1.83 us
    pallas_call x1, Pallas kernels, load(): pl.pallas_call(functools.partial(load_kernel, plan), in_specs=[HBM], out_...  1.74 us
  transfers between devices with their start and end apart: 20, of which 4 were waited for; matrix products, arithmetic and copies ran while one was open for 0% of the time, Pallas kernels for 12%

profile of v4, /device:TPU:1, one launch (start us, length us, event | category | flops | bytes accessed | tf_op | source)
XLA Modules:
  0.0 42.0 jit_solution(8708177995450920808)
XLA Ops:
  0.7 0.5 %collective-permute-start.1 = (bf16[3,8,2048]{2,1,0:T(8,128)(2,1)}, bf16[3,8,2048]{2,1,0:T(8,128)(2,1)S(1)}, u32[]{:S(2)}, u32[]{:S(2)}) collective-permute-start(bf16[3,8,2048]{2,1,0:T(8,128)(2,1)} %inc.1), channel_id=1, source_target_pairs={{0,1},{1,0},{2,3},{3,2},{4,5},{5,4},{6,7},{7,6},{8,9},{9,8},{10,11... | collective-permute-start | bytes 294920 | tf_op jit(solution)/shard_map/ppermute | solution.py:558
  1.2 1.1 %border.1 = (bf16[3,8,2048]{2,1,0:T(8,128)(2,1)S(1)}, bf16[3,8,2048]{2,1,0:T(8,128)(2,1)S(1)}, bf16[8,2304]{1,0:T(8,128)(2,1)S(1)}) custom-call(bf16[3,8,2048]{2,1,0:T(8,128)(2,1)} %traj.1, bf16[3,8,2048]{2,1,0:T(8,128)(2,1)} %inc.1), custom_call_target="tpu_custom_call" | custom-call | bytes 393216 | tf_op jit(solution)/shard_map/border/pallas_call | solution.py:166
  2.3 4.6 %collective-permute-start.2 = (bf16[8,2304]{1,0:T(8,128)(2,1)S(1)}, bf16[8,2304]{1,0:T(8,128)(2,1)S(1)}, u32[]{:S(2)}, u32[]{:S(2)}) collective-permute-start(bf16[8,2304]{1,0:T(8,128)(2,1)S(1)} %get-tuple-element.17), channel_id=1, source_target_pairs={{1,2},{2,1},{5,6},{6,5},{9,10},{10,9},{13,14},{14,13},{17,18},{18,... | collective-permute-start | bytes 110600 | tf_op jit(solution)/shard_map/ppermute | solution.py:554
  7.0 1.3 %collective-permute-start.3 = (bf16[8,2304]{1,0:T(8,128)(2,1)S(1)}, bf16[8,2304]{1,0:T(8,128)(2,1)S(1)}, u32[]{:S(2)}, u32[]{:S(2)}) collective-permute-start(bf16[8,2304]{1,0:T(8,128)(2,1)S(1)} %get-tuple-element.17), channel_id=1, source_target_pairs={{1,3},{2,0},{5,7},{6,4},{9,11},{10,8},{13,15},{14,12},{17,19},{18,... | collective-permute-start | bytes 110600 | tf_op jit(solution)/shard_map/ppermute | solution.py:555
  8.3 1.7 %fetch.1 = (bf16[4,512,512]{2,1,0:T(8,128)(2,1)S(1)}, bf16[4,8,512]{2,1,0:T(8,128)(2,1)S(1)}, bf16[4,8,512]{2,1,0:T(8,128)(2,1)S(1)}) custom-call(bf16[1,8,512,512]{3,2,1,0:T(8,128)(2,1)} %weight.5), custom_call_target="tpu_custom_call" | custom-call | bytes 4194304 | tf_op jit(solution)/shard_map/fetch/pallas_call | solution.py:208
  10.2 0.6 %shard_map.95 = f32[112,512]{1,0:T(8,128)S(1)} custom-call(s32[1,8]{1,0:T(1,128)S(1)} %copy-done.4, f32[112,2560]{1,0:T(8,128)S(1)} %gather.1.rows_in, f32[1,2048]{1,0:T(1,128)S(1)} %bitcast.4, f32[1,2048]{1,0:T(1,128)S(1)} %bitcast.9, s32[1,2048]{1,0:T(1,128)S(1)} %bitcast.14, bf16[4,512,512]{2,1,0:T(8,128)(2,1)S(1)} %get-tuple-element.18.w, ...), custom_call_target="tpu_custom_call" | custom-call | flops 58720256 | bytes 1146880 | tf_op jit(solution)/shard_map/pallas_call | solution.py:297
  10.7 0.6 %shard_map.96 = f32[112,512]{1,0:T(8,128)S(1)} custom-call(s32[1,8]{1,0:T(1,128)S(1)} %copy-done.4, f32[112,2560]{1,0:T(8,128)S(1)} %gather.1.rows_in, f32[1,2048]{1,0:T(1,128)S(1)} %bitcast.5, f32[1,2048]{1,0:T(1,128)S(1)} %bitcast.10, s32[1,2048]{1,0:T(1,128)S(1)} %bitcast.15, bf16[4,512,512]{2,1,0:T(8,128)(2,1)S(1)} %get-tuple-element.18.w, ...), custom_call_target="tpu_custom_call" | custom-call | flops 58720256 | bytes 1146880 | tf_op jit(solution)/shard_map/pallas_call | solution.py:297
  11.3 0.6 %shard_map.97 = f32[112,512]{1,0:T(8,128)S(1)} custom-call(s32[1,8]{1,0:T(1,128)S(1)} %copy-done.4, f32[112,2560]{1,0:T(8,128)S(1)} %gather.1.rows_in, f32[1,2048]{1,0:T(1,128)S(1)} %bitcast.6, f32[1,2048]{1,0:T(1,128)S(1)} %bitcast.11, s32[1,2048]{1,0:T(1,128)S(1)} %bitcast.16, bf16[4,512,512]{2,1,0:T(8,128)(2,1)S(1)} %get-tuple-element.18.w, ...), custom_call_target="tpu_custom_call" | custom-call | flops 58720256 | bytes 1146880 | tf_op jit(solution)/shard_map/pallas_call | solution.py:297
  11.9 2.4 %collective-permute-start.4 = (f16[112,512]{1,0:T(8,128)(2,1)S(1)}, f16[112,512]{1,0:T(8,128)(2,1)S(1)}, u32[]{:S(2)}, u32[]{:S(2)}) collective-permute-start(f16[112,512]{1,0:T(8,128)(2,1)S(1)} %convert_element_type.36), channel_id=1, source_target_pairs={{0,20},{1,17},{2,22},{3,19},{4,16},{5,21},{6,18},{7,23},{8,28},{9,... | collective-permute-start | bytes 344072 | tf_op jit(solution)/shard_map/ppermute | solution.py:568
  14.3 2.3 %collective-permute-start.5 = (f16[112,512]{1,0:T(8,128)(2,1)S(1)}, f16[112,512]{1,0:T(8,128)(2,1)S(1)}, u32[]{:S(2)}, u32[]{:S(2)}) collective-permute-start(f16[112,512]{1,0:T(8,128)(2,1)S(1)} %convert_element_type.38), channel_id=1, source_target_pairs={{0,8},{1,13},{2,10},{3,15},{4,12},{5,9},{6,14},{7,11},{8,0},{9,5},... | collective-permute-start | bytes 344072 | tf_op jit(solution)/shard_map/ppermute | solution.py:568
  16.7 0.6 %shard_map.98 = f32[112,512]{1,0:T(8,128)S(1)} custom-call(s32[1,8]{1,0:T(1,128)S(1)} %copy-done.4, f32[112,2560]{1,0:T(8,128)S(1)} %gather.1.rows_in, f32[1,2048]{1,0:T(1,128)S(1)} %bitcast.7, f32[1,2048]{1,0:T(1,128)S(1)} %bitcast.12, s32[1,2048]{1,0:T(1,128)S(1)} %bitcast.17, bf16[4,512,512]{2,1,0:T(8,128)(2,1)S(1)} %get-tuple-element.18.w, ...), custom_call_target="tpu_custom_call" | custom-call | flops 58720256 | bytes 1146880 | tf_op jit(solution)/shard_map/pallas_call | solution.py:297
  17.4 0.7 %collective-permute-start.7 = (f16[112,512]{1,0:T(8,128)(2,1)S(1)}, f16[112,512]{1,0:T(8,128)(2,1)S(1)}, u32[]{:S(2)}, u32[]{:S(2)}) collective-permute-start(f16[112,512]{1,0:T(8,128)(2,1)S(1)} %convert_element_type.42), channel_id=1, source_target_pairs={{0,4},{1,1},{2,6},{3,3},{4,0},{5,5},{6,2},{7,7},{8,12},{9,9},{10,1... | collective-permute-start | bytes 344072 | tf_op jit(solution)/shard_map/ppermute | solution.py:568
  18.0 0.1 collective-permute-done.4
  18.2 4.6 %collective-permute-start.8 = (f16[112,512]{1,0:T(8,128)(2,1)S(1)}, f16[112,512]{1,0:T(8,128)(2,1)S(1)}, u32[]{:S(2)}, u32[]{:S(2)}) collective-permute-start(f16[112,512]{1,0:T(8,128)(2,1)S(1)} %collective-permute-done.4), channel_id=1, source_target_pairs={{0,1},{1,0},{2,3},{3,2},{4,5},{5,4},{6,7},{7,6},{8,9},{9,8},{10,11... | collective-permute-start | bytes 344072 | tf_op jit(solution)/shard_map/ppermute | solution.py:580
  22.8 0.6 %collective-permute-start.9 = (f16[112,512]{1,0:T(8,128)(2,1)S(1)}, f16[112,512]{1,0:T(8,128)(2,1)S(1)}, u32[]{:S(2)}, u32[]{:S(2)}) collective-permute-start(f16[112,512]{1,0:T(8,128)(2,1)S(1)} %collective-permute-done.5), channel_id=1, source_target_pairs={{0,1},{1,0},{2,3},{3,2},{4,5},{5,4},{6,7},{7,6},{8,9},{9,8},{10,11... | collective-permute-start | bytes 344072 | tf_op jit(solution)/shard_map/ppermute | solution.py:580
  23.4 1.0 %collective-permute-done.6 = f16[112,512]{1,0:T(8,128)(2,1)S(1)} collective-permute-done((f16[112,512]{1,0:T(8,128)(2,1)S(1)}, f16[112,512]{1,0:T(8,128)(2,1)S(1)}, u32[]{:S(2)}, u32[]{:S(2)}) %collective-permute-start.6) | collective-permute-done | bytes 114720 | tf_op jit(solution)/shard_map/ppermute | solution.py:568
  24.4 0.2 collective-permute-start.10
  24.6 1.3 %collective-permute-start.11 = (f16[112,512]{1,0:T(8,128)(2,1)S(1)}, f16[112,512]{1,0:T(8,128)(2,1)S(1)}, u32[]{:S(2)}, u32[]{:S(2)}) collective-permute-start(f16[112,512]{1,0:T(8,128)(2,1)S(1)} %collective-permute-done.7), channel_id=1, source_target_pairs={{0,1},{1,0},{2,3},{3,2},{4,5},{5,4},{6,7},{7,6},{8,9},{9,8},{10,11... | collective-permute-start | bytes 344072 | tf_op jit(solution)/shard_map/ppermute | solution.py:580
  26.2 0.3 assemble.1
  26.4 0.5 %collective-permute-done.11 = f16[112,512]{1,0:T(8,128)(2,1)S(1)} collective-permute-done((f16[112,512]{1,0:T(8,128)(2,1)S(1)}, f16[112,512]{1,0:T(8,128)(2,1)S(1)}, u32[]{:S(2)}, u32[]{:S(2)}) %collective-permute-start.11) | collective-permute-done | bytes 114720 | tf_op jit(solution)/shard_map/ppermute | solution.py:580
  26.9 1.4 %stencil.1 = (f32[48,2048]{1,0:T(8,128)S(1)}, bf16[48,512]{1,0:T(8,128)(2,1)S(1)}, bf16[48,512]{1,0:T(8,128)(2,1)S(1)}, bf16[48,512]{1,0:T(8,128)(2,1)S(1)}, bf16[48,512]{1,0:T(8,128)(2,1)S(1)}) custom-call(f32[1,3]{1,0:T(1,128)S(1)} %bitcast.19, f32[112,2176]{1,0:T(8,128)S(1)} %get-tuple-element.21.acc_in, f32[32,128]{1,0:T(8,128)S(1)} %get-tuple-element.22.side, ...), custom_call_target="tpu_custom_call" | custom-call | flops 22937600 | bytes 1835008 | tf_op jit(solution)/shard_map/stencil/pallas_call | solution.py:459
  28.4 3.1 %collective-permute-start.14 = (bf16[48,512]{1,0:T(8,128)(2,1)S(1)}, bf16[48,512]{1,0:T(8,128)(2,1)S(1)}, u32[]{:S(2)}, u32[]{:S(2)}) collective-permute-start(bf16[48,512]{1,0:T(8,128)(2,1)S(1)} %get-tuple-element.25), channel_id=1, source_target_pairs={{20,0},{17,1},{22,2},{19,3},{16,4},{21,5},{18,6},{23,7},{28,8},{25... | collective-permute-start | bytes 147464 | tf_op jit(solution)/shard_map/ppermute | solution.py:592
  31.5 0.7 %collective-permute-start.15 = (bf16[48,512]{1,0:T(8,128)(2,1)S(1)}, bf16[48,512]{1,0:T(8,128)(2,1)S(1)}, u32[]{:S(2)}, u32[]{:S(2)}) collective-permute-start(bf16[48,512]{1,0:T(8,128)(2,1)S(1)} %get-tuple-element.26), channel_id=1, source_target_pairs={{8,0},{13,1},{10,2},{15,3},{12,4},{9,5},{14,6},{11,7},{0,8},{5,9},... | collective-permute-start | bytes 147464 | tf_op jit(solution)/shard_map/ppermute | solution.py:592
  32.2 1.4 %collective-permute-start.16 = (bf16[48,512]{1,0:T(8,128)(2,1)S(1)}, bf16[48,512]{1,0:T(8,128)(2,1)S(1)}, u32[]{:S(2)}, u32[]{:S(2)}) collective-permute-start(bf16[48,512]{1,0:T(8,128)(2,1)S(1)} %get-tuple-element.27), channel_id=1, source_target_pairs={{24,0},{29,1},{26,2},{31,3},{28,4},{25,5},{30,6},{27,7},{16,8},{21... | collective-permute-start | bytes 147464 | tf_op jit(solution)/shard_map/ppermute | solution.py:592
  33.6 0.7 %collective-permute-start.12 = (bf16[48,512]{1,0:T(8,128)(2,1)S(1)}, bf16[48,512]{1,0:T(8,128)(2,1)S(1)}, u32[]{:S(2)}, u32[]{:S(2)}) collective-permute-start(bf16[48,512]{1,0:T(8,128)(2,1)S(1)} %get-tuple-element.24), channel_id=1, source_target_pairs={{4,0},{1,1},{6,2},{3,3},{0,4},{5,5},{2,6},{7,7},{12,8},{9,9},{14,1... | collective-permute-start | bytes 147464 | tf_op jit(solution)/shard_map/ppermute | solution.py:592
  34.3 2.3 %collective-permute-start.17 = (bf16[48,512]{1,0:T(8,128)(2,1)S(1)}, bf16[48,512]{1,0:T(8,128)(2,1)S(1)}, u32[]{:S(2)}, u32[]{:S(2)}) collective-permute-start(bf16[48,512]{1,0:T(8,128)(2,1)S(1)} %collective-permute-done.14.refs_0_), channel_id=1, source_target_pairs={{0,1},{1,0},{2,3},{3,2},{4,5},{5,4},{6,7},{7,6},{8,9},{9,8},{10,11... | collective-permute-start | bytes 147464 | tf_op jit(solution)/shard_map/ppermute | solution.py:594
  36.7 1.2 %collective-permute-done.16.refs_2_ = bf16[48,512]{1,0:T(8,128)(2,1)S(1)} collective-permute-done((bf16[48,512]{1,0:T(8,128)(2,1)S(1)}, bf16[48,512]{1,0:T(8,128)(2,1)S(1)}, u32[]{:S(2)}, u32[]{:S(2)}) %collective-permute-start.16) | collective-permute-done | bytes 49184 | tf_op jit(solution)/shard_map/ppermute | solution.py:592
  37.9 1.0 %collective-permute-start.19 = (bf16[48,512]{1,0:T(8,128)(2,1)S(1)}, bf16[48,512]{1,0:T(8,128)(2,1)S(1)}, u32[]{:S(2)}, u32[]{:S(2)}) collective-permute-start(bf16[48,512]{1,0:T(8,128)(2,1)S(1)} %collective-permute-done.16.refs_2_), channel_id=1, source_target_pairs={{0,1},{1,0},{2,3},{3,2},{4,5},{5,4},{6,7},{7,6},{8,9},{9,8},{10,11... | collective-permute-start | bytes 147464 | tf_op jit(solution)/shard_map/ppermute | solution.py:594
  38.9 0.5 %collective-permute-start.13 = (bf16[48,512]{1,0:T(8,128)(2,1)S(1)}, bf16[48,512]{1,0:T(8,128)(2,1)S(1)}, u32[]{:S(2)}, u32[]{:S(2)}) collective-permute-start(bf16[48,512]{1,0:T(8,128)(2,1)S(1)} %collective-permute-done.12.refs_3_), channel_id=1, source_target_pairs={{0,1},{1,0},{2,3},{3,2},{4,5},{5,4},{6,7},{7,6},{8,9},{9,8},{10,11... | collective-permute-start | bytes 147464 | tf_op jit(solution)/shard_map/ppermute | solution.py:594
  39.5 0.7 %emit.1 = f32[3,8,2048]{2,1,0:T(8,128)} custom-call(f32[48,2048]{1,0:T(8,128)S(1)} %get-tuple-element.23.both), custom_call_target="tpu_custom_call" | custom-call | bytes 393216 | tf_op jit(solution)/shard_map/emit/pallas_call | solution.py:485
  40.2 0.8 %back.1.refs_1_ = f32[24,2560]{1,0:T(8,128)S(1)} custom-call(s32[1,8]{1,0:T(1,128)S(1)} %copy-done.4, bf16[1,8,512,512]{3,2,1,0:T(8,128)(2,1)S(1)} %copy-done, bf16[48,512]{1,0:T(8,128)(2,1)S(1)} %collective-permute-done.14.refs_0_, bf16[48,512]{1,0:T(8,128)(2,1)S(1)} %collective-permute-done.15.refs_1_, ...), custom_call_target="tpu_custom_call" | custom-call | flops 88080384 | bytes 2097152 | tf_op jit(solution)/shard_map/back/pallas_call | solution.py:524
  41.1 1.0 %back_last.1 = f32[3,8,2048]{2,1,0:T(8,128)} custom-call(s32[1,8]{1,0:T(1,128)S(1)} %copy-done.4, bf16[1,8,512,512]{3,2,1,0:T(8,128)(2,1)S(1)} %copy-done, bf16[48,512]{1,0:T(8,128)(2,1)S(1)} %collective-permute-done.13.refs_0_, f32[24,2560]{1,0:T(8,128)S(1)} %back.1.refs_1_), custom_call_target="tpu_custom_call" | custom-call | flops 12582912 | bytes 2097152 | tf_op jit(solution)/shard_map/back_last/pallas_call | solution.py:524
  (44 shorter events, 0.6 us)
Async XLA Ops:
  0.6 9.4 %collective-permute-start = (bf16[3,8,2048]{2,1,0:T(8,128)(2,1)}, bf16[3,8,2048]{2,1,0:T(8,128)(2,1)S(1)}, u32[]{:S(2)}, u32[]{:S(2)}) collective-permute-start(bf16[3,8,2048]{2,1,0:T(8,128)(2,1)} %traj.1), channel_id=1, source_target_pairs={{0,1},{1,0},{2,3},{3,2},{4,5},{5,4},{6,7},{7,6},{8,9},{9,8},{10,11... | collective-permute-start | bytes 294920 | tf_op jit(solution)/shard_map/ppermute | solution.py:557
  0.7 9.3 %collective-permute-start.1 = (bf16[3,8,2048]{2,1,0:T(8,128)(2,1)}, bf16[3,8,2048]{2,1,0:T(8,128)(2,1)S(1)}, u32[]{:S(2)}, u32[]{:S(2)}) collective-permute-start(bf16[3,8,2048]{2,1,0:T(8,128)(2,1)} %inc.1), channel_id=1, source_target_pairs={{0,1},{1,0},{2,3},{3,2},{4,5},{5,4},{6,7},{7,6},{8,9},{9,8},{10,11... | collective-permute-start | bytes 294920 | tf_op jit(solution)/shard_map/ppermute | solution.py:558
  2.3 7.9 %copy-start.1 = (f32[2048]{0:T(1024)S(1)}, f32[2048]{0:T(1024)}, u32[]{:S(2)}) copy-start(f32[2048]{0:T(1024)} %param.13) | copy-start | bytes 24580
  2.3 7.9 %copy-start.2 = (f32[2048]{0:T(1024)S(1)}, f32[2048]{0:T(1024)}, u32[]{:S(2)}) copy-start(f32[2048]{0:T(1024)} %param.14) | copy-start | bytes 24580
  2.3 7.9 %copy-start.3 = (s32[2048]{0:T(1024)S(1)}, s32[2048]{0:T(1024)}, u32[]{:S(2)}) copy-start(s32[2048]{0:T(1024)} %param.15) | copy-start | bytes 24580
  2.3 7.9 %copy-start.4 = (s32[1,8]{1,0:T(1,128)S(1)}, s32[1,8]{1,0:T(1,128)}, u32[]{:S(2)}) copy-start(s32[1,8]{1,0:T(1,128)} %counts.11) | copy-start | bytes 100
  2.3 7.7 %collective-permute-start.2 = (bf16[8,2304]{1,0:T(8,128)(2,1)S(1)}, bf16[8,2304]{1,0:T(8,128)(2,1)S(1)}, u32[]{:S(2)}, u32[]{:S(2)}) collective-permute-start(bf16[8,2304]{1,0:T(8,128)(2,1)S(1)} %get-tuple-element.17), channel_id=1, source_target_pairs={{1,2},{2,1},{5,6},{6,5},{9,10},{10,9},{13,14},{14,13},{17,18},{18,... | collective-permute-start | bytes 110600 | tf_op jit(solution)/shard_map/ppermute | solution.py:554
  7.0 3.1 %collective-permute-start.3 = (bf16[8,2304]{1,0:T(8,128)(2,1)S(1)}, bf16[8,2304]{1,0:T(8,128)(2,1)S(1)}, u32[]{:S(2)}, u32[]{:S(2)}) collective-permute-start(bf16[8,2304]{1,0:T(8,128)(2,1)S(1)} %get-tuple-element.17), channel_id=1, source_target_pairs={{1,3},{2,0},{5,7},{6,4},{9,11},{10,8},{13,15},{14,12},{17,19},{18,... | collective-permute-start | bytes 110600 | tf_op jit(solution)/shard_map/ppermute | solution.py:555
  11.9 6.2 %collective-permute-start.4 = (f16[112,512]{1,0:T(8,128)(2,1)S(1)}, f16[112,512]{1,0:T(8,128)(2,1)S(1)}, u32[]{:S(2)}, u32[]{:S(2)}) collective-permute-start(f16[112,512]{1,0:T(8,128)(2,1)S(1)} %convert_element_type.36), channel_id=1, source_target_pairs={{0,20},{1,17},{2,22},{3,19},{4,16},{5,21},{6,18},{7,23},{8,28},{9,... | collective-permute-start | bytes 344072 | tf_op jit(solution)/shard_map/ppermute | solution.py:568
  14.3 8.5 %collective-permute-start.5 = (f16[112,512]{1,0:T(8,128)(2,1)S(1)}, f16[112,512]{1,0:T(8,128)(2,1)S(1)}, u32[]{:S(2)}, u32[]{:S(2)}) collective-permute-start(f16[112,512]{1,0:T(8,128)(2,1)S(1)} %convert_element_type.38), channel_id=1, source_target_pairs={{0,8},{1,13},{2,10},{3,15},{4,12},{5,9},{6,14},{7,11},{8,0},{9,5},... | collective-permute-start | bytes 344072 | tf_op jit(solution)/shard_map/ppermute | solution.py:568
  16.7 7.7 %collective-permute-start.6 = (f16[112,512]{1,0:T(8,128)(2,1)S(1)}, f16[112,512]{1,0:T(8,128)(2,1)S(1)}, u32[]{:S(2)}, u32[]{:S(2)}) collective-permute-start(f16[112,512]{1,0:T(8,128)(2,1)S(1)} %convert_element_type.40), channel_id=1, source_target_pairs={{0,24},{1,29},{2,26},{3,31},{4,28},{5,25},{6,30},{7,27},{8,16},{9,... | collective-permute-start | bytes 344072 | tf_op jit(solution)/shard_map/ppermute | solution.py:568
  17.3 9.6 %copy-start.5 = (f32[3]{0:T(128)S(1)}, f32[3]{0:T(128)}, u32[]{:S(2)}) copy-start(f32[3]{0:T(128)} %param.12) | copy-start | bytes 40
  17.4 7.3 %collective-permute-start.7 = (f16[112,512]{1,0:T(8,128)(2,1)S(1)}, f16[112,512]{1,0:T(8,128)(2,1)S(1)}, u32[]{:S(2)}, u32[]{:S(2)}) collective-permute-start(f16[112,512]{1,0:T(8,128)(2,1)S(1)} %convert_element_type.42), channel_id=1, source_target_pairs={{0,4},{1,1},{2,6},{3,3},{4,0},{5,5},{6,2},{7,7},{8,12},{9,9},{10,1... | collective-permute-start | bytes 344072 | tf_op jit(solution)/shard_map/ppermute | solution.py:568
  18.2 7.9 %collective-permute-start.8 = (f16[112,512]{1,0:T(8,128)(2,1)S(1)}, f16[112,512]{1,0:T(8,128)(2,1)S(1)}, u32[]{:S(2)}, u32[]{:S(2)}) collective-permute-start(f16[112,512]{1,0:T(8,128)(2,1)S(1)} %collective-permute-done.4), channel_id=1, source_target_pairs={{0,1},{1,0},{2,3},{3,2},{4,5},{5,4},{6,7},{7,6},{8,9},{9,8},{10,11... | collective-permute-start | bytes 344072 | tf_op jit(solution)/shard_map/ppermute | solution.py:580
  22.8 3.3 %collective-permute-start.9 = (f16[112,512]{1,0:T(8,128)(2,1)S(1)}, f16[112,512]{1,0:T(8,128)(2,1)S(1)}, u32[]{:S(2)}, u32[]{:S(2)}) collective-permute-start(f16[112,512]{1,0:T(8,128)(2,1)S(1)} %collective-permute-done.5), channel_id=1, source_target_pairs={{0,1},{1,0},{2,3},{3,2},{4,5},{5,4},{6,7},{7,6},{8,9},{9,8},{10,11... | collective-permute-start | bytes 344072 | tf_op jit(solution)/shard_map/ppermute | solution.py:580
  24.4 1.7 %collective-permute-start.10 = (f16[112,512]{1,0:T(8,128)(2,1)S(1)}, f16[112,512]{1,0:T(8,128)(2,1)S(1)}, u32[]{:S(2)}, u32[]{:S(2)}) collective-permute-start(f16[112,512]{1,0:T(8,128)(2,1)S(1)} %collective-permute-done.6), channel_id=1, source_target_pairs={{0,1},{1,0},{2,3},{3,2},{4,5},{5,4},{6,7},{7,6},{8,9},{9,8},{10,11... | collective-permute-start | bytes 344072 | tf_op jit(solution)/shard_map/ppermute | solution.py:580
  24.6 2.3 %collective-permute-start.11 = (f16[112,512]{1,0:T(8,128)(2,1)S(1)}, f16[112,512]{1,0:T(8,128)(2,1)S(1)}, u32[]{:S(2)}, u32[]{:S(2)}) collective-permute-start(f16[112,512]{1,0:T(8,128)(2,1)S(1)} %collective-permute-done.7), channel_id=1, source_target_pairs={{0,1},{1,0},{2,3},{3,2},{4,5},{5,4},{6,7},{7,6},{8,9},{9,8},{10,11... | collective-permute-start | bytes 344072 | tf_op jit(solution)/shard_map/ppermute | solution.py:580
  26.1 14.1 %copy-start = (bf16[1,8,512,512]{3,2,1,0:T(8,128)(2,1)S(1)}, bf16[1,8,512,512]{3,2,1,0:T(8,128)(2,1)}, u32[]{:S(2)}) copy-start(bf16[1,8,512,512]{3,2,1,0:T(8,128)(2,1)} %weight.5) | copy-start | bytes 12582916
  28.4 5.9 %collective-permute-start.14 = (bf16[48,512]{1,0:T(8,128)(2,1)S(1)}, bf16[48,512]{1,0:T(8,128)(2,1)S(1)}, u32[]{:S(2)}, u32[]{:S(2)}) collective-permute-start(bf16[48,512]{1,0:T(8,128)(2,1)S(1)} %get-tuple-element.25), channel_id=1, source_target_pairs={{20,0},{17,1},{22,2},{19,3},{16,4},{21,5},{18,6},{23,7},{28,8},{25... | collective-permute-start | bytes 147464 | tf_op jit(solution)/shard_map/ppermute | solution.py:592
  31.5 5.2 %collective-permute-start.15 = (bf16[48,512]{1,0:T(8,128)(2,1)S(1)}, bf16[48,512]{1,0:T(8,128)(2,1)S(1)}, u32[]{:S(2)}, u32[]{:S(2)}) collective-permute-start(bf16[48,512]{1,0:T(8,128)(2,1)S(1)} %get-tuple-element.26), channel_id=1, source_target_pairs={{8,0},{13,1},{10,2},{15,3},{12,4},{9,5},{14,6},{11,7},{0,8},{5,9},... | collective-permute-start | bytes 147464 | tf_op jit(solution)/shard_map/ppermute | solution.py:592
  32.2 5.7 %collective-permute-start.16 = (bf16[48,512]{1,0:T(8,128)(2,1)S(1)}, bf16[48,512]{1,0:T(8,128)(2,1)S(1)}, u32[]{:S(2)}, u32[]{:S(2)}) collective-permute-start(bf16[48,512]{1,0:T(8,128)(2,1)S(1)} %get-tuple-element.27), channel_id=1, source_target_pairs={{24,0},{29,1},{26,2},{31,3},{28,4},{25,5},{30,6},{27,7},{16,8},{21... | collective-permute-start | bytes 147464 | tf_op jit(solution)/shard_map/ppermute | solution.py:592
  33.6 5.3 %collective-permute-start.12 = (bf16[48,512]{1,0:T(8,128)(2,1)S(1)}, bf16[48,512]{1,0:T(8,128)(2,1)S(1)}, u32[]{:S(2)}, u32[]{:S(2)}) collective-permute-start(bf16[48,512]{1,0:T(8,128)(2,1)S(1)} %get-tuple-element.24), channel_id=1, source_target_pairs={{4,0},{1,1},{6,2},{3,3},{0,4},{5,5},{2,6},{7,7},{12,8},{9,9},{14,1... | collective-permute-start | bytes 147464 | tf_op jit(solution)/shard_map/ppermute | solution.py:592
  34.3 5.9 %collective-permute-start.17 = (bf16[48,512]{1,0:T(8,128)(2,1)S(1)}, bf16[48,512]{1,0:T(8,128)(2,1)S(1)}, u32[]{:S(2)}, u32[]{:S(2)}) collective-permute-start(bf16[48,512]{1,0:T(8,128)(2,1)S(1)} %collective-permute-done.14.refs_0_), channel_id=1, source_target_pairs={{0,1},{1,0},{2,3},{3,2},{4,5},{5,4},{6,7},{7,6},{8,9},{9,8},{10,11... | collective-permute-start | bytes 147464 | tf_op jit(solution)/shard_map/ppermute | solution.py:594
  36.7 3.5 %collective-permute-start.18 = (bf16[48,512]{1,0:T(8,128)(2,1)S(1)}, bf16[48,512]{1,0:T(8,128)(2,1)S(1)}, u32[]{:S(2)}, u32[]{:S(2)}) collective-permute-start(bf16[48,512]{1,0:T(8,128)(2,1)S(1)} %collective-permute-done.15.refs_1_), channel_id=1, source_target_pairs={{0,1},{1,0},{2,3},{3,2},{4,5},{5,4},{6,7},{7,6},{8,9},{9,8},{10,11... | collective-permute-start | bytes 147464 | tf_op jit(solution)/shard_map/ppermute | solution.py:594
  37.9 2.3 %collective-permute-start.19 = (bf16[48,512]{1,0:T(8,128)(2,1)S(1)}, bf16[48,512]{1,0:T(8,128)(2,1)S(1)}, u32[]{:S(2)}, u32[]{:S(2)}) collective-permute-start(bf16[48,512]{1,0:T(8,128)(2,1)S(1)} %collective-permute-done.16.refs_2_), channel_id=1, source_target_pairs={{0,1},{1,0},{2,3},{3,2},{4,5},{5,4},{6,7},{7,6},{8,9},{9,8},{10,11... | collective-permute-start | bytes 147464 | tf_op jit(solution)/shard_map/ppermute | solution.py:594
  38.9 2.1 %collective-permute-start.13 = (bf16[48,512]{1,0:T(8,128)(2,1)S(1)}, bf16[48,512]{1,0:T(8,128)(2,1)S(1)}, u32[]{:S(2)}, u32[]{:S(2)}) collective-permute-start(bf16[48,512]{1,0:T(8,128)(2,1)S(1)} %collective-permute-done.12.refs_3_), channel_id=1, source_target_pairs={{0,1},{1,0},{2,3},{3,2},{4,5},{5,4},{6,7},{7,6},{8,9},{9,8},{10,11... | collective-permute-start | bytes 147464 | tf_op jit(solution)/shard_map/ppermute | solution.py:594

commit v5 on v4

--- a/solution.py
+++ b/solution.py
@@ -175,27 +175,22 @@
     )(traj, inc)
 
 
-def load_kernel(plan, weight, w_out, w_low, w_high, sems):
+def load_kernel(plan, weight, w_out, edges, sems):
     reach, win = weight.shape[1:3]
     half = win // 2
-    copies = []
-    for j in range(plan.rounds):
-        group = plan.sent(j)
-        low = lax.rem(group + reach - 1, reach)
-        high = lax.rem(group + 1, reach)
-        low_at = pl.multiple_of(jnp.where(group == 0, half, win) - SUB, SUB)
-        high_at = pl.multiple_of(jnp.where(group == reach - 2, half, 0), SUB)
-        copies.append(pltpu.make_async_copy(weight.at[0, group], w_out.at[j], sems.at[3 * j]))
+    copies = [
+        pltpu.make_async_copy(weight.at[0, plan.sent(j)], w_out.at[j], sems.at[j])
+        for j in range(plan.rounds)
+    ]
+    parts = ((reach - 1, half - SUB, 2 * SUB), (reach - 2, win - SUB, SUB), (0, 0, SUB))
+    at = 0
+    for part, (group, first, size) in enumerate(parts):
         copies.append(
             pltpu.make_async_copy(
-                weight.at[0, low, pl.ds(low_at, SUB)], w_low.at[j], sems.at[1 + 3 * j]
+                weight.at[0, group, pl.ds(first, size)], edges.at[pl.ds(at, size)], sems.at[plan.rounds + part]
             )
         )
-        copies.append(
-            pltpu.make_async_copy(
-                weight.at[0, high, pl.ds(high_at, SUB)], w_high.at[j], sems.at[2 + 3 * j]
-            )
-        )
+        at += size
     for copy in copies:
         copy.start()
     for copy in copies:
@@ -208,13 +203,9 @@
     return pl.pallas_call(
         functools.partial(load_kernel, plan),
         in_specs=[HBM],
-        out_specs=[VMEM] * 3,
-        out_shape=[
-            like(plan.rounds, win, slots),
-            like(plan.rounds, SUB, slots),
-            like(plan.rounds, SUB, slots),
-        ],
-        scratch_shapes=[pltpu.SemaphoreType.DMA((3 * plan.rounds,))],
+        out_specs=[VMEM] * 2,
+        out_shape=[like(plan.rounds, win, slots), like(4 * SUB, slots)],
+        scratch_shapes=[pltpu.SemaphoreType.DMA((plan.rounds + 3,))],
         compiler_params=pltpu.CompilerParams(vmem_limit_bytes=8 << 20),
         cost_estimate=cost(0, 4 * plan.rounds * win * slots),
         name="fetch",
@@ -248,7 +239,7 @@
     )(traj, inc, traj_too, inc_too, ext, ext_too)
 
 
-def forward_kernel(plan, which, scale, tail, counts, rows_in, courant, vertical, offset, w, w_low, w_high, out):
+def forward_kernel(plan, which, scale, tail, counts, rows_in, courant, vertical, offset, w, edges, out):
     reach, rows, cols = plan.reach, rows_in.shape[0], courant.shape[1]
     slots = w.shape[-1]
     contract = (((1,), (1,)), ((), ()))
@@ -281,27 +272,31 @@
     def edge(weights, group):
         base, shift, size = place(counts, group)
         lane = lax.broadcasted_iota(jnp.int32, (SUB, LANE), 1)
-        weights = shifted(weights.astype(jnp.float32), lane, shift, size).astype(jnp.bfloat16)
+        weights = shifted(weights, lane, shift, size).astype(jnp.bfloat16)
         x = rows_in[:, pl.ds(base, slots + LANE)].astype(jnp.bfloat16)
         return scale * lax.dot_general(weights, x, contract, preferred_element_type=jnp.float32)
 
-    e = edge(w_low[which], lax.rem(group + reach - 1, reach))
+    e_rows = edges[...].astype(jnp.float32)
+    low, high = (e_rows[at : at + SUB] for at in (0, SUB))
+    low = jnp.where(group == 0, low, e_rows[2 * SUB : 3 * SUB])
+    high = jnp.where(group == reach - 2, high, e_rows[3 * SUB :])
+    e = edge(low, lax.rem(group + reach - 1, reach))
     out[tail : tail + 2 * HALO, :rows] = e[SUB - 2 * HALO :]
-    e = edge(w_high[which], lax.rem(group + 1, reach))
+    e = edge(high, lax.rem(group + 1, reach))
     out[tail : tail + 2 * HALO, LANE : LANE + rows] = e[: 2 * HALO]
 
 
-def forward(plan, which, counts, rows_in, courant, vertical, offset, w, w_low, w_high, scale, tail):
+def forward(plan, which, counts, rows_in, courant, vertical, offset, w, edges, scale, tail):
     rows = rows_in.shape[0]
     win, slots = w.shape[1:]
     return pl.pallas_call(
         functools.partial(forward_kernel, plan, which, scale, tail),
-        in_specs=[VMEM] * 8,
+        in_specs=[VMEM] * 7,
         out_specs=VMEM,
         out_shape=jax.ShapeDtypeStruct((rows, win), jnp.float32),
         compiler_params=pltpu.CompilerParams(vmem_limit_bytes=8 << 20),
         cost_estimate=cost(2 * rows * win * slots, 4 * rows_in.size),
-    )(counts, rows_in, courant, vertical, offset, w, w_low, w_high)
+    )(counts, rows_in, courant, vertical, offset, w, edges)
 
 
 def collect(plan, unscale, tail, numbers, pieces, acc, low, high, c_low, c_high):
@@ -384,15 +379,16 @@
     rising = jnp.maximum(vertical, 0.0)
     sinking = jnp.maximum(-vertical, 0.0)
     shifts = range(-HALO, HALO + 1)
-    picked = {s: offset == jnp.float32(s) for s in shifts}
+    upwind = {s: jnp.where(offset == jnp.float32(s), courant, 0.0) for s in shifts}
     turned = lambda x, by: x if by % wide == 0 else pltpu.roll(x, by % wide, axis=1)
+    downwind = {s: turned(upwind[s], s) for s in shifts}
     keep = 1.0 - courant - rising - sinking
 
     def tangent_of(delta, loss, below, above):
-        departed = jnp.zeros_like(delta)
+        moved = (keep - loss) * delta
         for s in shifts:
-            departed = jnp.where(picked[s], turned(delta, -s), departed)
-        return (keep - loss) * delta + courant * departed + rising * below + sinking * above
+            moved = moved + upwind[s] * turned(delta, -s)
+        return moved + rising * below + sinking * above
 
     sub = lax.broadcasted_iota(jnp.int32, (SUB, wide), 0)
     has_prev, has_next = plan.has_prev(), plan.has_next()
@@ -438,11 +434,10 @@
         t_below, t_above = beside(tangents, x_tangent[m : m + 1])
         for h in range(2):
             tangent = tangents[h]
-            flux = courant * tangent
-            arrived = jnp.zeros_like(tangent)
+            adjoint = (keep - losses[h]) * tangent
             for s in shifts:
-                arrived = arrived + turned(jnp.where(picked[s], flux, 0.0), s)
-            adjoint = (keep - losses[h]) * tangent + arrived + rising * t_above[h] + sinking * t_below[h]
+                adjoint = adjoint + downwind[s] * turned(tangent, s)
+            adjoint = adjoint + rising * t_above[h] + sinking * t_below[h]
             at = h * main + m * levels
             adj[at : at + levels, :cols] = adjoint[:, :cols]
             adj[at : at + levels, cols:] = adjoint[:, :span]
@@ -557,12 +552,12 @@
     traj_too = lax.ppermute(trajectory, "lev", swap)
     inc_too = lax.ppermute(increment, "lev", swap)
 
-    w, w_low, w_high = load(plan, pltpu.with_memory_space_constraint(remap_weight, pltpu.HBM))
+    w, edges = load(plan, pltpu.with_memory_space_constraint(remap_weight, pltpu.HBM))
     lines = [x.reshape(1, cols) for x in (courant, vertical, offset)]
     rows_in = gather(plan, traj_own, inc_own, traj_too, inc_too, ext, ext_too, rows, cols + slots)
     pieces, message_0 = [], None
     for j, route in enumerate(routes):
-        message = forward(plan, j, counts, rows_in, *lines, w, w_low, w_high, scale, tail)
+        message = forward(plan, j, counts, rows_in, *lines, w, edges, scale, tail)
         message = message.astype(jnp.float16)
         message_0 = message_0 if j else message
         pieces.append(lax.ppermute(message, both, route))

time: 42.3 us -> 42.1 us (level)
  the two profiles are of different devices: /device:TPU:1 before, /device:TPU:0 now
where the time goes in v5:
time: 42.1 us; the launch traced here: 41.9 us
  starting transfers between devices  19.1 us (45%)
  waiting for transfers between devices  12.4 us (29%)
  Pallas kernels  9.16 us (22%)
  between operations  0.94 us (2%)
    ppermute x4, starting transfers between devices, step(): pieces.append(lax.ppermute(message, both, route))  7.95 us
    ppermute x4, starting transfers between devices, step(): returned.append(lax.ppermute(window, both, [(b, a) for a, b in route]))  7.81 us
    ppermute x4, waiting for transfers between devices, step(): pieces.append(lax.ppermute(message, both, route))  4.7 us
    ppermute x1, waiting for transfers between devices, step(): ext_too = lax.ppermute(border, 'lev', far)  4.46 us
    ppermute x4, waiting for transfers between devices, step(): returned.append(lax.ppermute(window, both, [(b, a) for a, b in route]))  2.33 us
    pallas_call x4, Pallas kernels, forward(): pl.pallas_call(functools.partial(forward_kernel, plan, which, scale, tail...  2.3 us
    pallas_call x2, Pallas kernels, backward(): pl.pallas_call(functools.partial(backward_kernel, plan, int(last), number...  1.82 us
    pallas_call x1, Pallas kernels, load(): pl.pallas_call(functools.partial(load_kernel, plan), in_specs=[HBM], out_...  1.6 us
  transfers between devices with their start and end apart: 20, of which 8 were waited for; matrix products, arithmetic and copies ran while one was open for 0% of the time, Pallas kernels for 12%

profile of v5, /device:TPU:0, one launch (start us, length us, event | category | flops | bytes accessed | tf_op | source)
XLA Modules:
  0.0 41.9 jit_solution(15112506303959306297)
XLA Ops:
  0.6 0.6 %collective-permute-start = (bf16[3,8,2048]{2,1,0:T(8,128)(2,1)}, bf16[3,8,2048]{2,1,0:T(8,128)(2,1)S(1)}, u32[]{:S(2)}, u32[]{:S(2)}) collective-permute-start(bf16[3,8,2048]{2,1,0:T(8,128)(2,1)} %traj.1), channel_id=1, source_target_pairs={{0,1},{1,0},{2,3},{3,2},{4,5},{5,4},{6,7},{7,6},{8,9},{9,8},{10,11... | collective-permute-start | bytes 294920 | tf_op jit(solution)/shard_map/ppermute | solution.py:552
  1.3 1.1 %border.1 = (bf16[3,8,2048]{2,1,0:T(8,128)(2,1)S(1)}, bf16[3,8,2048]{2,1,0:T(8,128)(2,1)S(1)}, bf16[8,2304]{1,0:T(8,128)(2,1)S(1)}) custom-call(bf16[3,8,2048]{2,1,0:T(8,128)(2,1)} %traj.1, bf16[3,8,2048]{2,1,0:T(8,128)(2,1)} %inc.1), custom_call_target="tpu_custom_call" | custom-call | bytes 393216 | tf_op jit(solution)/shard_map/border/pallas_call | solution.py:166
  2.4 0.8 %collective-permute-start.2 = (bf16[8,2304]{1,0:T(8,128)(2,1)S(1)}, bf16[8,2304]{1,0:T(8,128)(2,1)S(1)}, u32[]{:S(2)}, u32[]{:S(2)}) collective-permute-start(bf16[8,2304]{1,0:T(8,128)(2,1)S(1)} %get-tuple-element.16), channel_id=1, source_target_pairs={{1,2},{2,1},{5,6},{6,5},{9,10},{10,9},{13,14},{14,13},{17,18},{18,... | collective-permute-start | bytes 110600 | tf_op jit(solution)/shard_map/ppermute | solution.py:549
  3.2 1.3 %collective-permute-start.3 = (bf16[8,2304]{1,0:T(8,128)(2,1)S(1)}, bf16[8,2304]{1,0:T(8,128)(2,1)S(1)}, u32[]{:S(2)}, u32[]{:S(2)}) collective-permute-start(bf16[8,2304]{1,0:T(8,128)(2,1)S(1)} %get-tuple-element.16), channel_id=1, source_target_pairs={{1,3},{2,0},{5,7},{6,4},{9,11},{10,8},{13,15},{14,12},{17,19},{18,... | collective-permute-start | bytes 110600 | tf_op jit(solution)/shard_map/ppermute | solution.py:550
  4.5 1.6 %fetch.1 = (bf16[4,512,512]{2,1,0:T(8,128)(2,1)S(1)}, bf16[32,512]{1,0:T(8,128)(2,1)S(1)}) custom-call(bf16[1,8,512,512]{3,2,1,0:T(8,128)(2,1)} %weight.5), custom_call_target="tpu_custom_call" | custom-call | bytes 4194304 | tf_op jit(solution)/shard_map/fetch/pallas_call | solution.py:203
  6.1 4.5 %collective-permute-done.3.ext_too = bf16[8,2304]{1,0:T(8,128)(2,1)S(1)} collective-permute-done((bf16[8,2304]{1,0:T(8,128)(2,1)S(1)}, bf16[8,2304]{1,0:T(8,128)(2,1)S(1)}, u32[]{:S(2)}, u32[]{:S(2)}) %collective-permute-start.3) | collective-permute-done | bytes 36896 | tf_op jit(solution)/shard_map/ppermute | solution.py:550
  10.6 0.1 gather.1.rows_in
  10.7 0.6 %shard_map.95 = f32[112,512]{1,0:T(8,128)S(1)} custom-call(s32[1,8]{1,0:T(1,128)S(1)} %copy-done.4, f32[112,2560]{1,0:T(8,128)S(1)} %gather.1.rows_in, f32[1,2048]{1,0:T(1,128)S(1)} %bitcast.4, f32[1,2048]{1,0:T(1,128)S(1)} %bitcast.9, s32[1,2048]{1,0:T(1,128)S(1)} %bitcast.14, bf16[4,512,512]{2,1,0:T(8,128)(2,1)S(1)} %get-tuple-element.17.w, ...), custom_call_target="tpu_custom_call" | custom-call | flops 58720256 | bytes 1146880 | tf_op jit(solution)/shard_map/pallas_call | solution.py:292
  11.3 0.6 %shard_map.96 = f32[112,512]{1,0:T(8,128)S(1)} custom-call(s32[1,8]{1,0:T(1,128)S(1)} %copy-done.4, f32[112,2560]{1,0:T(8,128)S(1)} %gather.1.rows_in, f32[1,2048]{1,0:T(1,128)S(1)} %bitcast.5, f32[1,2048]{1,0:T(1,128)S(1)} %bitcast.10, s32[1,2048]{1,0:T(1,128)S(1)} %bitcast.15, bf16[4,512,512]{2,1,0:T(8,128)(2,1)S(1)} %get-tuple-element.17.w, ...), custom_call_target="tpu_custom_call" | custom-call | flops 58720256 | bytes 1146880 | tf_op jit(solution)/shard_map/pallas_call | solution.py:292
  11.8 0.6 %shard_map.97 = f32[112,512]{1,0:T(8,128)S(1)} custom-call(s32[1,8]{1,0:T(1,128)S(1)} %copy-done.4, f32[112,2560]{1,0:T(8,128)S(1)} %gather.1.rows_in, f32[1,2048]{1,0:T(1,128)S(1)} %bitcast.6, f32[1,2048]{1,0:T(1,128)S(1)} %bitcast.11, s32[1,2048]{1,0:T(1,128)S(1)} %bitcast.16, bf16[4,512,512]{2,1,0:T(8,128)(2,1)S(1)} %get-tuple-element.17.w, ...), custom_call_target="tpu_custom_call" | custom-call | flops 58720256 | bytes 1146880 | tf_op jit(solution)/shard_map/pallas_call | solution.py:292
  12.5 3.8 %collective-permute-start.4 = (f16[112,512]{1,0:T(8,128)(2,1)S(1)}, f16[112,512]{1,0:T(8,128)(2,1)S(1)}, u32[]{:S(2)}, u32[]{:S(2)}) collective-permute-start(f16[112,512]{1,0:T(8,128)(2,1)S(1)} %convert_element_type.36), channel_id=1, source_target_pairs={{0,20},{1,17},{2,22},{3,19},{4,16},{5,21},{6,18},{7,23},{8,28},{9,... | collective-permute-start | bytes 344072 | tf_op jit(solution)/shard_map/ppermute | solution.py:563
  16.3 1.6 %collective-permute-start.5 = (f16[112,512]{1,0:T(8,128)(2,1)S(1)}, f16[112,512]{1,0:T(8,128)(2,1)S(1)}, u32[]{:S(2)}, u32[]{:S(2)}) collective-permute-start(f16[112,512]{1,0:T(8,128)(2,1)S(1)} %convert_element_type.38), channel_id=1, source_target_pairs={{0,8},{1,13},{2,10},{3,15},{4,12},{5,9},{6,14},{7,11},{8,0},{9,5},... | collective-permute-start | bytes 344072 | tf_op jit(solution)/shard_map/ppermute | solution.py:563
  17.9 0.3 collective-permute-start.6
  18.2 0.6 %shard_map.98 = f32[112,512]{1,0:T(8,128)S(1)} custom-call(s32[1,8]{1,0:T(1,128)S(1)} %copy-done.4, f32[112,2560]{1,0:T(8,128)S(1)} %gather.1.rows_in, f32[1,2048]{1,0:T(1,128)S(1)} %bitcast.7, f32[1,2048]{1,0:T(1,128)S(1)} %bitcast.12, s32[1,2048]{1,0:T(1,128)S(1)} %bitcast.17, bf16[4,512,512]{2,1,0:T(8,128)(2,1)S(1)} %get-tuple-element.17.w, ...), custom_call_target="tpu_custom_call" | custom-call | flops 58720256 | bytes 1146880 | tf_op jit(solution)/shard_map/pallas_call | solution.py:292
  18.9 2.2 %collective-permute-start.7 = (f16[112,512]{1,0:T(8,128)(2,1)S(1)}, f16[112,512]{1,0:T(8,128)(2,1)S(1)}, u32[]{:S(2)}, u32[]{:S(2)}) collective-permute-start(f16[112,512]{1,0:T(8,128)(2,1)S(1)} %convert_element_type.42), channel_id=1, source_target_pairs={{0,4},{1,1},{2,6},{3,3},{4,0},{5,5},{6,2},{7,7},{8,12},{9,9},{10,1... | collective-permute-start | bytes 344072 | tf_op jit(solution)/shard_map/ppermute | solution.py:563
  21.1 1.4 %collective-permute-done.4 = f16[112,512]{1,0:T(8,128)(2,1)S(1)} collective-permute-done((f16[112,512]{1,0:T(8,128)(2,1)S(1)}, f16[112,512]{1,0:T(8,128)(2,1)S(1)}, u32[]{:S(2)}, u32[]{:S(2)}) %collective-permute-start.4) | collective-permute-done | bytes 114720 | tf_op jit(solution)/shard_map/ppermute | solution.py:563
  22.5 0.7 %collective-permute-done.5 = f16[112,512]{1,0:T(8,128)(2,1)S(1)} collective-permute-done((f16[112,512]{1,0:T(8,128)(2,1)S(1)}, f16[112,512]{1,0:T(8,128)(2,1)S(1)}, u32[]{:S(2)}, u32[]{:S(2)}) %collective-permute-start.5) | collective-permute-done | bytes 114720 | tf_op jit(solution)/shard_map/ppermute | solution.py:563
  23.2 1.4 %collective-permute-done.6 = f16[112,512]{1,0:T(8,128)(2,1)S(1)} collective-permute-done((f16[112,512]{1,0:T(8,128)(2,1)S(1)}, f16[112,512]{1,0:T(8,128)(2,1)S(1)}, u32[]{:S(2)}, u32[]{:S(2)}) %collective-permute-start.6) | collective-permute-done | bytes 114720 | tf_op jit(solution)/shard_map/ppermute | solution.py:563
  24.6 1.2 %collective-permute-done.7 = f16[112,512]{1,0:T(8,128)(2,1)S(1)} collective-permute-done((f16[112,512]{1,0:T(8,128)(2,1)S(1)}, f16[112,512]{1,0:T(8,128)(2,1)S(1)}, u32[]{:S(2)}, u32[]{:S(2)}) %collective-permute-start.7) | collective-permute-done | bytes 114720 | tf_op jit(solution)/shard_map/ppermute | solution.py:563
  26.0 0.3 assemble.1
  26.3 0.8 %collective-permute-done.11 = f16[112,512]{1,0:T(8,128)(2,1)S(1)} collective-permute-done((f16[112,512]{1,0:T(8,128)(2,1)S(1)}, f16[112,512]{1,0:T(8,128)(2,1)S(1)}, u32[]{:S(2)}, u32[]{:S(2)}) %collective-permute-start.11) | collective-permute-done | bytes 114720 | tf_op jit(solution)/shard_map/ppermute | solution.py:575
  27.1 1.3 %stencil.1 = (f32[48,2048]{1,0:T(8,128)S(1)}, bf16[48,512]{1,0:T(8,128)(2,1)S(1)}, bf16[48,512]{1,0:T(8,128)(2,1)S(1)}, bf16[48,512]{1,0:T(8,128)(2,1)S(1)}, bf16[48,512]{1,0:T(8,128)(2,1)S(1)}) custom-call(f32[1,3]{1,0:T(1,128)S(1)} %bitcast.19, f32[112,2176]{1,0:T(8,128)S(1)} %get-tuple-element.19.acc_in, f32[32,128]{1,0:T(8,128)S(1)} %get-tuple-element.20.side, ...), custom_call_target="tpu_custom_call" | custom-call | flops 22937600 | bytes 1835008 | tf_op jit(solution)/shard_map/stencil/pallas_call | solution.py:454
  28.5 3.8 %collective-permute-start.14 = (bf16[48,512]{1,0:T(8,128)(2,1)S(1)}, bf16[48,512]{1,0:T(8,128)(2,1)S(1)}, u32[]{:S(2)}, u32[]{:S(2)}) collective-permute-start(bf16[48,512]{1,0:T(8,128)(2,1)S(1)} %get-tuple-element.23), channel_id=1, source_target_pairs={{20,0},{17,1},{22,2},{19,3},{16,4},{21,5},{18,6},{23,7},{28,8},{25... | collective-permute-start | bytes 147464 | tf_op jit(solution)/shard_map/ppermute | solution.py:587
  32.3 0.6 %collective-permute-start.15 = (bf16[48,512]{1,0:T(8,128)(2,1)S(1)}, bf16[48,512]{1,0:T(8,128)(2,1)S(1)}, u32[]{:S(2)}, u32[]{:S(2)}) collective-permute-start(bf16[48,512]{1,0:T(8,128)(2,1)S(1)} %get-tuple-element.24), channel_id=1, source_target_pairs={{8,0},{13,1},{10,2},{15,3},{12,4},{9,5},{14,6},{11,7},{0,8},{5,9},... | collective-permute-start | bytes 147464 | tf_op jit(solution)/shard_map/ppermute | solution.py:587
  32.9 0.4 collective-permute-start.16
  33.3 3.0 %collective-permute-start.12 = (bf16[48,512]{1,0:T(8,128)(2,1)S(1)}, bf16[48,512]{1,0:T(8,128)(2,1)S(1)}, u32[]{:S(2)}, u32[]{:S(2)}) collective-permute-start(bf16[48,512]{1,0:T(8,128)(2,1)S(1)} %get-tuple-element.22), channel_id=1, source_target_pairs={{4,0},{1,1},{6,2},{3,3},{0,4},{5,5},{2,6},{7,7},{12,8},{9,9},{14,1... | collective-permute-start | bytes 147464 | tf_op jit(solution)/shard_map/ppermute | solution.py:587
  36.4 0.5 %collective-permute-start.18 = (bf16[48,512]{1,0:T(8,128)(2,1)S(1)}, bf16[48,512]{1,0:T(8,128)(2,1)S(1)}, u32[]{:S(2)}, u32[]{:S(2)}) collective-permute-start(bf16[48,512]{1,0:T(8,128)(2,1)S(1)} %collective-permute-done.15.refs_1_), channel_id=1, source_target_pairs={{0,1},{1,0},{2,3},{3,2},{4,5},{5,4},{6,7},{7,6},{8,9},{9,8},{10,11... | collective-permute-start | bytes 147464 | tf_op jit(solution)/shard_map/ppermute | solution.py:589
  36.9 1.9 %collective-permute-done.16.refs_2_ = bf16[48,512]{1,0:T(8,128)(2,1)S(1)} collective-permute-done((bf16[48,512]{1,0:T(8,128)(2,1)S(1)}, bf16[48,512]{1,0:T(8,128)(2,1)S(1)}, u32[]{:S(2)}, u32[]{:S(2)}) %collective-permute-start.16) | collective-permute-done | bytes 49184 | tf_op jit(solution)/shard_map/ppermute | solution.py:587
  38.8 0.4 %collective-permute-done.12.refs_3_ = bf16[48,512]{1,0:T(8,128)(2,1)S(1)} collective-permute-done((bf16[48,512]{1,0:T(8,128)(2,1)S(1)}, bf16[48,512]{1,0:T(8,128)(2,1)S(1)}, u32[]{:S(2)}, u32[]{:S(2)}) %collective-permute-start.12) | collective-permute-done | bytes 49184 | tf_op jit(solution)/shard_map/ppermute | solution.py:587
  39.3 0.7 %emit.1 = f32[3,8,2048]{2,1,0:T(8,128)} custom-call(f32[48,2048]{1,0:T(8,128)S(1)} %get-tuple-element.21.both), custom_call_target="tpu_custom_call" | custom-call | bytes 393216 | tf_op jit(solution)/shard_map/emit/pallas_call | solution.py:480
  40.0 0.8 %back.1.refs_1_ = f32[24,2560]{1,0:T(8,128)S(1)} custom-call(s32[1,8]{1,0:T(1,128)S(1)} %copy-done.4, bf16[1,8,512,512]{3,2,1,0:T(8,128)(2,1)S(1)} %copy-done, bf16[48,512]{1,0:T(8,128)(2,1)S(1)} %collective-permute-done.14.refs_0_, bf16[48,512]{1,0:T(8,128)(2,1)S(1)} %collective-permute-done.15.refs_1_, ...), custom_call_target="tpu_custom_call" | custom-call | flops 88080384 | bytes 2097152 | tf_op jit(solution)/shard_map/back/pallas_call | solution.py:519
  40.9 1.0 %back_last.1 = f32[3,8,2048]{2,1,0:T(8,128)} custom-call(s32[1,8]{1,0:T(1,128)S(1)} %copy-done.4, bf16[1,8,512,512]{3,2,1,0:T(8,128)(2,1)S(1)} %copy-done, bf16[48,512]{1,0:T(8,128)(2,1)S(1)} %collective-permute-done.13.refs_0_, f32[24,2560]{1,0:T(8,128)S(1)} %back.1.refs_1_), custom_call_target="tpu_custom_call" | custom-call | flops 12582912 | bytes 2097152 | tf_op jit(solution)/shard_map/back_last/pallas_call | solution.py:519
  (44 shorter events, 0.5 us)
Async XLA Ops:
  0.6 9.9 %collective-permute-start = (bf16[3,8,2048]{2,1,0:T(8,128)(2,1)}, bf16[3,8,2048]{2,1,0:T(8,128)(2,1)S(1)}, u32[]{:S(2)}, u32[]{:S(2)}) collective-permute-start(bf16[3,8,2048]{2,1,0:T(8,128)(2,1)} %traj.1), channel_id=1, source_target_pairs={{0,1},{1,0},{2,3},{3,2},{4,5},{5,4},{6,7},{7,6},{8,9},{9,8},{10,11... | collective-permute-start | bytes 294920 | tf_op jit(solution)/shard_map/ppermute | solution.py:552
  1.2 9.4 %collective-permute-start.1 = (bf16[3,8,2048]{2,1,0:T(8,128)(2,1)}, bf16[3,8,2048]{2,1,0:T(8,128)(2,1)S(1)}, u32[]{:S(2)}, u32[]{:S(2)}) collective-permute-start(bf16[3,8,2048]{2,1,0:T(8,128)(2,1)} %inc.1), channel_id=1, source_target_pairs={{0,1},{1,0},{2,3},{3,2},{4,5},{5,4},{6,7},{7,6},{8,9},{9,8},{10,11... | collective-permute-start | bytes 294920 | tf_op jit(solution)/shard_map/ppermute | solution.py:553
  2.3 8.3 %copy-start.1 = (f32[2048]{0:T(1024)S(1)}, f32[2048]{0:T(1024)}, u32[]{:S(2)}) copy-start(f32[2048]{0:T(1024)} %param.13) | copy-start | bytes 24580
  2.3 8.3 %copy-start.2 = (f32[2048]{0:T(1024)S(1)}, f32[2048]{0:T(1024)}, u32[]{:S(2)}) copy-start(f32[2048]{0:T(1024)} %param.14) | copy-start | bytes 24580
  2.4 8.3 %copy-start.3 = (s32[2048]{0:T(1024)S(1)}, s32[2048]{0:T(1024)}, u32[]{:S(2)}) copy-start(s32[2048]{0:T(1024)} %param.15) | copy-start | bytes 24580
  2.4 8.3 %copy-start.4 = (s32[1,8]{1,0:T(1,128)S(1)}, s32[1,8]{1,0:T(1,128)}, u32[]{:S(2)}) copy-start(s32[1,8]{1,0:T(1,128)} %counts.11) | copy-start | bytes 100
  2.4 3.7 %collective-permute-start.2 = (bf16[8,2304]{1,0:T(8,128)(2,1)S(1)}, bf16[8,2304]{1,0:T(8,128)(2,1)S(1)}, u32[]{:S(2)}, u32[]{:S(2)}) collective-permute-start(bf16[8,2304]{1,0:T(8,128)(2,1)S(1)} %get-tuple-element.16), channel_id=1, source_target_pairs={{1,2},{2,1},{5,6},{6,5},{9,10},{10,9},{13,14},{14,13},{17,18},{18,... | collective-permute-start | bytes 110600 | tf_op jit(solution)/shard_map/ppermute | solution.py:549
  3.2 7.4 %collective-permute-start.3 = (bf16[8,2304]{1,0:T(8,128)(2,1)S(1)}, bf16[8,2304]{1,0:T(8,128)(2,1)S(1)}, u32[]{:S(2)}, u32[]{:S(2)}) collective-permute-start(bf16[8,2304]{1,0:T(8,128)(2,1)S(1)} %get-tuple-element.16), channel_id=1, source_target_pairs={{1,3},{2,0},{5,7},{6,4},{9,11},{10,8},{13,15},{14,12},{17,19},{18,... | collective-permute-start | bytes 110600 | tf_op jit(solution)/shard_map/ppermute | solution.py:550
  12.5 10.0 %collective-permute-start.4 = (f16[112,512]{1,0:T(8,128)(2,1)S(1)}, f16[112,512]{1,0:T(8,128)(2,1)S(1)}, u32[]{:S(2)}, u32[]{:S(2)}) collective-permute-start(f16[112,512]{1,0:T(8,128)(2,1)S(1)} %convert_element_type.36), channel_id=1, source_target_pairs={{0,20},{1,17},{2,22},{3,19},{4,16},{5,21},{6,18},{7,23},{8,28},{9,... | collective-permute-start | bytes 344072 | tf_op jit(solution)/shard_map/ppermute | solution.py:563
  16.3 6.9 %collective-permute-start.5 = (f16[112,512]{1,0:T(8,128)(2,1)S(1)}, f16[112,512]{1,0:T(8,128)(2,1)S(1)}, u32[]{:S(2)}, u32[]{:S(2)}) collective-permute-start(f16[112,512]{1,0:T(8,128)(2,1)S(1)} %convert_element_type.38), channel_id=1, source_target_pairs={{0,8},{1,13},{2,10},{3,15},{4,12},{5,9},{6,14},{7,11},{8,0},{9,5},... | collective-permute-start | bytes 344072 | tf_op jit(solution)/shard_map/ppermute | solution.py:563
  17.9 6.7 %collective-permute-start.6 = (f16[112,512]{1,0:T(8,128)(2,1)S(1)}, f16[112,512]{1,0:T(8,128)(2,1)S(1)}, u32[]{:S(2)}, u32[]{:S(2)}) collective-permute-start(f16[112,512]{1,0:T(8,128)(2,1)S(1)} %convert_element_type.40), channel_id=1, source_target_pairs={{0,24},{1,29},{2,26},{3,31},{4,28},{5,25},{6,30},{7,27},{8,16},{9,... | collective-permute-start | bytes 344072 | tf_op jit(solution)/shard_map/ppermute | solution.py:563
  18.8 8.3 %copy-start.5 = (f32[3]{0:T(128)S(1)}, f32[3]{0:T(128)}, u32[]{:S(2)}) copy-start(f32[3]{0:T(128)} %param.12) | copy-start | bytes 40
  18.9 6.9 %collective-permute-start.7 = (f16[112,512]{1,0:T(8,128)(2,1)S(1)}, f16[112,512]{1,0:T(8,128)(2,1)S(1)}, u32[]{:S(2)}, u32[]{:S(2)}) collective-permute-start(f16[112,512]{1,0:T(8,128)(2,1)S(1)} %convert_element_type.42), channel_id=1, source_target_pairs={{0,4},{1,1},{2,6},{3,3},{4,0},{5,5},{6,2},{7,7},{8,12},{9,9},{10,1... | collective-permute-start | bytes 344072 | tf_op jit(solution)/shard_map/ppermute | solution.py:563
  22.5 3.4 %collective-permute-start.8 = (f16[112,512]{1,0:T(8,128)(2,1)S(1)}, f16[112,512]{1,0:T(8,128)(2,1)S(1)}, u32[]{:S(2)}, u32[]{:S(2)}) collective-permute-start(f16[112,512]{1,0:T(8,128)(2,1)S(1)} %collective-permute-done.4), channel_id=1, source_target_pairs={{0,1},{1,0},{2,3},{3,2},{4,5},{5,4},{6,7},{7,6},{8,9},{9,8},{10,11... | collective-permute-start | bytes 344072 | tf_op jit(solution)/shard_map/ppermute | solution.py:575
  23.2 2.7 %collective-permute-start.9 = (f16[112,512]{1,0:T(8,128)(2,1)S(1)}, f16[112,512]{1,0:T(8,128)(2,1)S(1)}, u32[]{:S(2)}, u32[]{:S(2)}) collective-permute-start(f16[112,512]{1,0:T(8,128)(2,1)S(1)} %collective-permute-done.5), channel_id=1, source_target_pairs={{0,1},{1,0},{2,3},{3,2},{4,5},{5,4},{6,7},{7,6},{8,9},{9,8},{10,11... | collective-permute-start | bytes 344072 | tf_op jit(solution)/shard_map/ppermute | solution.py:575
  24.6 1.4 %collective-permute-start.10 = (f16[112,512]{1,0:T(8,128)(2,1)S(1)}, f16[112,512]{1,0:T(8,128)(2,1)S(1)}, u32[]{:S(2)}, u32[]{:S(2)}) collective-permute-start(f16[112,512]{1,0:T(8,128)(2,1)S(1)} %collective-permute-done.6), channel_id=1, source_target_pairs={{0,1},{1,0},{2,3},{3,2},{4,5},{5,4},{6,7},{7,6},{8,9},{9,8},{10,11... | collective-permute-start | bytes 344072 | tf_op jit(solution)/shard_map/ppermute | solution.py:575
  25.8 1.3 %collective-permute-start.11 = (f16[112,512]{1,0:T(8,128)(2,1)S(1)}, f16[112,512]{1,0:T(8,128)(2,1)S(1)}, u32[]{:S(2)}, u32[]{:S(2)}) collective-permute-start(f16[112,512]{1,0:T(8,128)(2,1)S(1)} %collective-permute-done.7), channel_id=1, source_target_pairs={{0,1},{1,0},{2,3},{3,2},{4,5},{5,4},{6,7},{7,6},{8,9},{9,8},{10,11... | collective-permute-start | bytes 344072 | tf_op jit(solution)/shard_map/ppermute | solution.py:575
  25.9 14.1 %copy-start = (bf16[1,8,512,512]{3,2,1,0:T(8,128)(2,1)S(1)}, bf16[1,8,512,512]{3,2,1,0:T(8,128)(2,1)}, u32[]{:S(2)}) copy-start(bf16[1,8,512,512]{3,2,1,0:T(8,128)(2,1)} %weight.5) | copy-start | bytes 12582916
  28.5 7.8 %collective-permute-start.14 = (bf16[48,512]{1,0:T(8,128)(2,1)S(1)}, bf16[48,512]{1,0:T(8,128)(2,1)S(1)}, u32[]{:S(2)}, u32[]{:S(2)}) collective-permute-start(bf16[48,512]{1,0:T(8,128)(2,1)S(1)} %get-tuple-element.23), channel_id=1, source_target_pairs={{20,0},{17,1},{22,2},{19,3},{16,4},{21,5},{18,6},{23,7},{28,8},{25... | collective-permute-start | bytes 147464 | tf_op jit(solution)/shard_map/ppermute | solution.py:587
  32.3 4.1 %collective-permute-start.15 = (bf16[48,512]{1,0:T(8,128)(2,1)S(1)}, bf16[48,512]{1,0:T(8,128)(2,1)S(1)}, u32[]{:S(2)}, u32[]{:S(2)}) collective-permute-start(bf16[48,512]{1,0:T(8,128)(2,1)S(1)} %get-tuple-element.24), channel_id=1, source_target_pairs={{8,0},{13,1},{10,2},{15,3},{12,4},{9,5},{14,6},{11,7},{0,8},{5,9},... | collective-permute-start | bytes 147464 | tf_op jit(solution)/shard_map/ppermute | solution.py:587
  32.9 5.9 %collective-permute-start.16 = (bf16[48,512]{1,0:T(8,128)(2,1)S(1)}, bf16[48,512]{1,0:T(8,128)(2,1)S(1)}, u32[]{:S(2)}, u32[]{:S(2)}) collective-permute-start(bf16[48,512]{1,0:T(8,128)(2,1)S(1)} %get-tuple-element.25), channel_id=1, source_target_pairs={{24,0},{29,1},{26,2},{31,3},{28,4},{25,5},{30,6},{27,7},{16,8},{21... | collective-permute-start | bytes 147464 | tf_op jit(solution)/shard_map/ppermute | solution.py:587
  33.3 6.0 %collective-permute-start.12 = (bf16[48,512]{1,0:T(8,128)(2,1)S(1)}, bf16[48,512]{1,0:T(8,128)(2,1)S(1)}, u32[]{:S(2)}, u32[]{:S(2)}) collective-permute-start(bf16[48,512]{1,0:T(8,128)(2,1)S(1)} %get-tuple-element.22), channel_id=1, source_target_pairs={{4,0},{1,1},{6,2},{3,3},{0,4},{5,5},{2,6},{7,7},{12,8},{9,9},{14,1... | collective-permute-start | bytes 147464 | tf_op jit(solution)/shard_map/ppermute | solution.py:587
  36.3 3.7 %collective-permute-start.17 = (bf16[48,512]{1,0:T(8,128)(2,1)S(1)}, bf16[48,512]{1,0:T(8,128)(2,1)S(1)}, u32[]{:S(2)}, u32[]{:S(2)}) collective-permute-start(bf16[48,512]{1,0:T(8,128)(2,1)S(1)} %collective-permute-done.14.refs_0_), channel_id=1, source_target_pairs={{0,1},{1,0},{2,3},{3,2},{4,5},{5,4},{6,7},{7,6},{8,9},{9,8},{10,11... | collective-permute-start | bytes 147464 | tf_op jit(solution)/shard_map/ppermute | solution.py:589
  36.4 3.6 %collective-permute-start.18 = (bf16[48,512]{1,0:T(8,128)(2,1)S(1)}, bf16[48,512]{1,0:T(8,128)(2,1)S(1)}, u32[]{:S(2)}, u32[]{:S(2)}) collective-permute-start(bf16[48,512]{1,0:T(8,128)(2,1)S(1)} %collective-permute-done.15.refs_1_), channel_id=1, source_target_pairs={{0,1},{1,0},{2,3},{3,2},{4,5},{5,4},{6,7},{7,6},{8,9},{9,8},{10,11... | collective-permute-start | bytes 147464 | tf_op jit(solution)/shard_map/ppermute | solution.py:589
  38.8 1.2 %collective-permute-start.19 = (bf16[48,512]{1,0:T(8,128)(2,1)S(1)}, bf16[48,512]{1,0:T(8,128)(2,1)S(1)}, u32[]{:S(2)}, u32[]{:S(2)}) collective-permute-start(bf16[48,512]{1,0:T(8,128)(2,1)S(1)} %collective-permute-done.16.refs_2_), channel_id=1, source_target_pairs={{0,1},{1,0},{2,3},{3,2},{4,5},{5,4},{6,7},{7,6},{8,9},{9,8},{10,11... | collective-permute-start | bytes 147464 | tf_op jit(solution)/shard_map/ppermute | solution.py:589
  39.2 1.6 %collective-permute-start.13 = (bf16[48,512]{1,0:T(8,128)(2,1)S(1)}, bf16[48,512]{1,0:T(8,128)(2,1)S(1)}, u32[]{:S(2)}, u32[]{:S(2)}) collective-permute-start(bf16[48,512]{1,0:T(8,128)(2,1)S(1)} %collective-permute-done.12.refs_3_), channel_id=1, source_target_pairs={{0,1},{1,0},{2,3},{3,2},{4,5},{5,4},{6,7},{7,6},{8,9},{9,8},{10,11... | collective-permute-start | bytes 147464 | tf_op jit(solution)/shard_map/ppermute | solution.py:589

commit v6 on v5

--- a/solution.py
+++ b/solution.py
@@ -121,21 +121,21 @@
         return self.core() if k < self.rounds else 1 - self.core()
 
 
-def border_kernel(plan, traj, inc, traj_out, inc_out, border, lines, sems):
+def border_kernel(plan, traj, inc, fields, border, lines, sems):
+    tracers, levels, cols = traj.shape
     copies = [
-        pltpu.make_async_copy(traj, traj_out, sems.at[0]),
-        pltpu.make_async_copy(inc, inc_out, sems.at[1]),
+        pltpu.make_async_copy(traj, fields.at[pl.ds(0, tracers)], sems.at[0]),
+        pltpu.make_async_copy(inc, fields.at[pl.ds(tracers, tracers)], sems.at[1]),
     ]
     for copy in copies:
         copy.start()
     for copy in copies:
         copy.wait()
-    tracers, levels, cols = traj_out.shape
     lower = plan.core() == 1
     row = 0
-    for ref, depth in ((traj_out, 0), (inc_out, 0), (inc_out, 1)):
+    for start, depth in ((0, 0), (tracers, 0), (tracers, 1)):
         for m in range(tracers):
-            x = ref[m].astype(jnp.float32)
+            x = fields[start + m].astype(jnp.float32)
             low, high = levels - 1 - depth, depth
             line = jnp.where(lower, x[low : low + 1], x[high : high + 1])
             if row < SUB:
@@ -160,14 +160,14 @@
 
 
 def fetch_border(plan, traj, inc):
-    tracers, _, cols = traj.shape
+    tracers, levels, cols = traj.shape
     like = lambda *shape: jax.ShapeDtypeStruct(shape, traj.dtype)
     wide = cols + max(0, EDGE * tracers - SUB) * (cols // SUB)
     return pl.pallas_call(
         functools.partial(border_kernel, plan),
         in_specs=[HBM] * 2,
-        out_specs=[VMEM] * 3,
-        out_shape=[like(*traj.shape), like(*inc.shape), like(SUB, wide)],
+        out_specs=[VMEM] * 2,
+        out_shape=[like(2 * tracers, levels, cols), like(SUB, wide)],
         scratch_shapes=[pltpu.VMEM((SUB, wide), jnp.float32), pltpu.SemaphoreType.DMA((2,))],
         compiler_params=pltpu.CompilerParams(vmem_limit_bytes=4 << 20),
         cost_estimate=cost(0, 8 * traj.size),
@@ -212,31 +212,32 @@
     )(weight)
 
 
-def gather_kernel(plan, traj, inc, traj_too, inc_too, ext, ext_too, rows_out):
-    tracers, levels, cols = traj.shape
+def gather_kernel(plan, fields, fields_too, ext, ext_too, rows_out):
+    levels, cols = fields.shape[1:]
+    tracers = fields.shape[0] // 2
     main = tracers * levels
     mine = pl.multiple_of(plan.core() * 2 * main, SUB)
     theirs = pl.multiple_of((1 - plan.core()) * 2 * main, SUB)
     for m in range(tracers):
-        for at, t, i in ((mine, traj, inc), (theirs, traj_too, inc_too)):
-            rows_out[pl.ds(at + m * levels, levels), :cols] = t[m].astype(jnp.float32)
-            rows_out[pl.ds(at + main + m * levels, levels), :cols] = i[m].astype(jnp.float32)
+        for at, both in ((mine, fields), (theirs, fields_too)):
+            rows_out[pl.ds(at + m * levels, levels), :cols] = both[m].astype(jnp.float32)
+            rows_out[pl.ds(at + main + m * levels, levels), :cols] = both[tracers + m].astype(jnp.float32)
     rows_out[:, cols:] = jnp.zeros_like(rows_out[:, cols:])
     rows_out[4 * main :, :cols] = jnp.zeros_like(rows_out[4 * main :, :cols])
     beyond = ext[...].astype(jnp.float32) + ext_too[...].astype(jnp.float32)
     rows_out[4 * main : 4 * main + EDGE * tracers, :cols] = unpacked(beyond, EDGE * tracers, cols)
 
 
-def gather(plan, traj, inc, traj_too, inc_too, ext, ext_too, rows, cols):
+def gather(plan, fields, fields_too, ext, ext_too, rows, cols):
     return pl.pallas_call(
         functools.partial(gather_kernel, plan),
-        in_specs=[VMEM] * 6,
+        in_specs=[VMEM] * 4,
         out_specs=VMEM,
         out_shape=jax.ShapeDtypeStruct((rows, cols), jnp.float32),
         compiler_params=pltpu.CompilerParams(vmem_limit_bytes=8 << 20),
         cost_estimate=cost(0, 6 * rows * cols),
         name="gather",
-    )(traj, inc, traj_too, inc_too, ext, ext_too)
+    )(fields, fields_too, ext, ext_too)
 
 
 def forward_kernel(plan, which, scale, tail, counts, rows_in, courant, vertical, offset, w, edges, out):
@@ -545,16 +546,15 @@
     near = [(v, v + 1 if v % 2 else v - 1) for v in range(slabs)]
     far = [(v, v + 2 if v % 2 else v - 2) for v in range(slabs)]
     near, far = ([(a, b) for a, b in way if 0 <= b < slabs] for way in (near, far))
-    traj_own, inc_own, border = fetch_border(plan, *(pltpu.with_memory_space_constraint(x, pltpu.HBM) for x in (trajectory, increment)))
+    fields, border = fetch_border(plan, *(pltpu.with_memory_space_constraint(x, pltpu.HBM) for x in (trajectory, increment)))
     ext = lax.ppermute(border, "lev", near)
     ext_too = lax.ppermute(border, "lev", far)
 
-    traj_too = lax.ppermute(trajectory, "lev", swap)
-    inc_too = lax.ppermute(increment, "lev", swap)
+    fields_too = lax.ppermute(fields, "lev", swap)
 
     w, edges = load(plan, pltpu.with_memory_space_constraint(remap_weight, pltpu.HBM))
     lines = [x.reshape(1, cols) for x in (courant, vertical, offset)]
-    rows_in = gather(plan, traj_own, inc_own, traj_too, inc_too, ext, ext_too, rows, cols + slots)
+    rows_in = gather(plan, fields, fields_too, ext, ext_too, rows, cols + slots)
     pieces, message_0 = [], None
     for j, route in enumerate(routes):
         message = forward(plan, j, counts, rows_in, *lines, w, edges, scale, tail)

time: 42.1 us -> 41.9 us (level)
  waiting for transfers between devices: 12.4 us -> 11.3 us
  starting transfers between devices: 19.1 us -> 20 us
    ppermute x4, waiting for transfers between devices: 4.7 us -> 4.28 us  [step(): pieces.append(lax.ppermute(message, both, route))]
  transfers between devices with their start and end apart: 20 -> 19, of which waited for: 8 -> 9; matrix products, arithmetic and copies ran while one was open for 0% -> 0% of each run, Pallas kernels for 12% -> 10%
where the time goes in v6:
time: 41.9 us; the launch traced here: 41.6 us
  starting transfers between devices  20 us (48%)
  waiting for transfers between devices  11.3 us (27%)
  Pallas kernels  9.16 us (22%)
  between operations  0.91 us (2%)
    ppermute x4, starting transfers between devices, step(): pieces.append(lax.ppermute(message, both, route))  8.32 us
    ppermute x4, starting transfers between devices, step(): returned.append(lax.ppermute(window, both, [(b, a) for a, b in route]))  7.81 us
    ppermute x4, waiting for transfers between devices, step(): pieces.append(lax.ppermute(message, both, route))  4.28 us
    ppermute x1, waiting for transfers between devices, step(): ext_too = lax.ppermute(border, 'lev', far)  4.07 us
    pallas_call x4, Pallas kernels, forward(): pl.pallas_call(functools.partial(forward_kernel, plan, which, scale, tail...  2.3 us
    ppermute x4, waiting for transfers between devices, step(): returned.append(lax.ppermute(window, both, [(b, a) for a, b in route]))  2.09 us
    pallas_call x2, Pallas kernels, backward(): pl.pallas_call(functools.partial(backward_kernel, plan, int(last), number...  1.82 us
    pallas_call x1, Pallas kernels, load(): pl.pallas_call(functools.partial(load_kernel, plan), in_specs=[HBM], out_...  1.6 us
  transfers between devices with their start and end apart: 19, of which 9 were waited for; matrix products, arithmetic and copies ran while one was open for 0% of the time, Pallas kernels for 10%

profile of v6, /device:TPU:0, one launch (start us, length us, event | category | flops | bytes accessed | tf_op | source)
XLA Modules:
  0.0 41.6 jit_solution(6538118024286656766)
XLA Ops:
  0.6 1.1 %border.1 = (bf16[6,8,2048]{2,1,0:T(8,128)(2,1)S(1)}, bf16[8,2304]{1,0:T(8,128)(2,1)S(1)}) custom-call(bf16[3,8,2048]{2,1,0:T(8,128)(2,1)} %traj.1, bf16[3,8,2048]{2,1,0:T(8,128)(2,1)} %inc.1), custom_call_target="tpu_custom_call" | custom-call | bytes 393216 | tf_op jit(solution)/shard_map/border/pallas_call | solution.py:166
  1.7 0.6 %collective-permute-start = (bf16[6,8,2048]{2,1,0:T(8,128)(2,1)S(1)}, bf16[6,8,2048]{2,1,0:T(8,128)(2,1)S(1)}, u32[]{:S(2)}, u32[]{:S(2)}) collective-permute-start(bf16[6,8,2048]{2,1,0:T(8,128)(2,1)S(1)} %get-tuple-element.13.fields), channel_id=1, source_target_pairs={{0,1},{1,0},{2,3},{3,2},{4,5},{5,4},{6,7},{7,6},{8,9},{9,8},{10,11... | collective-permute-start | bytes 589832 | tf_op jit(solution)/shard_map/ppermute | solution.py:553
  2.3 0.8 %collective-permute-start.1 = (bf16[8,2304]{1,0:T(8,128)(2,1)S(1)}, bf16[8,2304]{1,0:T(8,128)(2,1)S(1)}, u32[]{:S(2)}, u32[]{:S(2)}) collective-permute-start(bf16[8,2304]{1,0:T(8,128)(2,1)S(1)} %get-tuple-element.14), channel_id=1, source_target_pairs={{1,2},{2,1},{5,6},{6,5},{9,10},{10,9},{13,14},{14,13},{17,18},{18,... | collective-permute-start | bytes 110600 | tf_op jit(solution)/shard_map/ppermute | solution.py:550
  3.1 1.3 %collective-permute-start.2 = (bf16[8,2304]{1,0:T(8,128)(2,1)S(1)}, bf16[8,2304]{1,0:T(8,128)(2,1)S(1)}, u32[]{:S(2)}, u32[]{:S(2)}) collective-permute-start(bf16[8,2304]{1,0:T(8,128)(2,1)S(1)} %get-tuple-element.14), channel_id=1, source_target_pairs={{1,3},{2,0},{5,7},{6,4},{9,11},{10,8},{13,15},{14,12},{17,19},{18,... | collective-permute-start | bytes 110600 | tf_op jit(solution)/shard_map/ppermute | solution.py:551
  4.4 1.6 %fetch.1 = (bf16[4,512,512]{2,1,0:T(8,128)(2,1)S(1)}, bf16[32,512]{1,0:T(8,128)(2,1)S(1)}) custom-call(bf16[1,8,512,512]{3,2,1,0:T(8,128)(2,1)} %weight.5), custom_call_target="tpu_custom_call" | custom-call | bytes 4194304 | tf_op jit(solution)/shard_map/fetch/pallas_call | solution.py:203
  6.0 4.1 %collective-permute-done.2.ext_too = bf16[8,2304]{1,0:T(8,128)(2,1)S(1)} collective-permute-done((bf16[8,2304]{1,0:T(8,128)(2,1)S(1)}, bf16[8,2304]{1,0:T(8,128)(2,1)S(1)}, u32[]{:S(2)}, u32[]{:S(2)}) %collective-permute-start.2) | collective-permute-done | bytes 36896 | tf_op jit(solution)/shard_map/ppermute | solution.py:551
  10.2 0.6 %shard_map.95 = f32[112,512]{1,0:T(8,128)S(1)} custom-call(s32[1,8]{1,0:T(1,128)S(1)} %copy-done.4, f32[112,2560]{1,0:T(8,128)S(1)} %gather.1.rows_in, f32[1,2048]{1,0:T(1,128)S(1)} %bitcast.4, f32[1,2048]{1,0:T(1,128)S(1)} %bitcast.9, s32[1,2048]{1,0:T(1,128)S(1)} %bitcast.14, bf16[4,512,512]{2,1,0:T(8,128)(2,1)S(1)} %get-tuple-element.15.w, ...), custom_call_target="tpu_custom_call" | custom-call | flops 58720256 | bytes 1146880 | tf_op jit(solution)/shard_map/pallas_call | solution.py:293
  10.8 0.6 %shard_map.96 = f32[112,512]{1,0:T(8,128)S(1)} custom-call(s32[1,8]{1,0:T(1,128)S(1)} %copy-done.4, f32[112,2560]{1,0:T(8,128)S(1)} %gather.1.rows_in, f32[1,2048]{1,0:T(1,128)S(1)} %bitcast.5, f32[1,2048]{1,0:T(1,128)S(1)} %bitcast.10, s32[1,2048]{1,0:T(1,128)S(1)} %bitcast.15, bf16[4,512,512]{2,1,0:T(8,128)(2,1)S(1)} %get-tuple-element.15.w, ...), custom_call_target="tpu_custom_call" | custom-call | flops 58720256 | bytes 1146880 | tf_op jit(solution)/shard_map/pallas_call | solution.py:293
  11.3 0.6 %shard_map.97 = f32[112,512]{1,0:T(8,128)S(1)} custom-call(s32[1,8]{1,0:T(1,128)S(1)} %copy-done.4, f32[112,2560]{1,0:T(8,128)S(1)} %gather.1.rows_in, f32[1,2048]{1,0:T(1,128)S(1)} %bitcast.6, f32[1,2048]{1,0:T(1,128)S(1)} %bitcast.11, s32[1,2048]{1,0:T(1,128)S(1)} %bitcast.16, bf16[4,512,512]{2,1,0:T(8,128)(2,1)S(1)} %get-tuple-element.15.w, ...), custom_call_target="tpu_custom_call" | custom-call | flops 58720256 | bytes 1146880 | tf_op jit(solution)/shard_map/pallas_call | solution.py:293
  12.0 4.2 %collective-permute-start.3 = (f16[112,512]{1,0:T(8,128)(2,1)S(1)}, f16[112,512]{1,0:T(8,128)(2,1)S(1)}, u32[]{:S(2)}, u32[]{:S(2)}) collective-permute-start(f16[112,512]{1,0:T(8,128)(2,1)S(1)} %convert_element_type.36), channel_id=1, source_target_pairs={{0,20},{1,17},{2,22},{3,19},{4,16},{5,21},{6,18},{7,23},{8,28},{9,... | collective-permute-start | bytes 344072 | tf_op jit(solution)/shard_map/ppermute | solution.py:563
  16.2 1.6 %collective-permute-start.4 = (f16[112,512]{1,0:T(8,128)(2,1)S(1)}, f16[112,512]{1,0:T(8,128)(2,1)S(1)}, u32[]{:S(2)}, u32[]{:S(2)}) collective-permute-start(f16[112,512]{1,0:T(8,128)(2,1)S(1)} %convert_element_type.38), channel_id=1, source_target_pairs={{0,8},{1,13},{2,10},{3,15},{4,12},{5,9},{6,14},{7,11},{8,0},{9,5},... | collective-permute-start | bytes 344072 | tf_op jit(solution)/shard_map/ppermute | solution.py:563
  17.8 0.3 collective-permute-start.5
  18.1 0.6 %shard_map.98 = f32[112,512]{1,0:T(8,128)S(1)} custom-call(s32[1,8]{1,0:T(1,128)S(1)} %copy-done.4, f32[112,2560]{1,0:T(8,128)S(1)} %gather.1.rows_in, f32[1,2048]{1,0:T(1,128)S(1)} %bitcast.7, f32[1,2048]{1,0:T(1,128)S(1)} %bitcast.12, s32[1,2048]{1,0:T(1,128)S(1)} %bitcast.17, bf16[4,512,512]{2,1,0:T(8,128)(2,1)S(1)} %get-tuple-element.15.w, ...), custom_call_target="tpu_custom_call" | custom-call | flops 58720256 | bytes 1146880 | tf_op jit(solution)/shard_map/pallas_call | solution.py:293
  18.7 2.2 %collective-permute-start.6 = (f16[112,512]{1,0:T(8,128)(2,1)S(1)}, f16[112,512]{1,0:T(8,128)(2,1)S(1)}, u32[]{:S(2)}, u32[]{:S(2)}) collective-permute-start(f16[112,512]{1,0:T(8,128)(2,1)S(1)} %convert_element_type.42), channel_id=1, source_target_pairs={{0,4},{1,1},{2,6},{3,3},{4,0},{5,5},{6,2},{7,7},{8,12},{9,9},{10,1... | collective-permute-start | bytes 344072 | tf_op jit(solution)/shard_map/ppermute | solution.py:563
  20.9 0.8 %collective-permute-done.3 = f16[112,512]{1,0:T(8,128)(2,1)S(1)} collective-permute-done((f16[112,512]{1,0:T(8,128)(2,1)S(1)}, f16[112,512]{1,0:T(8,128)(2,1)S(1)}, u32[]{:S(2)}, u32[]{:S(2)}) %collective-permute-start.3) | collective-permute-done | bytes 114720 | tf_op jit(solution)/shard_map/ppermute | solution.py:563
  21.7 0.3 collective-permute-done.4
  22.0 0.2 collective-permute-start.8
  22.2 2.3 %collective-permute-done.5 = f16[112,512]{1,0:T(8,128)(2,1)S(1)} collective-permute-done((f16[112,512]{1,0:T(8,128)(2,1)S(1)}, f16[112,512]{1,0:T(8,128)(2,1)S(1)}, u32[]{:S(2)}, u32[]{:S(2)}) %collective-permute-start.5) | collective-permute-done | bytes 114720 | tf_op jit(solution)/shard_map/ppermute | solution.py:563
  24.6 0.8 %collective-permute-done.6 = f16[112,512]{1,0:T(8,128)(2,1)S(1)} collective-permute-done((f16[112,512]{1,0:T(8,128)(2,1)S(1)}, f16[112,512]{1,0:T(8,128)(2,1)S(1)}, u32[]{:S(2)}, u32[]{:S(2)}) %collective-permute-start.6) | collective-permute-done | bytes 114720 | tf_op jit(solution)/shard_map/ppermute | solution.py:563
  25.6 0.3 collective-permute-done.9
  25.9 0.3 assemble.1
  26.2 0.6 %collective-permute-done.10 = f16[112,512]{1,0:T(8,128)(2,1)S(1)} collective-permute-done((f16[112,512]{1,0:T(8,128)(2,1)S(1)}, f16[112,512]{1,0:T(8,128)(2,1)S(1)}, u32[]{:S(2)}, u32[]{:S(2)}) %collective-permute-start.10) | collective-permute-done | bytes 114720 | tf_op jit(solution)/shard_map/ppermute | solution.py:575
  26.8 1.3 %stencil.1 = (f32[48,2048]{1,0:T(8,128)S(1)}, bf16[48,512]{1,0:T(8,128)(2,1)S(1)}, bf16[48,512]{1,0:T(8,128)(2,1)S(1)}, bf16[48,512]{1,0:T(8,128)(2,1)S(1)}, bf16[48,512]{1,0:T(8,128)(2,1)S(1)}) custom-call(f32[1,3]{1,0:T(1,128)S(1)} %bitcast.19, f32[112,2176]{1,0:T(8,128)S(1)} %get-tuple-element.17.acc_in, f32[32,128]{1,0:T(8,128)S(1)} %get-tuple-element.18.side, ...), custom_call_target="tpu_custom_call" | custom-call | flops 22937600 | bytes 1835008 | tf_op jit(solution)/shard_map/stencil/pallas_call | solution.py:455
  28.1 3.7 %collective-permute-start.13 = (bf16[48,512]{1,0:T(8,128)(2,1)S(1)}, bf16[48,512]{1,0:T(8,128)(2,1)S(1)}, u32[]{:S(2)}, u32[]{:S(2)}) collective-permute-start(bf16[48,512]{1,0:T(8,128)(2,1)S(1)} %get-tuple-element.21), channel_id=1, source_target_pairs={{20,0},{17,1},{22,2},{19,3},{16,4},{21,5},{18,6},{23,7},{28,8},{25... | collective-permute-start | bytes 147464 | tf_op jit(solution)/shard_map/ppermute | solution.py:587
  31.8 0.8 %collective-permute-start.14 = (bf16[48,512]{1,0:T(8,128)(2,1)S(1)}, bf16[48,512]{1,0:T(8,128)(2,1)S(1)}, u32[]{:S(2)}, u32[]{:S(2)}) collective-permute-start(bf16[48,512]{1,0:T(8,128)(2,1)S(1)} %get-tuple-element.22), channel_id=1, source_target_pairs={{8,0},{13,1},{10,2},{15,3},{12,4},{9,5},{14,6},{11,7},{0,8},{5,9},... | collective-permute-start | bytes 147464 | tf_op jit(solution)/shard_map/ppermute | solution.py:587
  32.6 3.3 %collective-permute-start.11 = (bf16[48,512]{1,0:T(8,128)(2,1)S(1)}, bf16[48,512]{1,0:T(8,128)(2,1)S(1)}, u32[]{:S(2)}, u32[]{:S(2)}) collective-permute-start(bf16[48,512]{1,0:T(8,128)(2,1)S(1)} %get-tuple-element.20), channel_id=1, source_target_pairs={{4,0},{1,1},{6,2},{3,3},{0,4},{5,5},{2,6},{7,7},{12,8},{9,9},{14,1... | collective-permute-start | bytes 147464 | tf_op jit(solution)/shard_map/ppermute | solution.py:587
  36.1 0.5 %collective-permute-start.17 = (bf16[48,512]{1,0:T(8,128)(2,1)S(1)}, bf16[48,512]{1,0:T(8,128)(2,1)S(1)}, u32[]{:S(2)}, u32[]{:S(2)}) collective-permute-start(bf16[48,512]{1,0:T(8,128)(2,1)S(1)} %collective-permute-done.14.refs_1_), channel_id=1, source_target_pairs={{0,1},{1,0},{2,3},{3,2},{4,5},{5,4},{6,7},{7,6},{8,9},{9,8},{10,11... | collective-permute-start | bytes 147464 | tf_op jit(solution)/shard_map/ppermute | solution.py:589
  36.5 2.0 %collective-permute-done.15.refs_2_ = bf16[48,512]{1,0:T(8,128)(2,1)S(1)} collective-permute-done((bf16[48,512]{1,0:T(8,128)(2,1)S(1)}, bf16[48,512]{1,0:T(8,128)(2,1)S(1)}, u32[]{:S(2)}, u32[]{:S(2)}) %collective-permute-start.15) | collective-permute-done | bytes 49184 | tf_op jit(solution)/shard_map/ppermute | solution.py:587
  38.6 0.4 collective-permute-start.12
  39.0 0.7 %emit.1 = f32[3,8,2048]{2,1,0:T(8,128)} custom-call(f32[48,2048]{1,0:T(8,128)S(1)} %get-tuple-element.19.both), custom_call_target="tpu_custom_call" | custom-call | bytes 393216 | tf_op jit(solution)/shard_map/emit/pallas_call | solution.py:481
  39.8 0.8 %back.1.refs_1_ = f32[24,2560]{1,0:T(8,128)S(1)} custom-call(s32[1,8]{1,0:T(1,128)S(1)} %copy-done.4, bf16[1,8,512,512]{3,2,1,0:T(8,128)(2,1)S(1)} %copy-done, bf16[48,512]{1,0:T(8,128)(2,1)S(1)} %collective-permute-done.13.refs_0_, bf16[48,512]{1,0:T(8,128)(2,1)S(1)} %collective-permute-done.14.refs_1_, ...), custom_call_target="tpu_custom_call" | custom-call | flops 88080384 | bytes 2097152 | tf_op jit(solution)/shard_map/back/pallas_call | solution.py:520
  40.6 1.0 %back_last.1 = f32[3,8,2048]{2,1,0:T(8,128)} custom-call(s32[1,8]{1,0:T(1,128)S(1)} %copy-done.4, bf16[1,8,512,512]{3,2,1,0:T(8,128)(2,1)S(1)} %copy-done, bf16[48,512]{1,0:T(8,128)(2,1)S(1)} %collective-permute-done.12.refs_0_, f32[24,2560]{1,0:T(8,128)S(1)} %back.1.refs_1_), custom_call_target="tpu_custom_call" | custom-call | flops 12582912 | bytes 2097152 | tf_op jit(solution)/shard_map/back_last/pallas_call | solution.py:520
  (42 shorter events, 0.6 us)
Async XLA Ops:
  1.7 8.4 %collective-permute-start = (bf16[6,8,2048]{2,1,0:T(8,128)(2,1)S(1)}, bf16[6,8,2048]{2,1,0:T(8,128)(2,1)S(1)}, u32[]{:S(2)}, u32[]{:S(2)}) collective-permute-start(bf16[6,8,2048]{2,1,0:T(8,128)(2,1)S(1)} %get-tuple-element.13.fields), channel_id=1, source_target_pairs={{0,1},{1,0},{2,3},{3,2},{4,5},{5,4},{6,7},{7,6},{8,9},{9,8},{10,11... | collective-permute-start | bytes 589832 | tf_op jit(solution)/shard_map/ppermute | solution.py:553
  2.3 7.9 %copy-start.1 = (f32[2048]{0:T(1024)S(1)}, f32[2048]{0:T(1024)}, u32[]{:S(2)}) copy-start(f32[2048]{0:T(1024)} %param.13) | copy-start | bytes 24580
  2.3 7.9 %copy-start.2 = (f32[2048]{0:T(1024)S(1)}, f32[2048]{0:T(1024)}, u32[]{:S(2)}) copy-start(f32[2048]{0:T(1024)} %param.14) | copy-start | bytes 24580
  2.3 7.9 %copy-start.3 = (s32[2048]{0:T(1024)S(1)}, s32[2048]{0:T(1024)}, u32[]{:S(2)}) copy-start(s32[2048]{0:T(1024)} %param.15) | copy-start | bytes 24580
  2.3 7.9 %copy-start.4 = (s32[1,8]{1,0:T(1,128)S(1)}, s32[1,8]{1,0:T(1,128)}, u32[]{:S(2)}) copy-start(s32[1,8]{1,0:T(1,128)} %counts.11) | copy-start | bytes 100
  2.3 3.7 %collective-permute-start.1 = (bf16[8,2304]{1,0:T(8,128)(2,1)S(1)}, bf16[8,2304]{1,0:T(8,128)(2,1)S(1)}, u32[]{:S(2)}, u32[]{:S(2)}) collective-permute-start(bf16[8,2304]{1,0:T(8,128)(2,1)S(1)} %get-tuple-element.14), channel_id=1, source_target_pairs={{1,2},{2,1},{5,6},{6,5},{9,10},{10,9},{13,14},{14,13},{17,18},{18,... | collective-permute-start | bytes 110600 | tf_op jit(solution)/shard_map/ppermute | solution.py:550
  3.1 7.0 %collective-permute-start.2 = (bf16[8,2304]{1,0:T(8,128)(2,1)S(1)}, bf16[8,2304]{1,0:T(8,128)(2,1)S(1)}, u32[]{:S(2)}, u32[]{:S(2)}) collective-permute-start(bf16[8,2304]{1,0:T(8,128)(2,1)S(1)} %get-tuple-element.14), channel_id=1, source_target_pairs={{1,3},{2,0},{5,7},{6,4},{9,11},{10,8},{13,15},{14,12},{17,19},{18,... | collective-permute-start | bytes 110600 | tf_op jit(solution)/shard_map/ppermute | solution.py:551
  12.0 9.8 %collective-permute-start.3 = (f16[112,512]{1,0:T(8,128)(2,1)S(1)}, f16[112,512]{1,0:T(8,128)(2,1)S(1)}, u32[]{:S(2)}, u32[]{:S(2)}) collective-permute-start(f16[112,512]{1,0:T(8,128)(2,1)S(1)} %convert_element_type.36), channel_id=1, source_target_pairs={{0,20},{1,17},{2,22},{3,19},{4,16},{5,21},{6,18},{7,23},{8,28},{9,... | collective-permute-start | bytes 344072 | tf_op jit(solution)/shard_map/ppermute | solution.py:563
  16.2 5.9 %collective-permute-start.4 = (f16[112,512]{1,0:T(8,128)(2,1)S(1)}, f16[112,512]{1,0:T(8,128)(2,1)S(1)}, u32[]{:S(2)}, u32[]{:S(2)}) collective-permute-start(f16[112,512]{1,0:T(8,128)(2,1)S(1)} %convert_element_type.38), channel_id=1, source_target_pairs={{0,8},{1,13},{2,10},{3,15},{4,12},{5,9},{6,14},{7,11},{8,0},{9,5},... | collective-permute-start | bytes 344072 | tf_op jit(solution)/shard_map/ppermute | solution.py:563
  17.8 6.8 %collective-permute-start.5 = (f16[112,512]{1,0:T(8,128)(2,1)S(1)}, f16[112,512]{1,0:T(8,128)(2,1)S(1)}, u32[]{:S(2)}, u32[]{:S(2)}) collective-permute-start(f16[112,512]{1,0:T(8,128)(2,1)S(1)} %convert_element_type.40), channel_id=1, source_target_pairs={{0,24},{1,29},{2,26},{3,31},{4,28},{5,25},{6,30},{7,27},{8,16},{9,... | collective-permute-start | bytes 344072 | tf_op jit(solution)/shard_map/ppermute | solution.py:563
  18.7 8.0 %copy-start.5 = (f32[3]{0:T(128)S(1)}, f32[3]{0:T(128)}, u32[]{:S(2)}) copy-start(f32[3]{0:T(128)} %param.12) | copy-start | bytes 40
  18.7 6.7 %collective-permute-start.6 = (f16[112,512]{1,0:T(8,128)(2,1)S(1)}, f16[112,512]{1,0:T(8,128)(2,1)S(1)}, u32[]{:S(2)}, u32[]{:S(2)}) collective-permute-start(f16[112,512]{1,0:T(8,128)(2,1)S(1)} %convert_element_type.42), channel_id=1, source_target_pairs={{0,4},{1,1},{2,6},{3,3},{4,0},{5,5},{6,2},{7,7},{8,12},{9,9},{10,1... | collective-permute-start | bytes 344072 | tf_op jit(solution)/shard_map/ppermute | solution.py:563
  21.7 3.8 %collective-permute-start.7 = (f16[112,512]{1,0:T(8,128)(2,1)S(1)}, f16[112,512]{1,0:T(8,128)(2,1)S(1)}, u32[]{:S(2)}, u32[]{:S(2)}) collective-permute-start(f16[112,512]{1,0:T(8,128)(2,1)S(1)} %collective-permute-done.3), channel_id=1, source_target_pairs={{0,1},{1,0},{2,3},{3,2},{4,5},{5,4},{6,7},{7,6},{8,9},{9,8},{10,11... | collective-permute-start | bytes 344072 | tf_op jit(solution)/shard_map/ppermute | solution.py:575
  22.0 3.5 %collective-permute-start.8 = (f16[112,512]{1,0:T(8,128)(2,1)S(1)}, f16[112,512]{1,0:T(8,128)(2,1)S(1)}, u32[]{:S(2)}, u32[]{:S(2)}) collective-permute-start(f16[112,512]{1,0:T(8,128)(2,1)S(1)} %collective-permute-done.4), channel_id=1, source_target_pairs={{0,1},{1,0},{2,3},{3,2},{4,5},{5,4},{6,7},{7,6},{8,9},{9,8},{10,11... | collective-permute-start | bytes 344072 | tf_op jit(solution)/shard_map/ppermute | solution.py:575
  24.6 1.3 %collective-permute-start.9 = (f16[112,512]{1,0:T(8,128)(2,1)S(1)}, f16[112,512]{1,0:T(8,128)(2,1)S(1)}, u32[]{:S(2)}, u32[]{:S(2)}) collective-permute-start(f16[112,512]{1,0:T(8,128)(2,1)S(1)} %collective-permute-done.5), channel_id=1, source_target_pairs={{0,1},{1,0},{2,3},{3,2},{4,5},{5,4},{6,7},{7,6},{8,9},{9,8},{10,11... | collective-permute-start | bytes 344072 | tf_op jit(solution)/shard_map/ppermute | solution.py:575
  25.4 1.3 %collective-permute-start.10 = (f16[112,512]{1,0:T(8,128)(2,1)S(1)}, f16[112,512]{1,0:T(8,128)(2,1)S(1)}, u32[]{:S(2)}, u32[]{:S(2)}) collective-permute-start(f16[112,512]{1,0:T(8,128)(2,1)S(1)} %collective-permute-done.6), channel_id=1, source_target_pairs={{0,1},{1,0},{2,3},{3,2},{4,5},{5,4},{6,7},{7,6},{8,9},{9,8},{10,11... | collective-permute-start | bytes 344072 | tf_op jit(solution)/shard_map/ppermute | solution.py:575
  25.6 14.2 %copy-start = (bf16[1,8,512,512]{3,2,1,0:T(8,128)(2,1)S(1)}, bf16[1,8,512,512]{3,2,1,0:T(8,128)(2,1)}, u32[]{:S(2)}) copy-start(bf16[1,8,512,512]{3,2,1,0:T(8,128)(2,1)} %weight.5) | copy-start | bytes 12582916
  28.1 7.8 %collective-permute-start.13 = (bf16[48,512]{1,0:T(8,128)(2,1)S(1)}, bf16[48,512]{1,0:T(8,128)(2,1)S(1)}, u32[]{:S(2)}, u32[]{:S(2)}) collective-permute-start(bf16[48,512]{1,0:T(8,128)(2,1)S(1)} %get-tuple-element.21), channel_id=1, source_target_pairs={{20,0},{17,1},{22,2},{19,3},{16,4},{21,5},{18,6},{23,7},{28,8},{25... | collective-permute-start | bytes 147464 | tf_op jit(solution)/shard_map/ppermute | solution.py:587
  31.8 4.3 %collective-permute-start.14 = (bf16[48,512]{1,0:T(8,128)(2,1)S(1)}, bf16[48,512]{1,0:T(8,128)(2,1)S(1)}, u32[]{:S(2)}, u32[]{:S(2)}) collective-permute-start(bf16[48,512]{1,0:T(8,128)(2,1)S(1)} %get-tuple-element.22), channel_id=1, source_target_pairs={{8,0},{13,1},{10,2},{15,3},{12,4},{9,5},{14,6},{11,7},{0,8},{5,9},... | collective-permute-start | bytes 147464 | tf_op jit(solution)/shard_map/ppermute | solution.py:587
  32.6 5.9 %collective-permute-start.15 = (bf16[48,512]{1,0:T(8,128)(2,1)S(1)}, bf16[48,512]{1,0:T(8,128)(2,1)S(1)}, u32[]{:S(2)}, u32[]{:S(2)}) collective-permute-start(bf16[48,512]{1,0:T(8,128)(2,1)S(1)} %get-tuple-element.23), channel_id=1, source_target_pairs={{24,0},{29,1},{26,2},{31,3},{28,4},{25,5},{30,6},{27,7},{16,8},{21... | collective-permute-start | bytes 147464 | tf_op jit(solution)/shard_map/ppermute | solution.py:587
  32.6 6.0 %collective-permute-start.11 = (bf16[48,512]{1,0:T(8,128)(2,1)S(1)}, bf16[48,512]{1,0:T(8,128)(2,1)S(1)}, u32[]{:S(2)}, u32[]{:S(2)}) collective-permute-start(bf16[48,512]{1,0:T(8,128)(2,1)S(1)} %get-tuple-element.20), channel_id=1, source_target_pairs={{4,0},{1,1},{6,2},{3,3},{0,4},{5,5},{2,6},{7,7},{12,8},{9,9},{14,1... | collective-permute-start | bytes 147464 | tf_op jit(solution)/shard_map/ppermute | solution.py:587
  36.0 3.8 %collective-permute-start.16 = (bf16[48,512]{1,0:T(8,128)(2,1)S(1)}, bf16[48,512]{1,0:T(8,128)(2,1)S(1)}, u32[]{:S(2)}, u32[]{:S(2)}) collective-permute-start(bf16[48,512]{1,0:T(8,128)(2,1)S(1)} %collective-permute-done.13.refs_0_), channel_id=1, source_target_pairs={{0,1},{1,0},{2,3},{3,2},{4,5},{5,4},{6,7},{7,6},{8,9},{9,8},{10,11... | collective-permute-start | bytes 147464 | tf_op jit(solution)/shard_map/ppermute | solution.py:589
  36.1 3.7 %collective-permute-start.17 = (bf16[48,512]{1,0:T(8,128)(2,1)S(1)}, bf16[48,512]{1,0:T(8,128)(2,1)S(1)}, u32[]{:S(2)}, u32[]{:S(2)}) collective-permute-start(bf16[48,512]{1,0:T(8,128)(2,1)S(1)} %collective-permute-done.14.refs_1_), channel_id=1, source_target_pairs={{0,1},{1,0},{2,3},{3,2},{4,5},{5,4},{6,7},{7,6},{8,9},{9,8},{10,11... | collective-permute-start | bytes 147464 | tf_op jit(solution)/shard_map/ppermute | solution.py:589
  38.5 1.2 %collective-permute-start.18 = (bf16[48,512]{1,0:T(8,128)(2,1)S(1)}, bf16[48,512]{1,0:T(8,128)(2,1)S(1)}, u32[]{:S(2)}, u32[]{:S(2)}) collective-permute-start(bf16[48,512]{1,0:T(8,128)(2,1)S(1)} %collective-permute-done.15.refs_2_), channel_id=1, source_target_pairs={{0,1},{1,0},{2,3},{3,2},{4,5},{5,4},{6,7},{7,6},{8,9},{9,8},{10,11... | collective-permute-start | bytes 147464 | tf_op jit(solution)/shard_map/ppermute | solution.py:589
  38.6 2.0 %collective-permute-start.12 = (bf16[48,512]{1,0:T(8,128)(2,1)S(1)}, bf16[48,512]{1,0:T(8,128)(2,1)S(1)}, u32[]{:S(2)}, u32[]{:S(2)}) collective-permute-start(bf16[48,512]{1,0:T(8,128)(2,1)S(1)} %collective-permute-done.11.refs_3_), channel_id=1, source_target_pairs={{0,1},{1,0},{2,3},{3,2},{4,5},{5,4},{6,7},{7,6},{8,9},{9,8},{10,11... | collective-permute-start | bytes 147464 | tf_op jit(solution)/shard_map/ppermute | solution.py:589
